TPU v7x, 128 devices: a whole 4x4x4 slice. The times are simulated.
128 devices in a mesh: tok: 8 (over y, z_lo), hid: 16 (over z_hi, x, core).
Axes of the slice: x: 4, y: 4, z: 4 (z_hi: 2, z_lo: 2; z = z_hi * 2 + z_lo), core: 2. Of those that a mesh axis runs over, the one named last changes fastest.
Arguments:
- tokens: bfloat16 [12288, 6144], P('tok', 'hid'), may hold values from -6 to 6
- cotangent: bfloat16 [12288, 6144], P('tok', 'hid'), may hold values from -6 to 6
- expert_choice: int32 [12288, 2], P('tok'), may hold values from 0 to 7, as said below
- router: bfloat16 [8, 6144], replicated, may hold values from -0.078125 to 0.078125
- gate_up: bfloat16 [6144, 2, 8192], P('tok', None, 'hid'), may hold values from -0.109375 to 0.109375
- w_down: bfloat16 [6144, 8192], P('tok', 'hid'), may hold values from -0.0625 to 0.0625
Outputs:
- grad_tokens: bfloat16 [12288, 6144], P('tok', 'hid')
- d_combine: float32 [12288, 2], P('tok')
- d_gate_up: float32 [6144, 2, 8192], P('tok', None, 'hid')
- d_down: float32 [6144, 8192], P('tok', 'hid')
Inputs may be any that keep to these rules, and one draw needn't show every extreme that they name: `expert_choice`: each row names 2 different experts. In every aligned block of 1536 rows at most 432 rows name expert 0 and at least half of 432 do; some block has exactly 432.
All inputs are finite; a program needn't handle non-finite values.
Results may differ from a plain program's by a relative error of at most 0.017.
Values may be sent and summed in bfloat16 or wider, within the bound.
A program may use at most 128 MiB of HBM per device.

v0:
```python
import jax
import jax.numpy as jnp
from jax import lax
from jax.sharding import Mesh
from jax.sharding import PartitionSpec as P

CAP = 432
TOK = ("tok_0", "tok_1")


def sent_together(arrays, axis, dim, along):
    both = jnp.concatenate(arrays, axis=along)
    result, at, outs = (lax.all_gather(both, axis, axis=dim, tiled=True), 0, [])
    for a in arrays:
        outs.append(lax.slice_in_dim(result, at, at + a.shape[along], axis=along))
        at += a.shape[along]
    return tuple(outs)


def sent_to_all(shard, axis):
    size = lax.axis_size(axis)
    return lax.all_to_all(
        jnp.broadcast_to(shard[None], (size, *shard.shape)), axis, 0, 0, tiled=True
    )


def of_everyone(shard, axis):
    everything = sent_to_all(shard, axis)
    return jnp.sum(everything, axis=0)


def summed_rows(terms, axes):
    so_far = terms.astype(jnp.bfloat16)
    for axis in axes:
        so_far = lax.psum_scatter(so_far, axis, scatter_dimension=0, tiled=True)
    return so_far.astype(jnp.float32)


def silu_pair(pre):
    sigma = jax.nn.sigmoid(pre)
    return (pre * sigma, sigma * (1.0 + pre * (1.0 - sigma)))


def contract_rows(left, right):
    return lax.dot_general(
        left, right, (((0,), (0,)), ((), ())), preferred_element_type=jnp.float32
    )


def contract_cols(left, right):
    return lax.dot_general(
        left, right, (((1,), (1,)), ((), ())), preferred_element_type=jnp.float32
    )


def local_grads(joined, raw, slot_gate):
    width = raw.shape[1]
    gate_pre = joined[:, :width]
    up_pre = joined[:, width:]
    active, slope = silu_pair(gate_pre)
    product = active * up_pre
    scale = slot_gate[:, None]
    scaled = (scale * product).astype(jnp.bfloat16)
    score_part = jnp.sum(product * raw, axis=1)
    upstream = scale * raw
    grads_mid = jnp.concatenate(
        [
            (upstream * up_pre * slope).astype(jnp.bfloat16),
            (upstream * active).astype(jnp.bfloat16),
        ],
        axis=1,
    )
    return (grads_mid, scaled, score_part)


def local(tokens, cotangent, expert_choice, router, gate_up, w_down):
    local_cols = tokens.shape[1]
    weight_rows = w_down.shape[0]
    hidden_local = w_down.shape[1]
    first = expert_choice[:, 0]
    second = expert_choice[:, 1]
    in_first = first == 0
    in_second = second == 0
    routed = jnp.logical_or(in_first, in_second)
    flags = routed.astype(jnp.int32)
    slot_rank = jnp.cumsum(flags) - flags
    slot_ids = jnp.arange(CAP, dtype=jnp.int32)
    placed = jnp.logical_and(routed[None, :], slot_rank[None, :] == slot_ids[:, None])
    stacked = jnp.concatenate([tokens, cotangent], axis=1)
    dispatched = jnp.dot(
        placed.astype(jnp.bfloat16), stacked, preferred_element_type=jnp.float32
    ).astype(jnp.bfloat16)
    expert_in, expert_cot = sent_together(
        (dispatched[:, :local_cols], dispatched[:, local_cols:]), "hid", 1, 0
    )
    router_cols = lax.dynamic_slice_in_dim(
        router, lax.axis_index("hid") * local_cols, local_cols, 1
    )
    logits = of_everyone(contract_cols(tokens, router_cols), "hid")
    other = first + second
    labels = jnp.arange(logits.shape[1], dtype=jnp.int32)
    other_logit = jnp.sum(jnp.where(other[:, None] == labels[None, :], logits, 0.0), axis=1)
    gating = jnp.where(routed, jax.nn.sigmoid(logits[:, 0] - other_logit), 0.0)
    slot_gate = jnp.sum(jnp.where(placed, gating[None, :], 0.0), axis=1)
    weights_in = gate_up.reshape(weight_rows, 2 * hidden_local)
    gathered = lax.all_gather(weights_in, TOK, axis=0, tiled=True)
    joined = jnp.dot(expert_in, gathered, preferred_element_type=jnp.float32)
    raw = jnp.dot(
        expert_cot,
        lax.all_gather(w_down, TOK, axis=0, tiled=True),
        preferred_element_type=jnp.float32,
    )
    grads_mid, scaled, score_part = local_grads(joined, raw, slot_gate)
    grads = summed_rows(
        jnp.concatenate(
            [contract_rows(expert_in, grads_mid), contract_rows(expert_cot, scaled)], axis=1
        ),
        TOK,
    )
    expert_back = contract_cols(grads_mid, gathered)
    back_cols = lax.psum_scatter(expert_back, "hid", scatter_dimension=1, tiled=True)
    scores = of_everyone(score_part, "hid")
    safe = jnp.minimum(slot_rank, CAP - 1)
    grad_tokens = jnp.where(routed[:, None], jnp.take(back_cols, safe, axis=0), 0.0).astype(
        jnp.bfloat16
    )
    token_score = jnp.where(routed, jnp.take(scores, safe, axis=0), 0.0)
    d_combine = jnp.stack(
        [jnp.where(in_first, token_score, 0.0), jnp.where(in_second, token_score, 0.0)], axis=1
    )
    d_gate_up = grads[:, : 2 * hidden_local].reshape(weight_rows, 2, hidden_local)
    d_down = grads[:, 2 * hidden_local :]
    return (grad_tokens, d_combine, d_gate_up, d_down)


def solution(mesh):
    split = Mesh(mesh.devices.reshape(4, 2, mesh.shape["hid"]), ("tok_0", "tok_1", "hid"))
    return jax.shard_map(
        local,
        mesh=split,
        in_specs=(
            P(TOK, "hid"),
            P(TOK, "hid"),
            P(TOK, None),
            P(),
            P(TOK, None, "hid"),
            P(TOK, "hid"),
        ),
        out_specs=(P(TOK, "hid"), P(TOK, None), P(TOK, None, "hid"), P(TOK, "hid")),
        check_vma=False,
    )
```

profile of v0, /device:TPU:24, one launch (start us, length us, event | category | flops | bytes accessed | tf_op | source)
XLA Modules:
  0.0 890.8 jit_solution(6275902168997579688)
XLA Ops:
  7.2 0.8 convert_reduce_fusion
  8.8 3.0 fusion.12
  11.9 0.9 pad_maximum_fusion.2
  12.8 0.6 copy-done.3
  13.4 1.6 copy.25
  15.1 0.7 all-gather.6.cloned.1.call-update
  16.3 26.7 %all_to_all.11 = f32[16,1536,8]{1,2,0:T(8,128)S(1)} all-to-all(f32[16,1536,8]{1,2,0:T(8,128)S(1)} %broadcast_in_dim.78), channel_id=1, replica_groups=mesh['tok_0'=4,'tok_1'=2,'hid'=16] {'hid'}, dimensions={0} | all-to-all | bytes 1572864 | tf_op jit(solution)/shard_map/all_to_all | solution.py:22
  43.1 0.6 select_reduce_fusion
  43.7 69.3 %all-gather.4.cloned.1.call-done = bf16[864,6144]{1,0:T(8,128)(2,1)} async-done(((bf16[864,384]{1,0:T(8,128)(2,1)}), bf16[864,6144]{1,0:T(8,128)(2,1)}) %all-gather.4.cloned.1.call-update) | async-done | bytes 10616848 | tf_op jit(solution)/shard_map/all_gather | solution.py:13
  113.1 247.4 %all-gather.8.cloned.1.call-done = bf16[6144,1024]{1,0:T(8,128)(2,1)} async-done(((bf16[768,1024]{1,0:T(8,128)(2,1)}), bf16[6144,1024]{1,0:T(8,128)(2,1)}) %all-gather.8.cloned.1.call-update) | async-done | bytes 12582928 | tf_op jit(solution)/shard_map/all_gather | solution.py:106
  360.5 11.9 %fusion.1 = f32[432,1024]{1,0:T(8,128)S(1)} fusion(bf16[6144,1024]{1,0:T(8,128)(2,1)} %all-gather.8.cloned.1.call-done, bf16[864,6144]{1,0:T(8,128)(2,1)} %all-gather.4.cloned.1.call-done), kind=kOutput, calls=%fused_computation.6 | convolution fusion | flops 5435817984 | bytes 19660800 | tf_op jit(solution)/shard_map/dot_general | solution.py:107
  372.4 1.2 copy-done.7
  373.6 5.7 convolution_convert_fusion.1
  379.3 112.9 %all-gather.6.cloned.1.call-done = bf16[6144,512]{1,0:T(8,128)(2,1)} async-done(((bf16[768,512]{1,0:T(8,128)(2,1)}), bf16[6144,512]{1,0:T(8,128)(2,1)}) %all-gather.6.cloned.1.call-update) | async-done | bytes 6291472 | tf_op jit(solution)/shard_map/all_gather | solution.py:110
  492.1 8.1 multiply_convert_fusion.2
  500.3 9.7 %convolution_convert_fusion = bf16[6144,1024]{0,1:T(8,128)(2,1)S(1)} fusion(bf16[864,6144]{1,0:T(8,128)(2,1)} %all-gather.4.cloned.1.call-done, bf16[432,512]{1,0:T(8,128)(2,1)S(1)} %get-tuple-element.31, bf16[432,512]{1,0:T(8,128)(2,1)S(1)} %get-tuple-element.30), kind=kOutput, calls=%fused_computation.3 | convolution fusion | flops 5443878912 | bytes 18776064 | tf_op jit(solution)/shard_map/dot_general | solution.py:45
  509.9 21.1 %pad_maximum_fusion = bf16[6144,1536]{0,1:T(8,128)(2,1)} fusion(bf16[6144,512]{0,1:T(8,128)(2,1)S(1)} %copy-done.2, bf16[6144,1024]{0,1:T(8,128)(2,1)S(1)} %convolution_convert_fusion), kind=kLoop, calls=%fused_computation.2 | loop fusion | flops 37748736 | bytes 37748736 | tf_op jit(solution)/shard_map/concatenate | solution.py:115
  531.1 19.3 %fusion.20 = f32[432,6144]{1,0:T(8,128)} fusion(bf16[6144,1024]{1,0:T(8,128)(2,1)} %all-gather.8.cloned.1.call-done, bf16[432,512]{1,0:T(8,128)(2,1)S(1)} %get-tuple-element.31, bf16[432,512]{1,0:T(8,128)(2,1)S(1)} %get-tuple-element.30), kind=kOutput, calls=%fused_computation.32 | convolution fusion | flops 5437587456 | bytes 24084480 | tf_op jit(solution)/shard_map/dot_general | solution.py:51
  550.5 145.0 %reduce-scatter.6.cloned.1.call-done = bf16[1536,1536]{0,1:T(8,128)(2,1)} async-done(((bf16[6144,1536]{0,1:T(8,128)(2,1)}), bf16[1536,1536]{0,1:T(8,128)(2,1)}) %reduce-scatter.6.cloned.1.call-update) | async-done | bytes 4718608 | tf_op jit(solution)/shard_map/reduce_scatter | solution.py:35
  695.6 0.6 broadcast_in_dim.85
  696.2 6.9 all-to-all-start.1
  703.2 7.6 all-to-all-done.1
  710.8 9.5 %gather_fusion.1 = f32[1536]{0:T(1024)S(1)} fusion(f32[432]{0:T(512)S(1)} %reduce_sum.49, s32[2048]{0:T(1024)S(1)} %pad_clamp_fusion), kind=kCustom, calls=%fused_computation.1 | custom fusion | bytes 18432 | tf_op jit(solution)/shard_map/jit(_take)/gather | solution.py:127
  720.4 0.6 pad_maximum_fusion.5
  721.0 91.5 %reduce-scatter.4.cloned.1.call-done = f32[432,384]{1,0:T(8,128)} async-done(((f32[432,6144]{1,0:T(8,128)}), f32[432,384]{1,0:T(8,128)}) %reduce-scatter.4.cloned.1.call-update) | async-done | bytes 663568 | tf_op jit(solution)/shard_map/reduce_scatter | solution.py:121
  812.5 5.4 gather_fusion
  817.9 1.9 select_convert_fusion
  819.9 56.2 %reduce-scatter.8.cloned.1.call-done = bf16[768,1536]{0,1:T(8,128)(2,1)} async-done(((bf16[1536,1536]{0,1:T(8,128)(2,1)}), bf16[768,1536]{0,1:T(8,128)(2,1)}) %reduce-scatter.8.cloned.1.call-update) | async-done | bytes 2359312 | tf_op jit(solution)/shard_map/reduce_scatter | solution.py:35
  876.1 1.2 slice.67
  877.4 1.6 copy.22
  879.0 1.6 slice.66
  880.6 3.4 copy.21
  (44 shorter events, 1.9 us)
Async XLA Ops:
  7.2 8.6 copy-start
  7.2 105.9 %all-gather.4.cloned.1.call-start = ((), (), s32[]{:S(2)}) async-start(), calls=%async_computation.5 | async-start | bytes 11280384 | tf_op jit(solution)/shard_map/all_gather | solution.py:13
  11.8 1.7 copy-start.3
  12.8 3.0 copy-start.4
  12.8 347.7 %all-gather.8.cloned.1.call-start = ((), (), s32[]{:S(2)}) async-start(), calls=%async_computation.7 | async-start | bytes 14155776 | tf_op jit(solution)/shard_map/all_gather | solution.py:106
  15.0 477.1 %all-gather.6.cloned.1.call-start = ((), (), s32[]{:S(2)}) async-start(), calls=%async_computation.6 | async-start | bytes 7077888 | tf_op jit(solution)/shard_map/all_gather | solution.py:110
  15.8 679.8 %reduce-scatter.6.cloned.1.call-start = ((), (), s32[]{:S(2)}) async-start(), calls=%async_computation.9 | async-start | bytes 23592960 | tf_op jit(solution)/shard_map/reduce_scatter | solution.py:35
  360.5 13.1 %copy-start.6 = (bf16[864,6144]{1,0:T(8,128)(2,1)S(1)}, bf16[864,6144]{1,0:T(8,128)(2,1)}, u32[]{:S(2)}) copy-start(bf16[864,6144]{1,0:T(8,128)(2,1)} %all-gather.4.cloned.1.call-done) | copy-start | bytes 31850500
  372.4 1.2 copy-start.7
  500.3 9.7 %copy-start.2 = (bf16[6144,512]{0,1:T(8,128)(2,1)S(1)}, bf16[6144,512]{0,1:T(8,128)(2,1)}, u32[]{:S(2)}) copy-start(bf16[6144,512]{0,1:T(8,128)(2,1)} %convolution_convert_fusion.1) | copy-start | bytes 18874372
  531.1 281.4 %reduce-scatter.4.cloned.1.call-start = ((), (), s32[]{:S(2)}) async-start(), calls=%async_computation.8 | async-start | bytes 11280384 | tf_op jit(solution)/shard_map/reduce_scatter | solution.py:121
  550.4 325.7 %reduce-scatter.8.cloned.1.call-start = ((), (), s32[]{:S(2)}) async-start(), calls=%async_computation.10 | async-start | bytes 7077888 | tf_op jit(solution)/shard_map/reduce_scatter | solution.py:35
  696.2 14.5 %all-to-all-start.1 = ((f32[16,1,432]{2,1,0:T(1,128)}), f32[16,1,432]{2,1,0:T(1,128)S(1)}, u32[]{:S(2)}, u32[]{:S(2)}) async-start(f32[16,1,432]{2,1,0:T(1,128)} %broadcast_in_dim.85), calls=%async_computation.2 | async-start | bytes 65536 | tf_op jit(solution)/shard_map/all_to_all | solution.py:22
  710.8 9.5 %copy-start.5 = (s32[1536,2]{0,1:T(2,128)S(1)}, s32[1536,2]{0,1:T(2,128)}, u32[]{:S(2)}) copy-start(s32[1536,2]{0,1:T(2,128)} %param.8) | copy-start | bytes 36868
  880.6 3.4 copy-start.1
Sparse Core Ops, SparseCore 0:
  12.9 100.1 all-gather.3
  115.3 245.1 all-gather.7
  362.1 129.9 all-gather.5
  531.2 164.2 reduce-scatter.5
  699.9 112.6 reduce-scatter.3
  814.8 61.2 reduce-scatter.7
where the time goes:
time: 892 us; the launch traced here: 891 us
  waiting for transfers between devices  731 us (82%)
  matrix products  58 us (7%)
  local copies, waits for them, and re-layouts  27.1 us (3%)
  other arithmetic  26.7 us (3%)
  blocking collectives  26.7 us (3%)
  between operations  14.3 us (2%)
    all_gather x1, waiting for transfers between devices, local(): gathered = lax.all_gather(weights_in, TOK, axis=0, tiled=True)  247 us
    reduce_scatter x2, waiting for transfers between devices, summed_rows(): so_far = lax.psum_scatter(so_far, axis, scatter_dimension=0, tiled=True)  201 us
    all_gather x1, waiting for transfers between devices, local(): lax.all_gather(w_down, TOK, axis=0, tiled=True)  113 us
    reduce_scatter x1, waiting for transfers between devices, local(): lax.psum_scatter(expert_back, 'hid', scatter_dimension=1, tiled=True)  91.5 us
    all_gather x1, waiting for transfers between devices, sent_together(): result, at, outs = (lax.all_gather(both, axis, axis=dim, tiled=True), 0, [])  69.3 us
    all_to_all x1, blocking collectives, sent_to_all(): lax.all_to_all(jnp.broadcast_to(shard[None], (size, *shard.shape)), axis,...  26.7 us
    concatenate x1, other arithmetic, local(): jnp.concatenate([contract_rows(expert_in, grads_mid), contract_rows(exper...  21.1 us
    dot_general x2, matrix products, contract_cols(): lax.dot_general(left, right, (((1,), (1,)), ((), ())), preferred_element_...  19.7 us
  transfers between devices with their start and end apart: 7, of which 7 were waited for; matrix products, arithmetic and copies ran while one was open for 6% of the time, Pallas kernels for 0%

commit v1 on v0

v1 whole, which is shorter than its diff:
```python
import jax
import jax.numpy as jnp
from jax import lax
from jax.sharding import Mesh
from jax.sharding import PartitionSpec as P

CAP = 432
TOK = ("y", "zl")
ALL = ("y", "zl", "hid")


def swap_pairs():
    pairs = []
    for y in range(4):
        for zl in range(2):
            for h in range(16):
                to_y, to_h = h // 4, y * 4 + h % 4
                pairs.append(((y * 2 + zl) * 16 + h, (to_y * 2 + zl) * 16 + to_h))
    return pairs


def silu_pair(pre):
    sigma = jax.nn.sigmoid(pre)
    return (pre * sigma, sigma * (1.0 + pre * (1.0 - sigma)))


def dot_f32(left, right, dims):
    return lax.dot_general(left, right, ((dims[0], dims[1]), ((), ())), preferred_element_type=jnp.float32)


def local(tokens, cotangent, expert_choice, router, gate_up, w_down):
    cols = tokens.shape[1]
    rows_own, hid = w_down.shape
    zl = lax.axis_index("zl")
    first = expert_choice[:, 0]
    second = expert_choice[:, 1]
    in_first = first == 0
    in_second = second == 0
    routed = jnp.logical_or(in_first, in_second)
    flags = routed.astype(jnp.int32)
    slot_rank = jnp.cumsum(flags) - flags
    slot_ids = jnp.arange(CAP, dtype=jnp.int32)
    placed = jnp.logical_and(routed[None, :], slot_rank[None, :] == slot_ids[:, None])
    select = placed.astype(jnp.bfloat16)

    weights = jnp.concatenate([gate_up.reshape(rows_own, 2 * hid), w_down], axis=1)
    other_weights = lax.ppermute(weights, "zl", [(0, 1), (1, 0)])

    dispatched = dot_f32(select, jnp.concatenate([tokens, cotangent], axis=1), ((1,), (0,)))
    moved = lax.ppermute(dispatched.astype(jnp.bfloat16), ALL, swap_pairs())
    gathered = lax.all_gather(moved, "hid", axis=0)

    router_cols = lax.dynamic_slice_in_dim(router, lax.axis_index("hid") * cols, cols, 1)
    logits = dot_f32(tokens, router_cols, ((1,), (1,)))
    other = first + second
    labels = jnp.arange(logits.shape[1], dtype=jnp.int32)
    other_logit = jnp.sum(jnp.where(other[:, None] == labels[None, :], logits, 0.0), axis=1)
    margin_part = jnp.sum(jnp.where(placed, (logits[:, 0] - other_logit)[None, :], 0.0), axis=1)
    margin = lax.psum(margin_part, "hid")
    filled = jnp.any(placed, axis=1)
    slot_gate = jnp.where(filled, jax.nn.sigmoid(margin), 0.0)

    parts = gathered.reshape(4, 4, CAP, 2, cols).transpose(3, 0, 2, 1, 4)
    parts = parts.reshape(2, 4 * CAP, 4 * cols)
    rows_in, rows_cot = parts[0], parts[1]

    low = jnp.where(zl == 0, weights, other_weights)
    high = jnp.where(zl == 0, other_weights, weights)
    both = jnp.concatenate([low, high], axis=0)
    w_gu = both[:, : 2 * hid]
    w_d = both[:, 2 * hid :]

    pre = jnp.concatenate(
        [
            dot_f32(rows_in, w_gu, ((1,), (0,))).astype(jnp.bfloat16),
            dot_f32(rows_cot, w_d, ((1,), (0,))).astype(jnp.bfloat16),
        ],
        axis=1,
    )
    pre = lax.psum_scatter(pre, "y", scatter_dimension=0, tiled=True).astype(jnp.float32)
    gate_pre, up_pre, raw = pre[:, :hid], pre[:, hid : 2 * hid], pre[:, 2 * hid :]
    active, slope = silu_pair(gate_pre)
    product = active * up_pre
    scale = slot_gate[:, None]
    score_part = jnp.sum(product * raw, axis=1)
    upstream = scale * raw
    mids = jnp.concatenate(
        [
            (upstream * up_pre * slope).astype(jnp.bfloat16),
            (upstream * active).astype(jnp.bfloat16),
            (scale * product).astype(jnp.bfloat16),
        ],
        axis=1,
    )
    mids = lax.all_gather(mids, "y", axis=0, tiled=True)
    mid_gu, mid_d = mids[:, : 2 * hid], mids[:, 2 * hid :]
    scores = lax.psum(score_part, "hid")

    back = dot_f32(mid_gu, w_gu, ((1,), (1,))).astype(jnp.bfloat16)
    back = back.reshape(4, CAP, 4, cols).transpose(0, 2, 1, 3).reshape(16, CAP, cols)
    back = lax.psum_scatter(back, "hid", scatter_dimension=0, tiled=False)

    def grads_of(rows):
        return jnp.concatenate(
            [
                dot_f32(lax.dynamic_slice_in_dim(rows_in, rows, rows_own, 1), mid_gu, ((0,), (0,))),
                dot_f32(lax.dynamic_slice_in_dim(rows_cot, rows, rows_own, 1), mid_d, ((0,), (0,))),
            ],
            axis=1,
        )

    sent = grads_of((1 - zl) * rows_own).astype(jnp.bfloat16)
    arrived = lax.ppermute(sent, "zl", [(0, 1), (1, 0)])
    grads = grads_of(zl * rows_own) + arrived.astype(jnp.float32)

    back = lax.ppermute(back, ALL, swap_pairs())
    grad_tokens = dot_f32(select, back, ((0,), (0,))).astype(jnp.bfloat16)
    token_score = jnp.sum(jnp.where(placed, scores[:, None], 0.0), axis=0)
    d_combine = jnp.stack(
        [jnp.where(in_first, token_score, 0.0), jnp.where(in_second, token_score, 0.0)], axis=1
    )
    d_gate_up = grads[:, : 2 * hid].reshape(rows_own, 2, hid)
    d_down = grads[:, 2 * hid :]
    return (grad_tokens, d_combine, d_gate_up, d_down)


def solution(mesh):
    split = Mesh(mesh.devices.reshape(4, 2, mesh.shape["hid"]), ("y", "zl", "hid"))
    return jax.shard_map(
        local,
        mesh=split,
        in_specs=(
            P(TOK, "hid"),
            P(TOK, "hid"),
            P(TOK, None),
            P(),
            P(TOK, None, "hid"),
            P(TOK, "hid"),
        ),
        out_specs=(P(TOK, "hid"), P(TOK, None), P(TOK, None, "hid"), P(TOK, "hid")),
        check_vma=False,
    )
```

time: 892 us -> 528 us (0.59)
  waiting for transfers between devices: 731 us -> 297 us
  blocking collectives: 26.7 us -> 71.2 us
  local copies, waits for them, and re-layouts: 27.1 us -> 63.7 us
  matrix products: 58 us -> 46.2 us
    all_gather x3 -> x2, waiting for transfers between devices: 430 us -> 71 us  [the longest x1 53 us: local(): mids = lax.all_gather(mids, 'y', axis=0, tiled=True)]
    reduce_scatter x3 -> x2, waiting for transfers between devices: 293 us -> 128 us  [the longest x1 75.8 us: local(): back = lax.psum_scatter(back, 'hid', scatter_dimension=0, tiled=False)]
    ppermute x0 -> x4, waiting for transfers between devices: none -> 97.2 us  [the longest x1 76.6 us: local(): other_weights = lax.ppermute(weights, 'zl', [(0, 1), (1, 0)])]
    psum x0 -> x2, blocking collectives: none -> 71.2 us  [the longest x1 37.8 us: local(): scores = lax.psum(score_part, 'hid')]
    reshape x0 -> x5, local copies, waits for them, and re-layouts: none -> 48.1 us  [the longest x2 29.2 us: local(): parts = gathered.reshape(4, 4, CAP, 2, cols).transpose(3, 0, 2, 1, 4)]
    all_to_all x1 -> x0, blocking collectives: 26.7 us -> none  [sent_to_all(): lax.all_to_all(jnp.broadcast_to(shard[None], (size, *shard.shape)), axis,...]
    concatenate x2 -> x3, other arithmetic: 22 us -> 5.6 us  [the longest x1 2.84 us: local(): jnp.concatenate([dot_f32(rows_in, w_gu, ((1,), (0,))).astype(jnp.bfloat16...]
    ppermute x0 -> x4, starting transfers between devices: none -> 15.5 us  [the longest x1 7.9 us: local(): moved = lax.ppermute(dispatched.astype(jnp.bfloat16), ALL, swap_pairs())]
  transfers between devices with their start and end apart: 7 -> 8, of which waited for: 7 -> 7; matrix products, arithmetic and copies ran while one was open for 6% -> 7% of each run, Pallas kernels for 0% -> 0%
where the time goes in v1:
time: 528 us; the launch traced here: 527 us
  waiting for transfers between devices  297 us (56%)
  blocking collectives  71.2 us (13%)
  local copies, waits for them, and re-layouts  63.7 us (12%)
  matrix products  46.2 us (9%)
  other arithmetic  19.1 us (4%)
  starting transfers between devices  15.7 us (3%)
  between operations  14.1 us (3%)
    ppermute x1, waiting for transfers between devices, local(): other_weights = lax.ppermute(weights, 'zl', [(0, 1), (1, 0)])  76.6 us
    reduce_scatter x1, waiting for transfers between devices, local(): back = lax.psum_scatter(back, 'hid', scatter_dimension=0, tiled=False)  75.8 us
    all_gather x1, waiting for transfers between devices, local(): mids = lax.all_gather(mids, 'y', axis=0, tiled=True)  53 us
    reduce_scatter x1, waiting for transfers between devices, local(): lax.psum_scatter(pre, 'y', scatter_dimension=0, tiled=True)  52.6 us
    dot_general x10, matrix products, dot_f32(): lax.dot_general(left, right, ((dims[0], dims[1]), ((), ())), preferred_el...  46.2 us
    psum x1, blocking collectives, local(): scores = lax.psum(score_part, 'hid')  37.8 us
    psum x1, blocking collectives, local(): margin = lax.psum(margin_part, 'hid')  33.4 us
    reshape x2, local copies, waits for them, and re-layouts, local(): parts = gathered.reshape(4, 4, CAP, 2, cols).transpose(3, 0, 2, 1, 4)  29.2 us
  transfers between devices with their start and end apart: 8, of which 7 were waited for; matrix products, arithmetic and copies ran while one was open for 7% of the time, Pallas kernels for 0%

profile of v1, /device:TPU:24, one launch (start us, length us, event | category | flops | bytes accessed | tf_op | source)
XLA Modules:
  0.0 526.6 jit_solution(5789460973194179525)
XLA Ops:
  8.7 3.1 fusion.33
  11.8 7.9 %collective-permute-start = (bf16[432,768]{1,0:T(8,128)(2,1)S(1)}, bf16[432,768]{1,0:T(8,128)(2,1)S(1)}, u32[]{:S(2)}, u32[]{:S(2)}) collective-permute-start(bf16[432,768]{1,0:T(8,128)(2,1)S(1)} %fusion.33), channel_id=1, source_target_pairs={{0,0},{1,1},{2,2},{3,3},{4,32},{5,33},{6,34},{7,35},{8,64},{9,65},... | collective-permute-start | bytes 1990664 | tf_op jit(solution)/shard_map/ppermute | solution.py:50
  19.7 16.6 %collective-permute-done = bf16[432,768]{1,0:T(8,128)(2,1)S(1)} collective-permute-done((bf16[432,768]{1,0:T(8,128)(2,1)S(1)}, bf16[432,768]{1,0:T(8,128)(2,1)S(1)}, u32[]{:S(2)}, u32[]{:S(2)}) %collective-permute-start) | collective-permute-done | bytes 663584 | tf_op jit(solution)/shard_map/ppermute | solution.py:50
  38.5 2.2 collective-permute-start.1
  40.6 76.6 %collective-permute-done.1 = bf16[768,1536]{1,0:T(8,128)(2,1)} collective-permute-done((bf16[768,1536]{1,0:T(8,128)(2,1)S(1)}, bf16[768,1536]{1,0:T(8,128)(2,1)}, u32[]{:S(2)}, u32[]{:S(2)}) %collective-permute-start.1) | collective-permute-done | bytes 2359328 | tf_op jit(solution)/shard_map/ppermute | solution.py:47
  117.3 4.2 broadcast_select_fusion.1
  121.5 18.0 %all-gather.6.cloned.1.call-done = bf16[6912,768]{1,0:T(8,128)(2,1)} async-done(((bf16[432,768]{1,0:T(8,128)(2,1)}), bf16[6912,768]{1,0:T(8,128)(2,1)}) %all-gather.6.cloned.1.call-update) | async-done | bytes 10616848 | tf_op jit(solution)/shard_map/all_gather | solution.py:51
  139.5 20.7 %reshape.96 = bf16[4,4,432,2,384]{4,3,2,1,0:T(2,128)(2,1)} reshape(bf16[6912,768]{1,0:T(8,128)(2,1)} %all-gather.6.cloned.1.call-done) | data formatting | bytes 21233664 | tf_op jit(solution)/shard_map/reshape | solution.py:63
  160.1 8.5 %copy.26 = bf16[4,4,432,2,384]{4,1,2,0,3:T(4,128)(2,1)S(1)} copy(bf16[4,4,432,2,384]{4,3,2,1,0:T(2,128)(2,1)} %reshape.96) | data formatting | bytes 21233664 | tf_op jit(solution)/shard_map/reshape | solution.py:63
  168.7 3.8 fusion.53
  176.9 2.4 copy-done.6
  179.3 6.1 %convolution_convert_fusion.1 = bf16[1728,1024]{1,0:T(8,128)(2,1)S(1)} fusion(bf16[1728,1536]{1,0:T(8,128)(2,1)S(1)} %bitcast.29, bf16[768,1536]{1,0:T(8,128)(2,1)S(1)} %copy-done.4, bf16[768,1536]{1,0:T(8,128)(2,1)S(1)} %copy-done.6), kind=kOutput, calls=%fused_computation.6 | convolution fusion | flops 5443878912 | bytes 13565952 | tf_op jit(solution)/shard_map/dot_general | solution.py:28
  185.4 3.1 convolution_convert_fusion.2
  188.5 2.8 pad_maximum_fusion
  193.5 52.6 %reduce-scatter.3.cloned.1.call-done = bf16[432,1536]{1,0:T(8,128)(2,1)} async-done(((bf16[1728,1536]{1,0:T(8,128)(2,1)}), bf16[432,1536]{1,0:T(8,128)(2,1)}) %reduce-scatter.3.cloned.1.call-update) | async-done | bytes 1327120 | tf_op jit(solution)/shard_map/reduce_scatter | solution.py:80
  248.1 37.8 %psum.15 = f32[432]{0:T(512)S(1)} all-reduce(f32[432]{0:T(512)S(1)} %multiply_reduce_fusion), channel_id=1, replica_groups=mesh['y'=4,'zl'=2,'hid'=16] {'hid'}, use_global_device_ids=true, to_apply=%region_9.10 | all-reduce | flops 432 | bytes 3456 | tf_op jit(solution)/shard_map/psum | solution.py:97
  286.9 33.4 %psum.14 = f32[432]{0:T(512)S(1)} all-reduce(f32[432]{0:T(512)S(1)} %get-tuple-element.5), channel_id=1, replica_groups=mesh['y'=4,'zl'=2,'hid'=16] {'hid'}, use_global_device_ids=true, to_apply=%region_5.6 | all-reduce | flops 432 | bytes 3456 | tf_op jit(solution)/shard_map/psum | solution.py:59
  322.1 53.0 %all-gather.4.cloned.1.call-done = bf16[1728,1536]{1,0:T(8,128)(2,1)} async-done(((bf16[432,1536]{1,0:T(8,128)(2,1)}), bf16[1728,1536]{1,0:T(8,128)(2,1)}) %all-gather.4.cloned.1.call-update) | async-done | bytes 5308432 | tf_op jit(solution)/shard_map/all_gather | solution.py:95
  375.1 9.7 %convolution_convert_fusion = bf16[1728,1536]{1,0:T(8,128)(2,1)} fusion(bf16[1728,1536]{1,0:T(8,128)(2,1)} %all-gather.4.cloned.1.call-done, bf16[768,1536]{1,0:T(8,128)(2,1)S(1)} %copy-done.5, bf16[768,1536]{1,0:T(8,128)(2,1)} %get-tuple-element.11), kind=kOutput, calls=%fused_computation.1 | convolution fusion | flops 5444763648 | bytes 13565952 | tf_op jit(solution)/shard_map/dot_general | solution.py:28
  384.9 9.7 %reshape.98 = bf16[4,432,4,384]{3,2,1,0:T(4,128)(2,1)} reshape(bf16[1728,1536]{1,0:T(8,128)(2,1)} %convolution_convert_fusion) | data formatting | bytes 10616832 | tf_op jit(solution)/shard_map/reshape | solution.py:100
  394.6 5.5 %copy.17 = bf16[4,432,4,384]{3,1,2,0:T(8,128)(2,1)} copy(bf16[4,432,4,384]{3,2,1,0:T(4,128)(2,1)} %reshape.98) | data formatting | bytes 10616832 | tf_op jit(solution)/shard_map/reshape | solution.py:100
  400.1 4.0 fusion.28
  404.2 5.1 fusion.20
  411.0 1.7 collective-permute-start.3
  413.3 4.4 fusion.9
  417.7 7.1 %fusion.3 = f32[768,1024]{1,0:T(8,128)} fusion(bf16[1728,1536]{1,0:T(8,128)(2,1)} %all-gather.4.cloned.1.call-done, bf16[1728,1536]{1,0:T(8,128)(2,1)S(1)} %bitcast.35, s32[]{:T(128)S(6)} %select_n.58), kind=kOutput, calls=%fused_computation.12 | convolution fusion | flops 2717908992 | bytes 9338884 | tf_op jit(solution)/shard_map/dot_general | solution.py:28
  424.8 75.8 %reduce-scatter.5.cloned.1.call-done = bf16[1,432,384]{2,1,0:T(8,128)(2,1)} async-done(((bf16[16,432,384]{2,1,0:T(8,128)(2,1)}), bf16[1,432,384]{2,1,0:T(8,128)(2,1)}) %reduce-scatter.5.cloned.1.call-update) | async-done | bytes 331792 | tf_op jit(solution)/shard_map/reduce_scatter | solution.py:101
  500.6 3.8 collective-permute-start.2
  504.4 3.4 maximum_add_fusion
  509.3 3.7 reshape.100
  513.1 3.9 collective-permute-done.2
  517.0 3.1 convolution_convert_fusion.3
  (69 shorter events, 18.7 us)
Async XLA Ops:
  7.2 184.2 %copy-start = (bf16[8,6144]{1,0:T(8,128)(2,1)S(1)}, bf16[8,6144]{1,0:T(8,128)(2,1)}, u32[]{:S(2)}) copy-start(bf16[8,6144]{1,0:T(8,128)(2,1)} %param.9) | copy-start | bytes 294916
  7.2 132.3 %all-gather.6.cloned.1.call-start = ((), (), s32[]{:S(2)}) async-start(), calls=%async_computation.5 | async-start | bytes 11280384 | tf_op jit(solution)/shard_map/all_gather | solution.py:51
  8.7 28.6 %copy-start.7 = (bf16[768,2,512]{2,1,0:T(2,128)(2,1)S(1)}, bf16[768,2,512]{2,1,0:T(2,128)(2,1)}, u32[]{:S(2)}) copy-start(bf16[768,2,512]{2,1,0:T(2,128)(2,1)} %param.10) | copy-start | bytes 4718596
  11.8 24.6 %collective-permute-start = (bf16[432,768]{1,0:T(8,128)(2,1)S(1)}, bf16[432,768]{1,0:T(8,128)(2,1)S(1)}, u32[]{:S(2)}, u32[]{:S(2)}) collective-permute-start(bf16[432,768]{1,0:T(8,128)(2,1)S(1)} %fusion.33), channel_id=1, source_target_pairs={{0,0},{1,1},{2,2},{3,3},{4,32},{5,33},{6,34},{7,35},{8,64},{9,65},... | collective-permute-start | bytes 1990664 | tf_op jit(solution)/shard_map/ppermute | solution.py:50
  36.3 0.8 copy-start.10
  37.2 208.9 %reduce-scatter.3.cloned.1.call-start = ((), (), s32[]{:S(2)}) async-start(), calls=%async_computation.2 | async-start | bytes 6635520 | tf_op jit(solution)/shard_map/reduce_scatter | solution.py:80
  37.3 1.1 copy-start.9
  38.5 78.8 %collective-permute-start.1 = (bf16[768,1536]{1,0:T(8,128)(2,1)S(1)}, bf16[768,1536]{1,0:T(8,128)(2,1)}, u32[]{:S(2)}, u32[]{:S(2)}) collective-permute-start(bf16[768,1536]{1,0:T(8,128)(2,1)S(1)} %constant_dynamic-update-slice_fusion), channel_id=1, source_target_pairs={{0,16},{16,0},{1,17},{17,1},{2,18},{18,2},{3,19},{19,3},{4,20},{20... | collective-permute-start | bytes 7077896 | tf_op jit(solution)/shard_map/ppermute | solution.py:47
  173.5 2.7 copy-start.2
  173.5 3.4 copy-start.4
  173.5 5.8 %copy-start.6 = (bf16[768,1536]{1,0:T(8,128)(2,1)S(1)}, bf16[768,1536]{1,0:T(8,128)(2,1)}, u32[]{:S(2)}) copy-start(bf16[768,1536]{1,0:T(8,128)(2,1)} %get-tuple-element.11) | copy-start | bytes 7077892
  174.5 10.9 %copy-start.3 = (bf16[216,8,4,384]{3,1,2,0:T(8,128)(2,1)}, bf16[216,8,4,384]{3,1,2,0:T(8,128)(2,1)S(1)}, u32[]{:S(2)}) copy-start(bf16[216,8,4,384]{3,1,2,0:T(8,128)(2,1)S(1)} %copy.24) | copy-start | bytes 15925252
  191.3 1.3 copy-start.8
  191.3 183.8 %all-gather.4.cloned.1.call-start = ((), (), s32[]{:S(2)}) async-start(), calls=%async_computation.3 | async-start | bytes 6635520 | tf_op jit(solution)/shard_map/all_gather | solution.py:95
  320.9 54.3 %copy-start.5 = (bf16[768,1536]{1,0:T(8,128)(2,1)S(1)}, bf16[768,1536]{1,0:T(8,128)(2,1)}, u32[]{:S(2)}) copy-start(bf16[768,1536]{1,0:T(8,128)(2,1)} %get-tuple-element.10) | copy-start | bytes 7077892
  322.1 178.5 %reduce-scatter.5.cloned.1.call-start = ((), (), s32[]{:S(2)}) async-start(), calls=%async_computation.4 | async-start | bytes 5640192 | tf_op jit(solution)/shard_map/reduce_scatter | solution.py:101
  400.1 4.1 slice-start
  400.1 4.1 slice-start.1
  409.3 3.3 copy-start.11
  409.4 8.4 %slice-start.2 = ((s8[5308416]{0:T(1024)(128)(4,1)}), s8[1114112]{0:T(1024)(128)(4,1)S(1)}, s32[]{:S(2)}) async-start(s8[5308416]{0:T(1024)(128)(4,1)} %bitcast.33), calls=%async_computation.8 | async-start | bytes 2228224
  411.0 93.4 %collective-permute-start.3 = (bf16[768,1536]{1,0:T(8,128)(2,1)}, bf16[768,1536]{1,0:T(8,128)(2,1)}, u32[]{:S(2)}, u32[]{:S(2)}) collective-permute-start(bf16[768,1536]{1,0:T(8,128)(2,1)} %pad_maximum_fusion.1), channel_id=1, source_target_pairs={{0,16},{16,0},{1,17},{17,1},{2,18},{18,2},{3,19},{19,3},{4,20},{20... | collective-permute-start | bytes 7077896 | tf_op jit(solution)/shard_map/ppermute | solution.py:113
  413.3 4.4 slice-start.3
  500.6 16.4 %collective-permute-start.2 = (bf16[432,384]{1,0:T(8,128)(2,1)}, bf16[432,384]{1,0:T(8,128)(2,1)}, u32[]{:S(2)}, u32[]{:S(2)}) collective-permute-start(bf16[432,384]{1,0:T(8,128)(2,1)} %bitcast.41), channel_id=1, source_target_pairs={{0,0},{1,1},{2,2},{3,3},{4,32},{5,33},{6,34},{7,35},{8,64},{9,65},... | collective-permute-start | bytes 995336 | tf_op jit(solution)/shard_map/ppermute | solution.py:116
  509.3 10.7 %copy-start.1 = (bf16[8,6144]{1,0:T(8,128)(2,1)S(1)}, bf16[8,6144]{1,0:T(8,128)(2,1)}, u32[]{:S(2)}) copy-start(bf16[8,6144]{1,0:T(8,128)(2,1)} %param.9) | copy-start | bytes 294916
Sparse Core Ops, SparseCore 0:
  37.3 102.1 all-gather.5
  191.5 54.6 reduce-scatter.2
  322.2 52.9 all-gather.3
  400.2 100.3 reduce-scatter.4

commit v2 on v1

v2 whole, which is shorter than its diff:
```python
import functools

import jax
import jax.numpy as jnp
from jax import lax
from jax.experimental import pallas as pl
from jax.experimental.pallas import tpu as pltpu
from jax.sharding import Mesh
from jax.sharding import PartitionSpec as P

CAP = 432
SUB = 384
PART = 128
TOK = ("y", "zl")
HID = ("zh", "x", "c")
ALL = TOK + HID
MESH = pl.DeviceIdType.MESH
F32 = jnp.float32
BF16 = jnp.bfloat16


def swap_pairs():
    pairs = []
    for y in range(4):
        for zl in range(2):
            for h in range(16):
                to_y, to_h = h // 4, y * 4 + h % 4
                pairs.append(((y * 2 + zl) * 16 + h, (to_y * 2 + zl) * 16 + to_h))
    return pairs


def dot_f32(left, right, dims):
    return lax.dot_general(left, right, ((dims[0], dims[1]), ((), ())), preferred_element_type=F32)


def kernel(
    xin, win, router, other,
    back_out, score_out, dgu_out, dd_out,
    rows, wgt, psend, pown, prelay, precv, lsend, lrecv, gate, sacc, mids,
    gsend, grecv, bsend, bown, brecv, xrelay, xrecv, zsend, zrecv, srow, srecv,
    ssem, rsem,
):
    y, zl, zh, x, c = (lax.axis_index(a) for a in ALL)
    yr, yl, yo = (y + 1) % 4, (y + 3) % 4, (y + 2) % 4
    xr, xl, xo = (x + 1) % 4, (x + 3) % 4, (x + 2) % 4
    D = rows.shape[2]
    own = D // 2

    number = {}
    started = []

    def copy(key, src, dst, **to):
        i = number.setdefault(key, len(number))
        return pltpu.make_async_remote_copy(
            src_ref=src, dst_ref=dst, send_sem=ssem.at[i], recv_sem=rsem.at[i],
            device_id=to, device_id_type=MESH,
        )

    def start(cp):
        cp.start()
        started.append(cp)
        return cp

    barrier = pltpu.get_barrier_semaphore()
    peers = (
        dict(y=yr), dict(y=yl), dict(y=yo), dict(zl=1 - zl), dict(zh=1 - zh),
        dict(x=xr), dict(x=xl), dict(x=xo), dict(c=1 - c),
    )
    for peer in peers:
        pl.semaphore_signal(barrier, inc=1, device_id=peer, device_id_type=MESH)
    pl.semaphore_wait(barrier, len(peers))

    def place(zh_, x_, c_):
        row = pl.multiple_of((2 * zh_ + x_ // 2) * CAP, 16)
        col = pl.multiple_of((2 * (x_ % 2) + c_) * SUB, 128)
        return rows.at[:, pl.ds(row, CAP), pl.ds(col, SUB)]

    def weights(sub, zl_):
        return wgt.at[sub, pl.ds(pl.multiple_of(zl_ * own, 16), own), :]

    here = place(zh, x, c)
    to_zh = start(copy("zh", xin, here, zh=1 - zh))
    from_l0 = start(copy("xr0", xin, here, x=xr))
    from_r0 = start(copy("xl0", xin, here, x=xl))
    cores = [start(copy("c0", xin, here, c=1 - c))]
    for sub in range(4):
        start(copy(("w", sub), win.at[sub], weights(sub, zl), zl=1 - zl))
    here[...] = xin[...]

    def put_weights(i, carry):
        for sub in range(4):
            at = pl.multiple_of(zl * own + i * 96, 16)
            wgt[sub, pl.ds(at, 96), :] = win[sub, pl.ds(pl.multiple_of(i * 96, 16), 96), :]
        return carry

    lax.fori_loop(0, own // 96, put_weights, 0)

    to_zh.wait_recv()
    there = place(1 - zh, x, c)
    from_l1 = start(copy("xr1", there, there, x=xr))
    from_r1 = start(copy("xl1", there, there, x=xl))
    cores.append(start(copy("c1", there, there, c=1 - c)))

    from_l0.wait_recv()
    at = place(zh, xl, c)
    from_lo = start(copy("xro", at, at, x=xr))
    cores.append(start(copy("c2", at, at, c=1 - c)))
    from_r0.wait_recv()
    at = place(zh, xr, c)
    cores.append(start(copy("c3", at, at, c=1 - c)))
    from_r1.wait_recv()
    at = place(1 - zh, xr, c)
    from_ro = start(copy("xlo", at, at, x=xl))
    cores.append(start(copy("c4", at, at, c=1 - c)))
    from_l1.wait_recv()
    at = place(1 - zh, xl, c)
    cores.append(start(copy("c5", at, at, c=1 - c)))
    from_lo.wait_recv()
    at = place(zh, xo, c)
    cores.append(start(copy("c6", at, at, c=1 - c)))
    from_ro.wait_recv()
    at = place(1 - zh, xo, c)
    cores.append(start(copy("c7", at, at, c=1 - c)))
    for cp in cores:
        cp.wait_recv()

    def block_of(ref, which, t):
        return ref[which, pl.ds(pl.multiple_of(t * CAP, 16), CAP), :]

    def rs(key, j):
        kind, half = key
        side = {
            "far_r": lambda: (psend.at[j, 0, half], prelay.at[j, 0], yr),
            "far_l": lambda: (psend.at[j, 0, half], prelay.at[j, 1], yl),
            "near_r": lambda: (psend.at[j, 1, half], precv.at[j, 0, half], yr),
            "near_l": lambda: (psend.at[j, 2, half], precv.at[j, 1, half], yl),
        }[kind]
        src, dst, to = side()
        return copy(("rs", key, j), src, dst, y=to)

    def logit(r):
        to = (yo, yr, yl)[r]
        return copy(("lg", r), lsend.at[r], lrecv.at[r], y=to)

    def pre_of(j):
        def one(r, carry):
            t = (y + jnp.where(r == 0, 2, jnp.where(r == 1, 1, jnp.where(r == 2, 3, 0)))) % 4
            x_in = block_of(rows, 0, t)
            x_cot = block_of(rows, 1, t)
            g0 = dot_f32(x_in, wgt[2 * j, :, : 2 * PART], ((1,), (0,)))
            g1 = dot_f32(x_in, wgt[2 * j + 1, :, : 2 * PART], ((1,), (0,)))
            w_d = jnp.concatenate([wgt[2 * j, :, 2 * PART :], wgt[2 * j + 1, :, 2 * PART :]], axis=1)
            d = dot_f32(x_cot, w_d, ((1,), (0,)))

            @pl.when(r < 3)
            def _():
                psend[j, r, 0, :, : 2 * PART] = g0.astype(BF16)
                psend[j, r, 1, :, : 2 * PART] = g1.astype(BF16)
                psend[j, r, 0, :, 2 * PART :] = d[:, :PART].astype(BF16)
                psend[j, r, 1, :, 2 * PART :] = d[:, PART:].astype(BF16)

            @pl.when(r == 3)
            def _():
                pown[j, 0, :, : 2 * PART] = g0
                pown[j, 1, :, : 2 * PART] = g1
                pown[j, 0, :, 2 * PART :] = d[:, :PART]
                pown[j, 1, :, 2 * PART :] = d[:, PART:]

            if j == 0:
                lsend[r, :, :CAP] = dot_f32(router[...], x_in, ((1,), (1,)))

            @pl.when(r == 0)
            def _():
                rs(("far_r", 0), j).start()
                rs(("far_l", 1), j).start()
                if j == 0:
                    logit(0).start()

            @pl.when(r == 1)
            def _():
                rs(("near_r", 1), j).start()
                if j == 0:
                    logit(1).start()

            @pl.when(r == 2)
            def _():
                rs(("near_l", 0), j).start()
                if j == 0:
                    logit(2).start()

            return carry

        lax.fori_loop(0, 4, one, 0)
        for key in (("far_r", 0), ("far_l", 1), ("near_r", 1), ("near_l", 0)):
            started.append(rs(key, j))
        if j == 0:
            for r in range(3):
                started.append(logit(r))

    def add_relays(j):
        for side, slot, half, kind in ((0, 1, 0, "far_r"), (1, 2, 1, "far_l")):
            rs((kind, half), j).wait_recv()

            def add(i, carry):
                at = pl.ds(pl.multiple_of(i * 144, 16), 144)
                total = psend[j, slot, half, at, :].astype(F32) + prelay[j, side, at, :].astype(F32)
                psend[j, slot, half, at, :] = total.astype(BF16)
                return carry

            lax.fori_loop(0, 3, add, 0)
            start(rs(("near_r" if side == 0 else "near_l", half), j))

    def gates():
        for r in range(3):
            logit(r).wait_recv()
        logits = (lsend[3] + lrecv[0]) + (lrecv[1] + lrecv[2])
        experts = lax.broadcasted_iota(jnp.int32, (8, 512), 0)
        picked = jnp.sum(jnp.where(other[...] == experts, logits[:8], 0.0), axis=0, keepdims=True)
        margin = logits[:1] - picked
        row = jnp.where(other[:1] >= 0, jax.nn.sigmoid(margin), 0.0)
        gate[...] = jnp.transpose(jnp.broadcast_to(row, (PART, 512)))
        sacc[...] = jnp.zeros_like(sacc)

    def gather(key, j):
        kind, half = key
        sub = 2 * j + half
        t, to = {"own_r": (y, yr), "own_l": (y, yl), "fwd_r": (yl, yr), "fwd_l": (yr, yl)}[kind]
        at = mids.at[sub, pl.ds(pl.multiple_of(t * CAP, 16), CAP), :]
        return copy(("ag", key, j), at, at, y=to)

    def pointwise(j):
        for half in range(2):
            for kind in ("near_r", "near_l"):
                rs((kind, half), j).wait_recv()
        for half in range(2):
            sub = 2 * j + half

            def one(i, carry):
                at = pl.ds(pl.multiple_of(i * 48, 16), 48)
                pre = pown[j, half, at, :] + (
                    precv[j, 0, half, at, :].astype(F32) + precv[j, 1, half, at, :].astype(F32)
                )
                g, up, raw = pre[:, :PART], pre[:, PART : 2 * PART], pre[:, 2 * PART :]
                sigma = jax.nn.sigmoid(g)
                active = g * sigma
                slope = sigma * (1.0 + g * (1.0 - sigma))
                product = active * up
                scale = gate[at, :]
                sacc[at, :] += product * raw
                upstream = scale * raw
                to = pl.ds(pl.multiple_of(y * CAP + i * 48, 16), 48)
                mids[sub, to, :PART] = (upstream * up * slope).astype(BF16)
                mids[sub, to, PART : 2 * PART] = (upstream * active).astype(BF16)
                mids[sub, to, 2 * PART :] = (scale * product).astype(BF16)
                return carry

            lax.fori_loop(0, CAP // 48, one, 0)
            for kind in (("own_r", half), ("own_l", half)):
                start(gather(kind, j))

    def forward(j):
        gather(("own_r", 0), j).wait_recv()
        start(gather(("fwd_r", 0), j))
        gather(("own_l", 1), j).wait_recv()
        start(gather(("fwd_l", 1), j))

    def gathered(j):
        for key in (("own_r", 1), ("own_l", 0), ("fwd_r", 0), ("fwd_l", 1)):
            gather(key, j).wait_recv()

    def exchange(j):
        return copy(("gz", j), gsend.at[j], grecv.at[j], zl=1 - zl)

    def grads_of(j):
        def tile(at):
            left = rows[0, :, pl.ds(at, 256)]
            mid_gu = jnp.concatenate([mids[2 * j, :, : 2 * PART], mids[2 * j + 1, :, : 2 * PART]], axis=1)
            gu = dot_f32(left, mid_gu, ((0,), (0,)))
            left = rows[1, :, pl.ds(at, 256)]
            mid_d = jnp.concatenate([mids[2 * j, :, 2 * PART :], mids[2 * j + 1, :, 2 * PART :]], axis=1)
            return gu, dot_f32(left, mid_d, ((0,), (0,)))

        def one(i, carry):
            mine = i >= own // 256
            k = i % (own // 256)
            half = jnp.where(mine, zl, 1 - zl)
            gu, d = tile(pl.multiple_of(half * own + k * 256, 256))
            to = pl.ds(pl.multiple_of(k * 256, 256), 256)

            @pl.when(jnp.logical_not(mine))
            def _():
                for s in range(2):
                    gsend[j, s, to, : 2 * PART] = gu[:, 2 * PART * s : 2 * PART * (s + 1)].astype(BF16)
                    gsend[j, s, to, 2 * PART :] = d[:, PART * s : PART * (s + 1)].astype(BF16)

            @pl.when(mine)
            def _():
                for s in range(2):
                    sub = 2 * j + s
                    dgu_out[to, sub * PART : (sub + 1) * PART] = gu[:, 2 * PART * s : 2 * PART * s + PART]
                    dgu_out[to, 512 + sub * PART : 512 + (sub + 1) * PART] = gu[
                        :, 2 * PART * s + PART : 2 * PART * (s + 1)
                    ]
                    dd_out[to, sub * PART : (sub + 1) * PART] = d[:, PART * s : PART * (s + 1)]

            @pl.when(i == own // 256 - 1)
            def _():
                exchange(j).start()

            return carry

        lax.fori_loop(0, 2 * (own // 256), one, 0)
        started.append(exchange(j))

    def add_grads(j):
        exchange(j).wait_recv()

        def one(i, carry):
            at = pl.ds(pl.multiple_of(i * 64, 16), 64)
            for s in range(2):
                sub = 2 * j + s
                got = grecv[j, s, at, :].astype(F32)
                dgu_out[at, sub * PART : (sub + 1) * PART] += got[:, :PART]
                dgu_out[at, 512 + sub * PART : 512 + (sub + 1) * PART] += got[:, PART : 2 * PART]
                dd_out[at, sub * PART : (sub + 1) * PART] += got[:, 2 * PART :]
            return carry

        lax.fori_loop(0, own // 64, one, 0)

    def score(key):
        src, dst, to = {
            "c": (0, 0, dict(c=1 - c)), "zh": (1, 1, dict(zh=1 - zh)),
            "x0": (2, 2, dict(x=xr)), "x1": (2, 3, dict(x=xl)), "x2": (2, 4, dict(x=xo)),
        }[key]
        return copy(("sc", key), srow.at[src], srecv.at[dst], **to)

    def scores():
        total = jnp.sum(jnp.transpose(sacc[...]), axis=0, keepdims=True)
        srow[0] = jnp.broadcast_to(total, (8, 512))
        start(score("c"))

    def scores_zh():
        score("c").wait_recv()
        srow[1] = srow[0] + srecv[0]
        start(score("zh"))

    def scores_x():
        score("zh").wait_recv()
        srow[2] = srow[1] + srecv[1]
        for key in ("x0", "x1", "x2"):
            start(score(key))

    def scores_end():
        for key in ("x0", "x1", "x2"):
            score(key).wait_recv()
        score_out[...] = (srow[2] + srecv[2]) + (srecv[3] + srecv[4])

    def pair(k, r):
        return copy(("bc", k, r), bsend.at[r, k], brecv.at[r, k], c=1 - c)

    def ring(key):
        kind, half = key
        src, dst, to = {
            "far_r": lambda: (bown.at[0, half], xrelay.at[0], xr),
            "far_l": lambda: (bown.at[0, half], xrelay.at[1], xl),
            "near_r": lambda: (bown.at[1, half], xrecv.at[0, half], xr),
            "near_l": lambda: (bown.at[2, half], xrecv.at[1, half], xl),
        }[kind]()
        return copy(("bx", key), src, dst, x=to)

    def last():
        return copy("bz", zsend, zrecv, zh=1 - zh)

    def add_tiles(out, a, b, also=None):
        def one(i, carry):
            at = pl.ds(pl.multiple_of(i * 144, 16), 144)
            total = a[at, :].astype(F32) + b[at, :].astype(F32)
            if also is not None:
                total = total + also[at, :].astype(F32)
            out[at, :] = total.astype(out.dtype)
            return carry

        lax.fori_loop(0, 3, one, 0)

    def back():
        for r, x_ in enumerate((xo, xr, xl, x)):

            def one(k, carry):
                t = 2 * k + x_ // 2
                col = pl.multiple_of((x_ % 2) * 2 * SUB, 128)
                acc = None
                for sub in range(4):
                    m = mids[sub, pl.ds(pl.multiple_of(t * CAP, 16), CAP), : 2 * PART]
                    w = wgt[sub, pl.ds(col, 2 * SUB), : 2 * PART]
                    part = dot_f32(m, w, ((1,), (1,)))
                    acc = part if acc is None else acc + part
                low, high = acc[:, :SUB], acc[:, SUB:]
                bown[r, k] = jnp.where(c == 0, low, high).astype(BF16)
                bsend[r, k] = jnp.where(c == 0, high, low).astype(BF16)
                return carry

            lax.fori_loop(0, 2, one, 0)
            for k in range(2):
                start(pair(k, r))

    def back_ring():
        for r in range(4):
            for k in range(2):
                pair(k, r).wait_recv()
                add_tiles(bown.at[r, k], bown.at[r, k], brecv.at[r, k])
            if r == 0:
                start(ring(("far_r", 0)))
                start(ring(("far_l", 1)))
            if r == 1:
                start(ring(("near_r", 1)))
            if r == 2:
                start(ring(("near_l", 0)))
        ring(("far_r", 0)).wait_recv()
        add_tiles(bown.at[1, 0], bown.at[1, 0], xrelay.at[0])
        start(ring(("near_r", 0)))
        ring(("far_l", 1)).wait_recv()
        add_tiles(bown.at[2, 1], bown.at[2, 1], xrelay.at[1])
        start(ring(("near_l", 1)))

    def back_end():
        for half in range(2):
            for kind in ("near_r", "near_l"):
                ring((kind, half)).wait_recv()
        add_tiles(zsend, bown.at[3, 1 - zh], xrecv.at[0, 1 - zh], xrecv.at[1, 1 - zh])
        start(last())
        last().wait_recv()
        add_tiles(zsend_own := bown.at[3, zh], bown.at[3, zh], xrecv.at[0, zh], xrecv.at[1, zh])
        add_tiles(back_out, zsend_own, zrecv)

    for sub in range(2):
        copy(("w", sub), win.at[sub], weights(sub, zl), zl=1 - zl).wait_recv()
    pre_of(0)
    for sub in range(2, 4):
        copy(("w", sub), win.at[sub], weights(sub, zl), zl=1 - zl).wait_recv()
    pre_of(1)
    add_relays(0)
    gates()
    add_relays(1)
    pointwise(0)
    pointwise(1)
    scores()
    forward(0)
    scores_zh()
    gathered(0)
    scores_x()
    grads_of(0)
    forward(1)
    scores_end()
    gathered(1)
    back()
    back_ring()
    grads_of(1)
    add_grads(0)
    back_end()
    add_grads(1)
    for cp in started:
        cp.wait_send()


def exchange_and_compute(xin, win, router, other):
    own = win.shape[1]
    rows_all = 4 * CAP
    vm = pltpu.VMEM
    piece = (CAP, SUB)
    flops = 2 * rows_all * 2 * own * 4 * SUB * 8 // 3
    return pl.pallas_call(
        kernel,
        out_shape=(
            jax.ShapeDtypeStruct(piece, BF16),
            jax.ShapeDtypeStruct((8, 512), F32),
            jax.ShapeDtypeStruct((own, 1024), F32),
            jax.ShapeDtypeStruct((own, 512), F32),
        ),
        in_specs=[pl.BlockSpec(memory_space=vm)] * 4,
        out_specs=[pl.BlockSpec(memory_space=vm)] * 4,
        scratch_shapes=[
            vm((2, rows_all, 2 * own), BF16),
            vm((4, 2 * own, SUB), BF16),
            vm((2, 3, 2) + piece, BF16),
            vm((2, 2) + piece, F32),
            vm((2, 2) + piece, BF16),
            vm((2, 2, 2) + piece, BF16),
            vm((4, 16, 512), F32),
            vm((3, 16, 512), F32),
            vm((512, PART), F32),
            vm((512, PART), F32),
            vm((4, rows_all, SUB), BF16),
            vm((2, 2, own, SUB), BF16),
            vm((2, 2, own, SUB), BF16),
            vm((4, 2) + piece, BF16),
            vm((4, 2) + piece, BF16),
            vm((4, 2) + piece, BF16),
            vm((2,) + piece, BF16),
            vm((2, 2) + piece, BF16),
            vm(piece, BF16),
            vm(piece, BF16),
            vm((3, 8, 512), F32),
            vm((5, 8, 512), F32),
            pltpu.SemaphoreType.DMA((80,)),
            pltpu.SemaphoreType.DMA((80,)),
        ],
        cost_estimate=pl.CostEstimate(flops=flops, bytes_accessed=20 << 20, transcendentals=CAP * 512),
        compiler_params=pltpu.CompilerParams(
            collective_id=0, has_side_effects=True, vmem_limit_bytes=67043328
        ),
    )(xin, win, router, other)


def local(tokens, cotangent, expert_choice, router, gate_up, w_down):
    own, hid = w_down.shape
    first = expert_choice[:, 0]
    second = expert_choice[:, 1]
    in_first = first == 0
    in_second = second == 0
    routed = jnp.logical_or(in_first, in_second)
    flags = routed.astype(jnp.int32)
    slot_rank = jnp.cumsum(flags) - flags
    slot_ids = jnp.arange(CAP, dtype=jnp.int32)
    placed = jnp.logical_and(routed[None, :], slot_rank[None, :] == slot_ids[:, None])
    select = placed.astype(BF16)

    picked = [dot_f32(select, a, ((1,), (0,))).astype(BF16) for a in (tokens, cotangent)]
    xin = lax.ppermute(jnp.stack(picked), ALL, swap_pairs())

    win = jnp.stack(
        [
            jnp.concatenate(
                [
                    gate_up[:, 0, PART * s : PART * (s + 1)],
                    gate_up[:, 1, PART * s : PART * (s + 1)],
                    w_down[:, PART * s : PART * (s + 1)],
                ],
                axis=1,
            )
            for s in range(hid // PART)
        ]
    )
    router_cols = lax.dynamic_slice_in_dim(router, lax.axis_index("y") * 2 * own, 2 * own, 1)
    router_cols = jnp.pad(router_cols, ((0, 8), (0, 0)))
    other = jnp.sum(jnp.where(placed, (first + second + 1)[None, :], 0), axis=1) - 1
    other = jnp.pad(other, (0, 512 - CAP), constant_values=-1)
    other = jnp.broadcast_to(other[None, :], (8, 512))

    back, score, d_gu, d_down = exchange_and_compute(xin, win, router_cols, other)

    back = lax.ppermute(back, ALL, swap_pairs())
    grad_tokens = dot_f32(select, back, ((0,), (0,))).astype(BF16)
    token_score = jnp.sum(jnp.where(placed, score[0, :CAP, None], 0.0), axis=0)
    d_combine = jnp.stack(
        [jnp.where(in_first, token_score, 0.0), jnp.where(in_second, token_score, 0.0)], axis=1
    )
    return (grad_tokens, d_combine, d_gu.reshape(own, 2, hid), d_down)


def solution(mesh):
    split = Mesh(mesh.devices.reshape(4, 2, 2, 4, 2), ALL)
    return jax.shard_map(
        local,
        mesh=split,
        in_specs=(
            P(TOK, HID),
            P(TOK, HID),
            P(TOK, None),
            P(),
            P(TOK, None, HID),
            P(TOK, HID),
        ),
        out_specs=(P(TOK, HID), P(TOK, None), P(TOK, None, HID), P(TOK, HID)),
        check_vma=False,
    )
```

time: 528 us -> 257 us (0.49)
  waiting for transfers between devices: 297 us -> 11.6 us
  Pallas kernels: 0 us -> 204 us
  blocking collectives: 71.2 us -> 0 us
  local copies, waits for them, and re-layouts: 63.7 us -> 12.7 us
  matrix products: 46.2 us -> 5.2 us
  between operations: 14.1 us -> 0.88 us
  other arithmetic: 19.1 us -> 6.74 us
    pallas_call x0 -> x1, Pallas kernels: none -> 204 us  [exchange_and_compute(): pl.pallas_call(kernel, out_shape=(jax.ShapeDtypeStruct(piece, BF16), jax....]
    reduce_scatter x2 -> x0, waiting for transfers between devices: 128 us -> none  [the longest x1 75.8 us: local(): back = lax.psum_scatter(back, 'hid', scatter_dimension=0, tiled=False)]
    ppermute x3 -> x1, waiting for transfers between devices: 93.3 us -> 9.49 us  [local(): xin = lax.ppermute(jnp.stack(picked), ALL, swap_pairs())]
    psum x2 -> x0, blocking collectives: 71.2 us -> none  [the longest x1 37.8 us: local(): scores = lax.psum(score_part, 'hid')]
    all_gather x2 -> x0, waiting for transfers between devices: 71 us -> none  [the longest x1 53 us: local(): mids = lax.all_gather(mids, 'y', axis=0, tiled=True)]
    reshape x5 -> x1, local copies, waits for them, and re-layouts: 48.1 us -> 5.58 us  [local(): return (grad_tokens, d_combine, d_gu.reshape(own, 2, hid), d_down)]
    dot_general x10 -> x3, matrix products: 46.2 us -> 5.2 us  [dot_f32(): lax.dot_general(left, right, ((dims[0], dims[1]), ((), ())), preferred_el...]
    unnamed x36 -> x25, local copies, waits for them, and re-layouts: 9.92 us -> 1.41 us
  transfers between devices with their start and end apart: 8 -> 2, of which waited for: 7 -> 2; matrix products, arithmetic and copies ran while one was open for 7% -> 6% of each run, Pallas kernels for 0% -> 0%
where the time goes in v2:
time: 257 us; the launch traced here: 255 us
  Pallas kernels  204 us (79%)
  starting transfers between devices  14 us (5%)
  local copies, waits for them, and re-layouts  12.7 us (5%)
  waiting for transfers between devices  11.6 us (5%)
  other arithmetic  6.74 us (3%)
  matrix products  5.2 us (2%)
    pallas_call x1, Pallas kernels, exchange_and_compute(): pl.pallas_call(kernel, out_shape=(jax.ShapeDtypeStruct(piece, BF16), jax....  204 us
    ppermute x1, waiting for transfers between devices, local(): xin = lax.ppermute(jnp.stack(picked), ALL, swap_pairs())  9.49 us
    ppermute x1, starting transfers between devices, local(): xin = lax.ppermute(jnp.stack(picked), ALL, swap_pairs())  7.91 us
    ppermute x1, starting transfers between devices, local(): back = lax.ppermute(back, ALL, swap_pairs())  6.07 us
    reshape x1, local copies, waits for them, and re-layouts, local(): return (grad_tokens, d_combine, d_gu.reshape(own, 2, hid), d_down)  5.58 us
    dot_general x3, matrix products, dot_f32(): lax.dot_general(left, right, ((dims[0], dims[1]), ((), ())), preferred_el...  5.2 us
  transfers between devices with their start and end apart: 2, of which 2 were waited for; matrix products, arithmetic and copies ran while one was open for 6% of the time, Pallas kernels for 0%

profile of v2, /device:TPU:24, one launch (start us, length us, event | category | flops | bytes accessed | tf_op | source)
XLA Modules:
  0.0 255.2 jit_solution(10015771918477889067)
XLA Ops:
  0.6 0.8 convert_reduce_fusion
  1.5 0.3 reduce-window.9
  1.7 0.1 slice.69
  1.9 0.1 slice_reduce_fusion
  2.0 0.0 copy-start.5
  2.0 0.1 bitcast_subtract_fusion
  2.1 2.2 fusion.21
  4.3 0.0 copy-start
  4.3 0.9 fusion.18
  5.2 0.1 pad_maximum_fusion.1
  5.3 7.9 %collective-permute-start = (bf16[2,432,384]{2,1,0:T(8,128)(2,1)S(1)}, bf16[2,432,384]{2,1,0:T(8,128)(2,1)}, u32[]{:S(2)}, u32[]{:S(2)}) collective-permute-start(bf16[2,432,384]{2,1,0:T(8,128)(2,1)S(1)} %pad_maximum_fusion.1), channel_id=1, source_target_pairs={{0,0},{1,1},{2,2},{3,3},{4,32},{5,33},{6,34},{7,35},{8,64},{9,65},... | collective-permute-start | bytes 1990664 | tf_op jit(solution)/shard_map/ppermute | solution.py:528
  13.2 2.7 %fusion.24 = (bf16[768,1,128]{2,1,0:T(2,128)(2,1)S(1)}, bf16[768,1,128]{2,1,0:T(2,128)(2,1)S(1)}, bf16[768,1,128]{2,1,0:T(2,128)(2,1)S(1)}, bf16[768,1,128]{2,1,...) fusion(bf16[768,2,512]{2,1,0:T(2,128)(2,1)S(1)} %copy-done), kind=kLoop, calls=%fused_computation.41 | loop fusion | bytes 3145728 | tf_op jit(solution)/shard_map/slice | solution.py:534
  16.0 0.0 copy-start.2
  16.2 0.6 select_reduce_fusion.1
  16.9 0.7 constant_dynamic-slice_fusion
  17.6 0.6 pad.8.router
  18.2 0.1 fusion.25
  18.4 0.2 maximum_bitcast_fusion
  18.5 0.2 maximum_bitcast_fusion.2
  18.7 1.8 pad_maximum_fusion.win
  20.5 9.5 %collective-permute-done.xin = bf16[2,432,384]{2,1,0:T(8,128)(2,1)} collective-permute-done((bf16[2,432,384]{2,1,0:T(8,128)(2,1)S(1)}, bf16[2,432,384]{2,1,0:T(8,128)(2,1)}, u32[]{:S(2)}, u32[]{:S(2)}) %collective-permute-start) | collective-permute-done | bytes 663584 | tf_op jit(solution)/shard_map/ppermute | solution.py:528
  30.0 0.6 broadcast_in_dim.43.other
  30.6 204.1 %shard_map.93 = (bf16[432,384]{1,0:T(8,128)(2,1)}, f32[8,512]{1,0:T(8,128)}, f32[768,1024]{1,0:T(8,128)}, f32[768,512]{1,0:T(8,128)}) custom-call(bf16[2,432,384]{2,1,0:T(8,128)(2,1)} %collective-permute-done.xin, bf16[4,768,384]{2,1,0:T(8,128)(2,1)} %pad_maximum_fusion.win, bf16[16,1536]{1,0:T(8,128)(2,1)} %pad.8.router, s32[8,512]{1,0:T(8,128)} %broadcast_in_dim.43.other), custom_call_target="tpu_custom_call" | custom-call | flops 21743271936 | bytes 20971520 | tf_op jit(solution)/shard_map/pallas_call | solution.py:471
  234.7 0.7 slice.68
  235.4 1.3 select_reduce_fusion
  236.7 6.1 %collective-permute-start.1 = (bf16[432,384]{1,0:T(8,128)(2,1)}, bf16[432,384]{1,0:T(8,128)(2,1)S(1)}, u32[]{:S(2)}, u32[]{:S(2)}) collective-permute-start(bf16[432,384]{1,0:T(8,128)(2,1)} %get-tuple-element.8), channel_id=1, source_target_pairs={{0,0},{1,1},{2,2},{3,3},{4,32},{5,33},{6,34},{7,35},{8,64},{9,65},... | collective-permute-start | bytes 995336 | tf_op jit(solution)/shard_map/ppermute | solution.py:551
  242.8 0.8 compare_select_fusion.1
  243.6 5.6 %reshape.85 = f32[768,2,512]{2,1,0:T(2,128)} reshape(f32[768,1024]{1,0:T(8,128)} %get-tuple-element.10) | data formatting | bytes 6291456 | tf_op jit(solution)/shard_map/reshape | solution.py:557
  249.2 0.6 pad_maximum_fusion.2
  249.8 2.1 collective-permute-done.1
  251.9 2.1 convolution_convert_fusion
  254.1 1.1 copy.59
  (25 shorter events, 0.3 us)
Async XLA Ops:
  2.0 14.2 %copy-start.5 = (pred[1536]{0:T(1024)(128)(4,1)}, pred[1536]{0:T(1024)(128)(4,1)S(1)}, u32[]{:S(2)}) copy-start(pred[1536]{0:T(1024)(128)(4,1)S(1)} %reduce) | copy-start | bytes 4612
  2.1 14.1 %copy-start.3 = (s32[1536]{0:T(1024)}, s32[1536]{0:T(1024)S(1)}, u32[]{:S(2)}) copy-start(s32[1536]{0:T(1024)S(1)} %bitcast_subtract_fusion) | copy-start | bytes 18436
  2.1 2.2 copy-start.7
  4.3 8.9 %copy-start = (bf16[768,2,512]{2,1,0:T(2,128)(2,1)S(1)}, bf16[768,2,512]{2,1,0:T(2,128)(2,1)}, u32[]{:S(2)}) copy-start(bf16[768,2,512]{2,1,0:T(2,128)(2,1)} %param.10) | copy-start | bytes 4718596
  5.3 24.7 %collective-permute-start = (bf16[2,432,384]{2,1,0:T(8,128)(2,1)S(1)}, bf16[2,432,384]{2,1,0:T(8,128)(2,1)}, u32[]{:S(2)}, u32[]{:S(2)}) collective-permute-start(bf16[2,432,384]{2,1,0:T(8,128)(2,1)S(1)} %pad_maximum_fusion.1), channel_id=1, source_target_pairs={{0,0},{1,1},{2,2},{3,3},{4,32},{5,33},{6,34},{7,35},{8,64},{9,65},... | collective-permute-start | bytes 1990664 | tf_op jit(solution)/shard_map/ppermute | solution.py:528
  16.0 2.2 copy-start.2
  236.7 15.2 %collective-permute-start.1 = (bf16[432,384]{1,0:T(8,128)(2,1)}, bf16[432,384]{1,0:T(8,128)(2,1)S(1)}, u32[]{:S(2)}, u32[]{:S(2)}) collective-permute-start(bf16[432,384]{1,0:T(8,128)(2,1)} %get-tuple-element.8), channel_id=1, source_target_pairs={{0,0},{1,1},{2,2},{3,3},{4,32},{5,33},{6,34},{7,35},{8,64},{9,65},... | collective-permute-start | bytes 995336 | tf_op jit(solution)/shard_map/ppermute | solution.py:551
  243.6 8.4 %copy-start.4 = (s32[1536]{0:T(1024)S(1)}, s32[1536]{0:T(1024)}, u32[]{:S(2)}) copy-start(s32[1536]{0:T(1024)} %copy-done.3) | copy-start | bytes 18436
  243.6 8.3 %copy-start.6 = (pred[1536]{0:T(1024)(128)(4,1)S(1)}, pred[1536]{0:T(1024)(128)(4,1)}, u32[]{:S(2)}) copy-start(pred[1536]{0:T(1024)(128)(4,1)} %copy-done.5) | copy-start | bytes 4612
  249.8 4.3 %copy-start.1 = (f32[768,512]{1,0:T(8,128)S(1)}, f32[768,512]{1,0:T(8,128)}, u32[]{:S(2)}) copy-start(f32[768,512]{1,0:T(8,128)} %get-tuple-element.40) | copy-start | bytes 4718596

commit v3 on v2

v3 whole, which is shorter than its diff:
```python
import jax
import jax.numpy as jnp
from jax import lax
from jax.experimental import pallas as pl
from jax.experimental.pallas import tpu as pltpu
from jax.sharding import Mesh
from jax.sharding import PartitionSpec as P

CAP = 432
SUB = 384
PART = 128
TOK = ("y", "zl")
HID = ("zh", "x", "c")
ALL = TOK + HID
MESH = pl.DeviceIdType.MESH
F32 = jnp.float32
BF16 = jnp.bfloat16


def dot_f32(left, right, dims):
    return lax.dot_general(left, right, ((dims[0], dims[1]), ((), ())), preferred_element_type=F32)


def kernel(
    tokens, cotangent, win, router, meta,
    gtok_out, score_out, dgu_out, dd_out,
    select, xin, rows, wgt, psend, pown, prelay, precv, lsend, lrecv, gate, sacc, mids,
    gsend, grecv, bown, brecv, xrelay, xrecv, zsend, zrecv, fsend, fin, srow, srecv, labels,
    ssem, rsem,
):
    y, zl, zh, x, c = (lax.axis_index(a) for a in ALL)
    yr, yl, yo = (y + 1) % 4, (y + 3) % 4, (y + 2) % 4
    xr, xl, xo = (x + 1) % 4, (x + 3) % 4, (x + 2) % 4
    D = rows.shape[2]
    own = D // 2
    swap_y, swap_zh, swap_x = 2 * zh + x // 2, y // 2, 2 * (y % 2) + x % 2
    fixed = swap_y == y
    swap = dict(y=swap_y, zh=swap_zh, x=swap_x)

    number = {}
    started = []

    def index(key, n=1):
        if key not in number:
            number[key] = number.get("next", 0)
            number["next"] = number[key] + n
        return number[key]

    def copy_at(i, src, dst, **to):
        return pltpu.make_async_remote_copy(
            src_ref=src, dst_ref=dst, send_sem=ssem.at[i], recv_sem=rsem.at[i],
            device_id=to, device_id_type=MESH,
        )

    def copy(key, src, dst, **to):
        return copy_at(index(key), src, dst, **to)

    def start(cp):
        cp.start()
        started.append(cp)
        return cp

    barrier = pltpu.get_barrier_semaphore()
    peers = (
        dict(y=yr), dict(y=yl), dict(y=yo), dict(zl=1 - zl), dict(zh=1 - zh),
        dict(x=xr), dict(x=xl), dict(x=xo), dict(c=1 - c),
    )
    for peer in peers:
        pl.semaphore_signal(barrier, inc=1, device_id=peer, device_id_type=MESH)

    @pl.when(jnp.logical_not(fixed))
    def _():
        pl.semaphore_signal(barrier, inc=1, device_id=swap, device_id_type=MESH)
        pl.semaphore_wait(barrier, len(peers) + 1)

    @pl.when(fixed)
    def _():
        pl.semaphore_wait(barrier, len(peers))

    def place(zh_, x_, c_):
        row = pl.multiple_of((2 * zh_ + x_ // 2) * CAP, 16)
        col = pl.multiple_of((2 * (x_ % 2) + c_) * SUB, 128)
        return rows.at[:, pl.ds(row, CAP), pl.ds(col, SUB)]

    def weights(sub):
        at = wgt.at[sub, pl.ds(pl.multiple_of(zl * own, 16), own), :]
        return copy(("w", sub), win.at[sub], at, zl=1 - zl)

    here = place(zh, x, c)
    start(weights(0))
    start(weights(1))

    slots = lax.broadcasted_iota(jnp.int32, (CAP, tokens.shape[0]), 0)
    select[...] = jnp.where(slots == meta[0:1, :], 1.0, 0.0).astype(BF16)

    def move():
        return copy("move", xin, place(swap_zh, swap_x, c), **swap)

    xin[0] = dot_f32(select[...], tokens[...], ((1,), (0,))).astype(BF16)
    xin[1] = dot_f32(select[...], cotangent[...], ((1,), (0,))).astype(BF16)

    @pl.when(fixed)
    def _():
        here[...] = xin[...]

    @pl.when(jnp.logical_not(fixed))
    def _():
        move().start()

    def put_weights(i, carry):
        for sub in range(4):
            at = pl.multiple_of(zl * own + i * 96, 16)
            wgt[sub, pl.ds(at, 96), :] = win[sub, pl.ds(pl.multiple_of(i * 96, 16), 96), :]
        return carry

    lax.fori_loop(0, own // 96, put_weights, 0)
    named = jnp.broadcast_to(meta[1:2, :].astype(F32).astype(BF16), (16, tokens.shape[0]))
    labels[:, :CAP] = dot_f32(named, select[...], ((1,), (1,)))

    @pl.when(jnp.logical_not(fixed))
    def _():
        move().wait_recv()

    to_zh = start(copy("zh", here, here, zh=1 - zh))
    from_l0 = start(copy("xr0", here, here, x=xr))
    from_r0 = start(copy("xl0", here, here, x=xl))
    cores = {}

    def other_core(n, at):
        cores[n] = start(copy(("core", n), at, at, c=1 - c))

    other_core(0, here)
    start(weights(2))
    start(weights(3))

    def block_of(which, t):
        return rows[which, pl.ds(pl.multiple_of(t * CAP, 16), CAP), :]

    def ps(j, slot, half):
        return (j * 3 + slot) * 2 + half

    def rs(kind, half, j):
        src, dst, to = {
            "far_r": lambda: (psend.at[ps(j, 0, half)], prelay.at[j, 0], yr),
            "far_l": lambda: (psend.at[ps(j, 0, half)], prelay.at[j, 1], yl),
            "near_r": lambda: (psend.at[ps(j, 1, half)], precv.at[j, 0, half], yr),
            "near_l": lambda: (psend.at[ps(j, 2, half)], precv.at[j, 1, half], yl),
        }[kind]()
        return copy(("rs", kind, half, j), src, dst, y=to)

    def logit(r):
        to = (yo, yr, yl)[r]
        return copy(("lg", r), lsend.at[r], lrecv.at[r], y=to)

    def pre_block(j, t):
        r = (t - y + 4) % 4
        slot = jnp.where(r == 2, 0, jnp.where(r == 1, 1, jnp.where(r == 3, 2, 3)))
        x_in = block_of(0, t)
        x_cot = block_of(1, t)
        g0 = dot_f32(x_in, wgt[2 * j, :, : 2 * PART], ((1,), (0,)))
        g1 = dot_f32(x_in, wgt[2 * j + 1, :, : 2 * PART], ((1,), (0,)))
        w_d = jnp.concatenate([wgt[2 * j, :, 2 * PART :], wgt[2 * j + 1, :, 2 * PART :]], axis=1)
        d = dot_f32(x_cot, w_d, ((1,), (0,)))

        @pl.when(r != 0)
        def _():
            at = ps(j, slot, 0)
            psend[at, :, : 2 * PART] = g0.astype(BF16)
            psend[at + 1, :, : 2 * PART] = g1.astype(BF16)
            psend[at, :, 2 * PART :] = d[:, :PART].astype(BF16)
            psend[at + 1, :, 2 * PART :] = d[:, PART:].astype(BF16)

        @pl.when(r == 0)
        def _():
            pown[j, 0, :, : 2 * PART] = g0
            pown[j, 1, :, : 2 * PART] = g1
            pown[j, 0, :, 2 * PART :] = d[:, :PART]
            pown[j, 1, :, 2 * PART :] = d[:, PART:]

        @pl.when(r == 2)
        def _():
            rs("far_r", 0, j).start()
            rs("far_l", 1, j).start()

        @pl.when(r == 1)
        def _():
            rs("near_r", 1, j).start()

        @pl.when(r == 3)
        def _():
            rs("near_l", 0, j).start()

    def logits_of(r, carry):
        t = (y + jnp.where(r == 0, 2, jnp.where(r == 1, 1, jnp.where(r == 2, 3, 0)))) % 4
        cols = router[:, pl.ds(pl.multiple_of(y * D, 128), D)]
        lsend[r, :, :CAP] = dot_f32(cols, block_of(0, t), ((1,), (1,)))
        for k in range(3):

            @pl.when(r == k)
            def _():
                logit(k).start()

        return carry

    from_l0.wait_recv()
    at = place(zh, xl, c)
    from_lo = start(copy("xro", at, at, x=xr))
    other_core(2, at)
    from_r0.wait_recv()
    other_core(3, place(zh, xr, c))
    weights(0).wait_recv()
    weights(1).wait_recv()
    for n in (0, 2, 3):
        cores[n].wait_recv()
    pre_block(0, 2 * zh + x // 2)
    to_zh.wait_recv()
    there = place(1 - zh, x, c)
    from_l1 = start(copy("xr1", there, there, x=xr))
    from_r1 = start(copy("xl1", there, there, x=xl))
    other_core(1, there)
    from_lo.wait_recv()
    other_core(6, place(zh, xo, c))
    cores[6].wait_recv()
    pre_block(0, 2 * zh + 1 - x // 2)
    from_r1.wait_recv()
    at = place(1 - zh, xr, c)
    from_ro = start(copy("xlo", at, at, x=xl))
    other_core(4, at)
    from_l1.wait_recv()
    other_core(5, place(1 - zh, xl, c))
    for n in (1, 4, 5):
        cores[n].wait_recv()
    pre_block(0, 2 * (1 - zh) + x // 2)
    from_ro.wait_recv()
    other_core(7, place(1 - zh, xo, c))
    cores[7].wait_recv()
    pre_block(0, 2 * (1 - zh) + 1 - x // 2)

    def add_relays(j):
        for side, slot, half in ((0, 1, 0), (1, 2, 1)):
            rs(("far_r", "far_l")[side], half, j).wait_recv()
            mine = ps(j, slot, half)

            def add(i, carry):
                at = pl.ds(pl.multiple_of(i * 144, 16), 144)
                total = psend[mine, at, :].astype(F32) + prelay[j, side, at, :].astype(F32)
                psend[mine, at, :] = total.astype(BF16)
                return carry

            lax.fori_loop(0, 3, add, 0)
            rs(("near_r", "near_l")[side], half, j).start()

    def gates():
        for r in range(3):
            logit(r).wait_recv()
        logits = (lsend[3] + lrecv[0]) + (lrecv[1] + lrecv[2])
        label = labels[:8] - 1.0
        experts = lax.broadcasted_iota(jnp.int32, (8, 512), 0).astype(F32)
        picked = jnp.sum(jnp.where(label == experts, logits, 0.0), axis=0, keepdims=True)
        margin = logits[:1] - picked
        row = jnp.where(label[:1] > -0.5, jax.nn.sigmoid(margin), 0.0)
        gate[...] = jnp.transpose(jnp.broadcast_to(row, (PART, 512)))
        sacc[...] = jnp.zeros_like(sacc)

    def gather(kind, half, j):
        sub = 2 * j + half
        t, to = {"own_r": (y, yr), "own_l": (y, yl), "fwd_r": (yl, yr), "fwd_l": (yr, yl)}[kind]
        at = mids.at[sub, pl.ds(pl.multiple_of(t * CAP, 16), CAP), :]
        return copy(("ag", kind, half, j), at, at, y=to)

    def pointwise(j):
        for half in range(2):
            for kind in ("near_r", "near_l"):
                rs(kind, half, j).wait_recv()
        for half in range(2):
            sub = 2 * j + half

            def one(i, carry):
                at = pl.ds(pl.multiple_of(i * 48, 16), 48)
                pre = pown[j, half, at, :] + (
                    precv[j, 0, half, at, :].astype(F32) + precv[j, 1, half, at, :].astype(F32)
                )
                g, up, raw = pre[:, :PART], pre[:, PART : 2 * PART], pre[:, 2 * PART :]
                sigma = jax.nn.sigmoid(g)
                active = g * sigma
                slope = sigma * (1.0 + g * (1.0 - sigma))
                product = active * up
                scale = gate[at, :]
                sacc[at, :] += product * raw
                upstream = scale * raw
                to = pl.ds(pl.multiple_of(y * CAP + i * 48, 16), 48)
                mids[sub, to, :PART] = (upstream * up * slope).astype(BF16)
                mids[sub, to, PART : 2 * PART] = (upstream * active).astype(BF16)
                mids[sub, to, 2 * PART :] = (scale * product).astype(BF16)
                return carry

            lax.fori_loop(0, CAP // 48, one, 0)
            for kind in ("own_r", "own_l"):
                start(gather(kind, half, j))

    def forward(j):
        gather("own_r", 0, j).wait_recv()
        start(gather("fwd_r", 0, j))
        gather("own_l", 1, j).wait_recv()
        start(gather("fwd_l", 1, j))

    def near(j):
        gather("own_r", 1, j).wait_recv()
        gather("own_l", 0, j).wait_recv()

    def far(j):
        gather("fwd_r", 0, j).wait_recv()
        gather("fwd_l", 1, j).wait_recv()

    def exchange(j, s):
        return copy(("gz", j, s), gsend.at[j, s], grecv.at[j, s], zl=1 - zl)

    def out_rows(first, count, sub, g):
        return pl.ds(first * 8 + 2 * sub + g, count, stride=8)

    def grads_tile(j, at):
        mid_gu = jnp.concatenate([mids[2 * j, :, : 2 * PART], mids[2 * j + 1, :, : 2 * PART]], axis=1)
        gu = dot_f32(rows[0, :, pl.ds(at, 256)], mid_gu, ((0,), (0,)))
        mid_d = jnp.concatenate([mids[2 * j, :, 2 * PART :], mids[2 * j + 1, :, 2 * PART :]], axis=1)
        return gu, dot_f32(rows[1, :, pl.ds(at, 256)], mid_d, ((0,), (0,)))

    def grads_theirs(j):
        def one(i, carry):
            gu, d = grads_tile(j, pl.multiple_of((1 - zl) * own + i * 256, 256))
            to = pl.ds(pl.multiple_of(i * 256, 256), 256)
            for s in range(2):
                gsend[j, s, to, : 2 * PART] = gu[:, 2 * PART * s : 2 * PART * (s + 1)].astype(BF16)
                gsend[j, s, to, 2 * PART :] = d[:, PART * s : PART * (s + 1)].astype(BF16)
            return carry

        lax.fori_loop(0, own // 256, one, 0)

    def grads_mine(j):
        def one(i, carry):
            gu, d = grads_tile(j, pl.multiple_of(zl * own + i * 256, 256))
            to = pl.ds(pl.multiple_of(i * 256, 256), 256)
            for s in range(2):
                sub = 2 * j + s
                for g in range(2):
                    dgu_out[out_rows(i * 256, 256, sub, g), :] = gu[:, PART * (2 * s + g) : PART * (2 * s + g + 1)]
                dd_out[to, sub * PART : (sub + 1) * PART] = d[:, PART * s : PART * (s + 1)]
            return carry

        lax.fori_loop(0, own // 256, one, 0)

    def add_grads(j, s):
        exchange(j, s).wait_recv()
        sub = 2 * j + s

        def one(i, carry):
            at = pl.ds(pl.multiple_of(i * 64, 16), 64)
            got = grecv[j, s, at, :].astype(F32)
            for g in range(2):
                to = out_rows(i * 64, 64, sub, g)
                dgu_out[to, :] = dgu_out[to, :] + got[:, PART * g : PART * (g + 1)]
            dd_out[at, sub * PART : (sub + 1) * PART] += got[:, 2 * PART :]
            return carry

        lax.fori_loop(0, own // 64, one, 0)

    def score(key):
        src, dst, to = {
            "c": (0, 0, dict(c=1 - c)), "zh": (1, 1, dict(zh=1 - zh)),
            "x0": (2, 2, dict(x=xr)), "x1": (2, 3, dict(x=xl)), "x2": (2, 4, dict(x=xo)),
        }[key]
        return copy(("sc", key), srow.at[src], srecv.at[dst], **to)

    def scores():
        total = jnp.sum(jnp.transpose(sacc[...]), axis=0, keepdims=True)
        srow[0] = jnp.broadcast_to(total, (8, 512))
        start(score("c"))

    def scores_zh():
        score("c").wait_recv()
        srow[1] = srow[0] + srecv[0]
        start(score("zh"))

    def scores_x():
        score("zh").wait_recv()
        srow[2] = srow[1] + srecv[1]
        for key in ("x0", "x1", "x2"):
            start(score(key))

    def scores_end():
        for key in ("x0", "x1", "x2"):
            score(key).wait_recv()
        score_out[...] = (srow[2] + srecv[2]) + (srecv[3] + srecv[4])

    pair_base = index("pair", 8)

    def pair(i):
        return copy_at(pair_base + i, psend.at[i], brecv.at[i], c=1 - c)

    def ring(kind, half):
        src, dst, to = {
            "far_r": lambda: (bown.at[xo, half], xrelay.at[0], xr),
            "far_l": lambda: (bown.at[xo, half], xrelay.at[1], xl),
            "near_r": lambda: (bown.at[xr, half], xrecv.at[0, half], xr),
            "near_l": lambda: (bown.at[xl, half], xrecv.at[1, half], xl),
        }[kind]()
        return copy(("bx", kind, half), src, dst, x=to)

    def last():
        return copy("bz", zsend, zrecv, zh=1 - zh)

    def home():
        return copy("home", fsend, fin, **swap)

    def add_tiles(outs, refs):
        def one(i, carry):
            at = pl.ds(pl.multiple_of(i * 144, 16), 144)
            total = refs[0][at, :].astype(F32)
            for ref in refs[1:]:
                total = total + ref[at, :].astype(F32)
            for out in outs:
                out[at, :] = total.astype(out.dtype)
            return carry

        lax.fori_loop(0, 3, one, 0)

    def back_block(t):
        k = t // 2

        def one(b, carry):
            x_ = 2 * (t % 2) + b
            col = pl.multiple_of(b * 2 * SUB, 128)
            acc = None
            for sub in range(4):
                m = mids[sub, pl.ds(pl.multiple_of(t * CAP, 16), CAP), : 2 * PART]
                w = wgt[sub, pl.ds(col, 2 * SUB), : 2 * PART]
                part = dot_f32(m, w, ((1,), (1,)))
                acc = part if acc is None else acc + part
            low, high = acc[:, :SUB], acc[:, SUB:]
            i = x_ * 2 + k
            bown[x_, k] = jnp.where(c == 0, low, high).astype(BF16)
            psend[i] = jnp.where(c == 0, high, low).astype(BF16)
            pair(i).start()
            return carry

        lax.fori_loop(0, 2, one, 0)

    def back_sum(t):
        k = t // 2

        def one(b, carry):
            x_ = 2 * (t % 2) + b
            i = x_ * 2 + k
            r = (x_ - x + 4) % 4
            pair(i).wait_recv()
            add_tiles([bown.at[x_, k]], [bown.at[x_, k], brecv.at[i]])
            for r_, k_, kind in ((2, 0, "far_r"), (2, 1, "far_l"), (1, 1, "near_r"), (3, 0, "near_l")):

                @pl.when(jnp.logical_and(r == r_, k == k_))
                def _():
                    ring(kind, k_).start()

            return carry

        lax.fori_loop(0, 2, one, 0)

    weights(2).wait_recv()
    weights(3).wait_recv()

    def pre_one(n, carry):
        pre_block(1, (y + 2 + jnp.where(n == 0, 0, jnp.where(n == 1, 3, jnp.where(n == 2, 1, 2)))) % 4)
        return carry

    lax.fori_loop(0, 4, pre_one, 0)
    add_relays(0)
    lax.fori_loop(0, 4, logits_of, 0)
    add_relays(1)
    gates()
    pointwise(0)
    forward(0)
    pointwise(1)
    scores()
    for j in range(2):
        for kind in ("far_r", "far_l", "near_r", "near_l"):
            for half in range(2):
                if ("rs", kind, half, j) in number:
                    rs(kind, half, j).wait_send()
    back_block(y)
    scores_zh()
    near(0)
    far(0)
    grads_theirs(0)
    start(exchange(0, 0))
    start(exchange(0, 1))
    forward(1)
    grads_mine(0)
    scores_x()
    back_sum(y)
    near(1)
    back_block(yr)
    back_block(yl)
    back_sum(yr)
    back_sum(yl)
    scores_end()
    far(1)
    back_block(yo)
    grads_theirs(1)
    start(exchange(1, 0))
    back_sum(yo)
    grads_mine(1)
    ring("far_r", 0).wait_recv()
    add_tiles([bown.at[xr, 0]], [bown.at[xr, 0], xrelay.at[0]])
    ring("near_r", 0).start()
    ring("far_l", 1).wait_recv()
    add_tiles([bown.at[xl, 1]], [bown.at[xl, 1], xrelay.at[1]])
    ring("near_l", 1).start()
    add_grads(0, 0)
    add_grads(0, 1)
    for half in range(2):
        for kind in ("near_r", "near_l"):
            ring(kind, half).wait_recv()
    add_tiles([zsend], [bown.at[x, 1 - zh], xrecv.at[0, 1 - zh], xrecv.at[1, 1 - zh]])
    start(last())
    start(exchange(1, 1))
    add_grads(1, 0)
    last().wait_recv()
    add_tiles([fsend], [bown.at[x, zh], xrecv.at[0, zh], xrecv.at[1, zh], zrecv])

    @pl.when(fixed)
    def _():
        fin[...] = fsend[...]

    @pl.when(jnp.logical_not(fixed))
    def _():
        home().start()
        home().wait_recv()

    def put_tokens(i, carry):
        at = pl.ds(pl.multiple_of(i * 256, 256), 256)
        gtok_out[at, :] = dot_f32(select[:, at], fin[...], ((0,), (0,))).astype(BF16)
        return carry

    lax.fori_loop(0, tokens.shape[0] // 256, put_tokens, 0)
    add_grads(1, 1)

    @pl.when(jnp.logical_not(fixed))
    def _():
        move().wait_send()
        home().wait_send()

    for r in range(3):
        logit(r).wait_send()
    for kind in ("far_r", "far_l", "near_r", "near_l"):
        for half in range(2):
            if ("bx", kind, half) in number:
                ring(kind, half).wait_send()
    for i in range(8):
        pair(i).wait_send()
    for cp in started:
        cp.wait_send()


def exchange_and_compute(tokens, cotangent, win, router, meta):
    own = win.shape[1]
    rows_all = 4 * CAP
    vm = pltpu.VMEM
    piece = (CAP, SUB)
    flops = 2 * rows_all * 2 * own * 4 * SUB * 8 // 3
    return pl.pallas_call(
        kernel,
        out_shape=(
            jax.ShapeDtypeStruct(tokens.shape, BF16),
            jax.ShapeDtypeStruct((8, 512), F32),
            jax.ShapeDtypeStruct((own * 8, PART), F32),
            jax.ShapeDtypeStruct((own, 512), F32),
        ),
        in_specs=[pl.BlockSpec(memory_space=vm)] * 5,
        out_specs=[pl.BlockSpec(memory_space=vm)] * 4,
        scratch_shapes=[
            vm((CAP, tokens.shape[0]), BF16),
            vm((2,) + piece, BF16),
            vm((2, rows_all, 2 * own), BF16),
            vm((4, 2 * own, SUB), BF16),
            vm((12,) + piece, BF16),
            vm((2, 2) + piece, F32),
            vm((2, 2) + piece, BF16),
            vm((2, 2, 2) + piece, BF16),
            vm((4, 8, 512), F32),
            vm((3, 8, 512), F32),
            vm((512, PART), F32),
            vm((512, PART), F32),
            vm((4, rows_all, SUB), BF16),
            vm((2, 2, own, SUB), BF16),
            vm((2, 2, own, SUB), BF16),
            vm((4, 2) + piece, BF16),
            vm((8,) + piece, BF16),
            vm((2,) + piece, BF16),
            vm((2, 2) + piece, BF16),
            vm(piece, BF16),
            vm(piece, BF16),
            vm(piece, BF16),
            vm(piece, BF16),
            vm((3, 8, 512), F32),
            vm((5, 8, 512), F32),
            vm((16, 512), F32),
            pltpu.SemaphoreType.DMA((96,)),
            pltpu.SemaphoreType.DMA((96,)),
        ],
        cost_estimate=pl.CostEstimate(flops=flops, bytes_accessed=20 << 20, transcendentals=CAP * 512),
        compiler_params=pltpu.CompilerParams(
            collective_id=0, has_side_effects=True, vmem_limit_bytes=67043328
        ),
    )(tokens, cotangent, win, router, meta)


def local(tokens, cotangent, expert_choice, router, gate_up, w_down):
    own, hid = w_down.shape
    first = expert_choice[:, 0]
    second = expert_choice[:, 1]
    in_first = first == 0
    in_second = second == 0
    routed = jnp.logical_or(in_first, in_second)
    flags = routed.astype(jnp.int32)
    slot_rank = jnp.where(routed, jnp.cumsum(flags) - flags, -1)
    meta = jnp.stack([slot_rank, first + second + 1] + [flags] * 6)

    win = jnp.stack(
        [
            jnp.concatenate(
                [
                    gate_up[:, 0, PART * s : PART * (s + 1)],
                    gate_up[:, 1, PART * s : PART * (s + 1)],
                    w_down[:, PART * s : PART * (s + 1)],
                ],
                axis=1,
            )
            for s in range(hid // PART)
        ]
    )
    grad_tokens, score, d_gu, d_down = exchange_and_compute(tokens, cotangent, win, router, meta)

    slot_ids = jnp.arange(CAP, dtype=jnp.int32)
    placed = slot_rank[None, :] == slot_ids[:, None]
    token_score = jnp.sum(jnp.where(placed, score[0, :CAP, None], 0.0), axis=0)
    d_combine = jnp.stack(
        [jnp.where(in_first, token_score, 0.0), jnp.where(in_second, token_score, 0.0)], axis=1
    )
    d_gate_up = d_gu.reshape(own, hid // PART, 2, PART).transpose(0, 2, 1, 3).reshape(own, 2, hid)
    return (grad_tokens, d_combine, d_gate_up, d_down)


def solution(mesh):
    split = Mesh(mesh.devices.reshape(4, 2, 2, 4, 2), ALL)
    return jax.shard_map(
        local,
        mesh=split,
        in_specs=(
            P(TOK, HID),
            P(TOK, HID),
            P(TOK, None),
            P(),
            P(TOK, None, HID),
            P(TOK, HID),
        ),
        out_specs=(P(TOK, HID), P(TOK, None), P(TOK, None, HID), P(TOK, HID)),
        check_vma=False,
    )
```

time: 257 us -> 259 us (level)
  the two profiles are of different devices: /device:TPU:24 before, /device:TPU:31 now
where the time goes in v3:
time: 259 us
  Pallas kernels  236 us (91%)
  local copies, waits for them, and re-layouts  14.1 us (5%)
  other arithmetic  7.39 us (3%)
    pallas_call x1, Pallas kernels, exchange_and_compute(): pl.pallas_call(kernel, out_shape=(jax.ShapeDtypeStruct(tokens.shape, BF16...  236 us
    unnamed x15, local copies, waits for them, and re-layouts  8.53 us

profile of v3, /device:TPU:31, one launch (start us, length us, event | category | flops | bytes accessed | tf_op | source)
XLA Modules:
  0.0 258.7 jit_solution(7418545540167065055)
XLA Ops:
  0.6 0.0 copy-start
  0.6 0.9 add_bitcast_fusion.1
  1.5 0.8 fusion.1
  2.4 0.3 reduce-window.9
  2.6 0.1 slice.69
  2.8 0.1 slice_reduce_fusion
  2.9 0.7 fusion
  3.6 0.1 add_bitcast_fusion
  3.6 0.7 stack.36.meta
  4.3 1.3 fusion.3
  5.6 0.0 copy-done
  5.6 2.7 %fusion.2 = (bf16[768,1,128]{2,1,0:T(2,128)(2,1)S(1)}, bf16[768,1,128]{2,1,0:T(2,128)(2,1)S(1)}, bf16[768,1,128]{2,1,0:T(2,128)(2,1)S(1)}, bf16[768,1,128]{2,1,0...) fusion(bf16[768,2,512]{2,1,0:T(2,128)(2,1)S(1)} %copy-done), kind=kLoop, calls=%fused_computation.29 | loop fusion | bytes 3145728 | tf_op jit(solution)/shard_map/slice | solution.py:630
  8.6 0.2 maximum_bitcast_fusion
  8.8 0.2 maximum_bitcast_fusion.2
  8.9 1.8 pad_maximum_fusion.win
  10.7 236.4 %shard_map.93 = (bf16[1536,384]{1,0:T(8,128)(2,1)}, f32[8,512]{1,0:T(8,128)}, f32[6144,128]{1,0:T(8,128)}, f32[768,512]{1,0:T(8,128)}) custom-call(bf16[1536,384]{1,0:T(8,128)(2,1)} %tokens.1, bf16[1536,384]{1,0:T(8,128)(2,1)} %cotangent.1, bf16[4,768,384]{2,1,0:T(8,128)(2,1)} %pad_maximum_fusion.win, bf16[8,6144]{1,0:T(8,128)(2,1)} %router.1, ...), custom_call_target="tpu_custom_call" | custom-call | flops 21743271936 | bytes 20971520 | tf_op jit(solution)/shard_map/pallas_call | solution.py:568
  247.2 0.7 slice.68
  247.9 1.1 select_reduce_fusion
  249.0 0.8 compare_select_fusion.1
  249.8 0.6 pad_maximum_fusion.1
  250.4 2.4 copy.66
  252.8 0.0 copy-start.1
  252.8 4.7 %copy.67 = f32[768,2,512]{2,1,0:T(2,128)} copy(f32[768,2,512]{2,1,0:T(2,128)} %bitcast.57) | data formatting | bytes 6291456
  257.5 0.0 copy-done.1
  257.6 1.1 copy.68
  (12 shorter events, 0.3 us)
Async XLA Ops:
  0.6 5.0 %copy-start = (bf16[768,2,512]{2,1,0:T(2,128)(2,1)S(1)}, bf16[768,2,512]{2,1,0:T(2,128)(2,1)}, u32[]{:S(2)}) copy-start(bf16[768,2,512]{2,1,0:T(2,128)(2,1)} %param.10) | copy-start | bytes 4718596
  252.8 4.8 %copy-start.1 = (f32[768,512]{1,0:T(8,128)S(1)}, f32[768,512]{1,0:T(8,128)}, u32[]{:S(2)}) copy-start(f32[768,512]{1,0:T(8,128)} %get-tuple-element.39) | copy-start | bytes 4718596

commit v4 on v1

v4 whole, which is shorter than its diff:
```python
import jax
import jax.numpy as jnp
from jax import lax
from jax.experimental import pallas as pl
from jax.experimental.pallas import tpu as pltpu
from jax.sharding import Mesh
from jax.sharding import PartitionSpec as P

CAP = 432
SUB = 384
PART = 128
TOK = ("y", "zl")
HID = ("zh", "x", "c")
ALL = TOK + HID
MESH = pl.DeviceIdType.MESH
F32 = jnp.float32
BF16 = jnp.bfloat16


def dot_f32(left, right, dims):
    return lax.dot_general(left, right, ((dims[0], dims[1]), ((), ())), preferred_element_type=F32)


P0, PN = (0, 224), (224, 208)
Q0, QN = (0, 112, 224, 336), (112, 112, 112, 96)
RS_KINDS = ("far_r", "far_l", "nr_raw", "nl_raw", "nr_rel", "nl_rel")
AG_KINDS = ("own_r0", "own_l1", "own_r1", "own_l0", "fwd_r", "fwd_l")


def kernel(
    tokens, cotangent, gate_w, up_w, down_w, router, meta,
    fin, score_out, dgu_out, dd_out,
    select, xin, rows, wgt, psend, pown, prelay, precv, lsend, lrecv, gate, sacc, mids,
    gsend, grecv, bown, brecv, xrelay, xrecv, zsend, zrecv, fsend, stage, zstage, srow, srecv, labels,
    ssem, rsem,
):
    y, zl, zh, x, c = (lax.axis_index(a) for a in ALL)
    yr, yl, yo = (y + 1) % 4, (y + 3) % 4, (y + 2) % 4
    xr, xl, xo = (x + 1) % 4, (x + 3) % 4, (x + 2) % 4
    D = rows.shape[2]
    own = D // 2
    swap_y, swap_zh, swap_x = 2 * zh + x // 2, y // 2, 2 * (y % 2) + x % 2
    fixed = swap_y == y
    moves = jnp.logical_not(fixed)
    swap = dict(y=swap_y, zh=swap_zh, x=swap_x)

    number = {}
    started = []

    def index(key, n=1):
        if key not in number:
            number[key] = number.get("next", 0)
            number["next"] = number[key] + n
        return number[key]

    def copy_at(i, src, dst, **to):
        return pltpu.make_async_remote_copy(
            src_ref=src, dst_ref=dst, send_sem=ssem.at[i], recv_sem=rsem.at[i],
            device_id=to, device_id_type=MESH,
        )

    def copy(key, src, dst, **to):
        return copy_at(index(key), src, dst, **to)

    def start(cp):
        cp.start()
        started.append(cp)
        return cp

    barrier = pltpu.get_barrier_semaphore()
    peers = (
        dict(y=yr), dict(y=yl), dict(y=yo), dict(zl=1 - zl), dict(zh=1 - zh),
        dict(x=xr), dict(x=xl), dict(x=xo), dict(c=1 - c), dict(zl=1 - zl, zh=1 - zh),
    )
    for peer in peers:
        pl.semaphore_signal(barrier, inc=1, device_id=peer, device_id_type=MESH)

    @pl.when(moves)
    def _():
        pl.semaphore_signal(barrier, inc=1, device_id=swap, device_id_type=MESH)

    def place(p, zh_, x_, c_):
        row = pl.multiple_of((2 * zh_ + x_ // 2) * CAP + P0[p], 16)
        col = pl.multiple_of((2 * (x_ % 2) + c_) * SUB, 128)
        return rows.at[:, pl.ds(row, PN[p]), pl.ds(col, SUB)]

    def weights(sub):
        at = wgt.at[sub, pl.ds(pl.multiple_of(zl * own, 16), own), :]
        return copy(("w", sub), at, at, zl=1 - zl)

    def part(p):
        return pl.ds(P0[p], PN[p])

    def quarter(q):
        return pl.ds(Q0[q], QN[q])

    def move(p):
        return copy(("move", p), xin.at[:, part(p), :], place(p, swap_zh, swap_x, c), **swap)

    for p in range(2):
        slots = lax.broadcasted_iota(jnp.int32, (PN[p], tokens.shape[0]), 0) + P0[p]
        select[part(p), :] = jnp.where(slots == meta[0:1, :], 1.0, 0.0).astype(BF16)
        xin[0, part(p), :] = dot_f32(select[part(p), :], tokens[...], ((1,), (0,))).astype(BF16)
        xin[1, part(p), :] = dot_f32(select[part(p), :], cotangent[...], ((1,), (0,))).astype(BF16)

    def put_weights(i, carry):
        at = pl.ds(pl.multiple_of(zl * own + i * 96, 16), 96)
        of = pl.ds(pl.multiple_of(i * 96, 16), 96)
        for sub in range(4):
            for n, ref in enumerate((gate_w, up_w, down_w)):
                wgt[sub, at, PART * n : PART * (n + 1)] = ref[of, PART * sub : PART * (sub + 1)]
        return carry

    lax.fori_loop(0, own // 96, put_weights, 0)

    @pl.when(moves)
    def _():
        pl.semaphore_wait(barrier, len(peers) + 1)

    @pl.when(fixed)
    def _():
        pl.semaphore_wait(barrier, len(peers))

    for p in range(2):

        @pl.when(fixed)
        def _():
            place(p, zh, x, c)[...] = xin[:, part(p), :]

        @pl.when(moves)
        def _():
            move(p).start()

    start(weights(0))
    named = jnp.broadcast_to(meta[1:2, :].astype(F32).astype(BF16), (16, tokens.shape[0]))
    labels[:, :CAP] = dot_f32(named, select[...], ((1,), (1,)))

    steps = {
        "za": (lambda p: (place(p, zh, x, c), stage.at[:, part(p), :]), dict(zl=1 - zl)),
        "zb": (lambda p: (stage.at[:, part(p), :], place(p, zh, x, c)), dict(zl=1 - zl, zh=1 - zh)),
        "xr0": (lambda p: place(p, zh, x, c), dict(x=xr)),
        "xl0": (lambda p: place(p, zh, x, c), dict(x=xl)),
        "xro": (lambda p: place(p, zh, xl, c), dict(x=xr)),
        "xr1": (lambda p: place(p, 1 - zh, x, c), dict(x=xr)),
        "xl1": (lambda p: place(p, 1 - zh, x, c), dict(x=xl)),
        "xlo": (lambda p: place(p, 1 - zh, xr, c), dict(x=xl)),
        "c_own": (lambda p: place(p, zh, x, c), dict(c=1 - c)),
        "c_zh": (lambda p: place(p, 1 - zh, x, c), dict(c=1 - c)),
        "c_xr0": (lambda p: place(p, zh, xl, c), dict(c=1 - c)),
        "c_xl0": (lambda p: place(p, zh, xr, c), dict(c=1 - c)),
        "c_xr1": (lambda p: place(p, 1 - zh, xl, c), dict(c=1 - c)),
        "c_xl1": (lambda p: place(p, 1 - zh, xr, c), dict(c=1 - c)),
        "c_xro": (lambda p: place(p, zh, xo, c), dict(c=1 - c)),
        "c_xlo": (lambda p: place(p, 1 - zh, xo, c), dict(c=1 - c)),
    }

    def hop(name, p):
        at, to = steps[name]
        ends = at(p)
        src, dst = ends if isinstance(ends, tuple) else (ends, ends)
        return copy((name, p), src, dst, **to)

    def arrive(name, p, *then):
        hop(name, p).wait_recv()
        for follow in then:
            start(hop(follow, p))

    def all_cores(p):
        for name in steps:
            if name.startswith("c_"):
                hop(name, p).wait_recv()

    for p in range(2):

        @pl.when(moves)
        def _():
            move(p).wait_recv()

        for name in ("za", "xr0", "xl0", "c_own"):
            start(hop(name, p))
        start(weights(p + 1))
    start(weights(3))

    rs_base = index("rs", 48)
    ag_base = index("ag", 48)

    def rs(kind, p, s):
        q = 2 * p + (kind in ("far_l", "nr_raw", "nl_rel"))
        at = quarter(q)
        src, dst, to = {
            "fa": lambda: (psend.at[0, s, at, :], prelay.at[s, at, :], yr if kind == "far_r" else yl),
            "nr": lambda: (psend.at[1, s, at, :], precv.at[0, s, at, :], yr),
            "nl": lambda: (psend.at[2, s, at, :], precv.at[1, s, at, :], yl),
        }[kind[:2]]()
        return copy_at(rs_base + (p * 4 + s) * 6 + RS_KINDS.index(kind), src, dst, y=to)

    def logit(r):
        to = (yo, yr, yl)[r]
        return copy(("lg", r), lsend.at[r], lrecv.at[r], y=to)

    def pre(p, j):
        s0, s1 = 2 * j, 2 * j + 1

        def one(n, carry):
            r = jnp.where(n == 0, 2, jnp.where(n == 1, 1, jnp.where(n == 2, 3, 0)))
            t = (y + r) % 4
            at = pl.ds(pl.multiple_of(t * CAP + P0[p], 16), PN[p])
            x_in = rows[0, at, :]
            g0 = dot_f32(x_in, wgt[s0, :, : 2 * PART], ((1,), (0,)))
            g1 = dot_f32(x_in, wgt[s1, :, : 2 * PART], ((1,), (0,)))
            w_d = jnp.concatenate([wgt[s0, :, 2 * PART :], wgt[s1, :, 2 * PART :]], axis=1)
            d = dot_f32(rows[1, at, :], w_d, ((1,), (0,)))

            @pl.when(n < 3)
            def _():
                psend[n, s0, part(p), : 2 * PART] = g0.astype(BF16)
                psend[n, s1, part(p), : 2 * PART] = g1.astype(BF16)
                psend[n, s0, part(p), 2 * PART :] = d[:, :PART].astype(BF16)
                psend[n, s1, part(p), 2 * PART :] = d[:, PART:].astype(BF16)

            @pl.when(n == 3)
            def _():
                pown[s0, part(p), : 2 * PART] = g0
                pown[s1, part(p), : 2 * PART] = g1
                pown[s0, part(p), 2 * PART :] = d[:, :PART]
                pown[s1, part(p), 2 * PART :] = d[:, PART:]

            for m, kinds in ((0, ("far_r", "far_l")), (1, ("nr_raw",)), (2, ("nl_raw",))):

                @pl.when(n == m)
                def _():
                    for s in (s0, s1):
                        for kind in kinds:
                            rs(kind, p, s).start()

            return carry

        lax.fori_loop(0, 4, one, 0)

    def logits():
        cols = router[:, pl.ds(pl.multiple_of(y * D, 128), D)]

        def one(n, carry):
            t = (y + jnp.where(n == 0, 2, jnp.where(n == 1, 1, jnp.where(n == 2, 3, 0)))) % 4
            at = pl.ds(pl.multiple_of(t * CAP, 16), CAP)
            lsend[n, :, :CAP] = dot_f32(cols, rows[0, at, :], ((1,), (1,)))
            return carry

        lax.fori_loop(0, 4, one, 0)
        for r in range(3):
            start(logit(r))

    def relay(p, s):
        for side, slot, rel in (("far_r", 1, "nr_rel"), ("far_l", 2, "nl_rel")):
            at = quarter(2 * p + (side == "far_l"))
            rs(side, p, s).wait_recv()
            total = psend[slot, s, at, :].astype(F32) + prelay[s, at, :].astype(F32)
            psend[slot, s, at, :] = total.astype(BF16)
            rs(rel, p, s).start()

    def gates():
        for r in range(3):
            logit(r).wait_recv()
        total = (lsend[3] + lrecv[0]) + (lrecv[1] + lrecv[2])
        label = labels[:8] - 1.0
        experts = lax.broadcasted_iota(jnp.int32, (8, 512), 0).astype(F32)
        picked = jnp.sum(jnp.where(label == experts, total, 0.0), axis=0, keepdims=True)
        margin = total[:1] - picked
        row = jnp.where(label[:1] > -0.5, jax.nn.sigmoid(margin), 0.0)
        gate[...] = jnp.transpose(jnp.broadcast_to(row, (PART, 512)))
        sacc[...] = jnp.zeros_like(sacc)

    def ag(kind, p, s):
        q = 2 * p + (kind in ("own_r1", "own_l1", "fwd_l"))
        t = {"own": y, "fwd": yl if kind == "fwd_r" else yr}[kind[:3]]
        to = yr if kind[4] == "r" else yl
        at = mids.at[s, pl.ds(pl.multiple_of(t * CAP + Q0[q], 16), QN[q]), :]
        return copy_at(ag_base + (p * 4 + s) * 6 + AG_KINDS.index(kind), at, at, y=to)

    def pointwise(p, s):
        for kind in RS_KINDS[2:]:
            rs(kind, p, s).wait_recv()
        for q in (2 * p, 2 * p + 1):
            at = quarter(q)
            near = precv[0, s, at, :].astype(F32) + precv[1, s, at, :].astype(F32)
            now = pown[s, at, :] + near
            g, up, raw = now[:, :PART], now[:, PART : 2 * PART], now[:, 2 * PART :]
            sigma = jax.nn.sigmoid(g)
            active = g * sigma
            slope = sigma * (1.0 + g * (1.0 - sigma))
            product = active * up
            scale = gate[at, :]
            sacc[at, :] += product * raw
            upstream = scale * raw
            to = pl.ds(pl.multiple_of(y * CAP + Q0[q], 16), QN[q])
            mids[s, to, :PART] = (upstream * up * slope).astype(BF16)
            mids[s, to, PART : 2 * PART] = (upstream * active).astype(BF16)
            mids[s, to, 2 * PART :] = (scale * product).astype(BF16)
        for kind in AG_KINDS[:4]:
            ag(kind, p, s).start()

    def forward(p, s):
        for kind, fwd in (("own_r0", "fwd_r"), ("own_l1", "fwd_l")):
            ag(kind, p, s).wait_recv()
            ag(fwd, p, s).start()

    def near(p, s):
        ag("own_r1", p, s).wait_recv()
        ag("own_l0", p, s).wait_recv()

    def far(p, s):
        ag("fwd_r", p, s).wait_recv()
        ag("fwd_l", p, s).wait_recv()

    def exchange(s, half=None):
        at = pl.ds(0, own) if half is None else pl.ds(half * (own // 2), own // 2)
        return copy(("gz", s, half), gsend.at[s, at, :], grecv.at[s, at, :], zl=1 - zl)

    def out_rows(first, count, sub, g):
        return pl.ds(first * 8 + 2 * sub + g, count, stride=8)

    def grads_tile(s, at):
        gu = dot_f32(rows[0, :, pl.ds(at, 256)], mids[s, :, : 2 * PART], ((0,), (0,)))
        return gu, dot_f32(rows[1, :, pl.ds(at, 256)], mids[s, :, 2 * PART :], ((0,), (0,)))

    def grads_theirs(s):
        def one(i, carry):
            gu, d = grads_tile(s, pl.multiple_of((1 - zl) * own + i * 256, 256))
            to = pl.ds(pl.multiple_of(i * 256, 256), 256)
            gsend[s, to, : 2 * PART] = gu.astype(BF16)
            gsend[s, to, 2 * PART :] = d.astype(BF16)
            return carry

        lax.fori_loop(0, own // 256, one, 0)

    def grads_mine(s):
        def one(i, carry):
            gu, d = grads_tile(s, pl.multiple_of(zl * own + i * 256, 256))
            for g in range(2):
                dgu_out[out_rows(i * 256, 256, s, g), :] = gu[:, PART * g : PART * (g + 1)]
            to = pl.ds(pl.multiple_of(i * 256, 256), 256)
            dd_out[to, s * PART : (s + 1) * PART] = d
            return carry

        lax.fori_loop(0, own // 256, one, 0)

    def add_grads(s, half=None):
        exchange(s, half).wait_recv()

        def one(i, carry):
            at = pl.ds(pl.multiple_of(i * 64, 16), 64)
            got = grecv[s, at, :].astype(F32)
            for g in range(2):
                to = out_rows(i * 64, 64, s, g)
                dgu_out[to, :] = dgu_out[to, :] + got[:, PART * g : PART * (g + 1)]
            dd_out[at, s * PART : (s + 1) * PART] += got[:, 2 * PART :]
            return carry

        count = own // 64
        if half is None:
            lax.fori_loop(0, count, one, 0)
        else:
            lax.fori_loop(half * (count // 2), (half + 1) * (count // 2), one, 0)

    def score(key):
        src, dst, to = {
            "c": (0, 0, dict(c=1 - c)), "zh": (1, 1, dict(zh=1 - zh)),
            "x0": (2, 2, dict(x=xr)), "x1": (2, 3, dict(x=xl)), "x2": (2, 4, dict(x=xo)),
        }[key]
        return copy(("sc", key), srow.at[src], srecv.at[dst], **to)

    def scores():
        total = jnp.sum(jnp.transpose(sacc[...]), axis=0, keepdims=True)
        srow[0] = jnp.broadcast_to(total, (8, 512))
        start(score("c"))

    def scores_zh():
        score("c").wait_recv()
        srow[1] = srow[0] + srecv[0]
        start(score("zh"))

    def scores_x():
        score("zh").wait_recv()
        srow[2] = srow[1] + srecv[1]
        for key in ("x0", "x1", "x2"):
            start(score(key))

    def scores_end():
        for key in ("x0", "x1", "x2"):
            score(key).wait_recv()
        score_out[...] = (srow[2] + srecv[2]) + (srecv[3] + srecv[4])

    pair_base = index("pair", 16)

    def pair(p, i):
        src = psend.at[i // 4, i % 4, part(p), :]
        return copy_at(pair_base + p * 8 + i, src, brecv.at[i, part(p), :], c=1 - c)

    def ring(kind, half, p):
        at = part(p)
        src, dst, to = {
            "far_r": lambda: (bown.at[xo, half, at, :], xrelay.at[0, at, :], xr),
            "far_l": lambda: (bown.at[xo, half, at, :], xrelay.at[1, at, :], xl),
            "near_r": lambda: (bown.at[xr, half, at, :], xrecv.at[0, half, at, :], xr),
            "near_l": lambda: (bown.at[xl, half, at, :], xrecv.at[1, half, at, :], xl),
        }[kind]()
        return copy(("bx", kind, half, p), src, dst, x=to)

    def last_a(p):
        return copy(("bza", p), zsend.at[part(p), :], zstage.at[part(p), :], zl=1 - zl)

    def last_b(p):
        return copy(("bzb", p), zstage.at[part(p), :], zrecv.at[part(p), :], zl=1 - zl, zh=1 - zh)

    def last_relay(p):
        last_a(p).wait_recv()
        start(last_b(p))

    def home(p):
        return copy(("home", p), fsend.at[part(p), :], fin.at[part(p), :], **swap)

    def add_rows(p, out, refs):
        for q in (2 * p, 2 * p + 1):
            at = quarter(q)
            total = refs[0][at, :].astype(F32)
            for ref in refs[1:]:
                total = total + ref[at, :].astype(F32)
            out[at, :] = total.astype(out.dtype)

    def back_block(p, t):
        k = t // 2

        def one(b, carry):
            x_ = 2 * (t % 2) + b
            col = pl.multiple_of(b * 2 * SUB, 128)
            acc = None
            for sub in range(4):
                m = mids[sub, pl.ds(pl.multiple_of(t * CAP + P0[p], 16), PN[p]), : 2 * PART]
                w = wgt[sub, pl.ds(col, 2 * SUB), : 2 * PART]
                piece = dot_f32(m, w, ((1,), (1,)))
                acc = piece if acc is None else acc + piece
            low, high = acc[:, :SUB], acc[:, SUB:]
            i = x_ * 2 + k
            bown[x_, k, part(p), :] = jnp.where(c == 0, low, high).astype(BF16)
            psend[i // 4, i % 4, part(p), :] = jnp.where(c == 0, high, low).astype(BF16)
            pair(p, i).start()
            return carry

        lax.fori_loop(0, 2, one, 0)

    def back_sum(p, t):
        k = t // 2

        def one(b, carry):
            x_ = 2 * (t % 2) + b
            i = x_ * 2 + k
            r = (x_ - x + 4) % 4
            pair(p, i).wait_recv()
            add_rows(p, bown.at[x_, k], [bown.at[x_, k], brecv.at[i]])
            for r_, k_, kind in ((2, 0, "far_r"), (2, 1, "far_l"), (1, 1, "near_r"), (3, 0, "near_l")):

                @pl.when(jnp.logical_and(r == r_, k == k_))
                def _():
                    ring(kind, k_, p).start()

            return carry

        lax.fori_loop(0, 2, one, 0)

    def ring_relay(p):
        ring("far_r", 0, p).wait_recv()
        add_rows(p, bown.at[xr, 0], [bown.at[xr, 0], xrelay.at[0]])
        ring("near_r", 0, p).start()
        ring("far_l", 1, p).wait_recv()
        add_rows(p, bown.at[xl, 1], [bown.at[xl, 1], xrelay.at[1]])
        ring("near_l", 1, p).start()

    def ring_end(p):
        for half in range(2):
            for kind in ("near_r", "near_l"):
                ring(kind, half, p).wait_recv()
        add_rows(p, zsend, [bown.at[x, 1 - zh], xrecv.at[0, 1 - zh], xrecv.at[1, 1 - zh]])
        start(last_a(p))

    def go_home(p):
        last_b(p).wait_recv()
        add_rows(p, fsend, [bown.at[x, zh], xrecv.at[0, zh], xrecv.at[1, zh], zrecv])

        @pl.when(fixed)
        def _():
            fin[part(p), :] = fsend[part(p), :]

        @pl.when(moves)
        def _():
            home(p).start()

    arrive("xr0", 0, "xro", "c_xr0")
    arrive("xl0", 0, "c_xl0")
    arrive("za", 0, "zb")
    arrive("zb", 0, "xr1", "xl1", "c_zh")
    arrive("xr0", 1, "xro", "c_xr0")
    arrive("xl0", 1, "c_xl0")
    arrive("za", 1, "zb")
    arrive("xl1", 0, "xlo", "c_xl1")
    arrive("zb", 1, "xr1", "xl1", "c_zh")
    arrive("xro", 0, "c_xro")
    arrive("xr1", 0, "c_xr1")
    arrive("xl1", 1, "xlo", "c_xl1")
    arrive("xlo", 0, "c_xlo")
    weights(0).wait_recv()
    weights(1).wait_recv()
    all_cores(0)
    pre(0, 0)
    arrive("xro", 1, "c_xro")
    arrive("xr1", 1, "c_xr1")
    arrive("xlo", 1, "c_xlo")
    all_cores(1)
    pre(1, 0)
    relay(0, 0)
    relay(0, 1)
    logits()
    weights(2).wait_recv()
    weights(3).wait_recv()
    pre(0, 1)
    relay(1, 0)
    relay(1, 1)
    pre(1, 1)
    gates()
    pointwise(0, 0)
    pointwise(1, 0)
    relay(0, 2)
    relay(0, 3)
    pointwise(0, 1)
    pointwise(1, 1)
    relay(1, 2)
    relay(1, 3)
    forward(0, 0)
    forward(1, 0)
    pointwise(0, 2)
    pointwise(0, 3)
    forward(0, 1)
    forward(1, 1)
    pointwise(1, 2)
    pointwise(1, 3)
    scores()
    near(0, 0)
    near(1, 0)
    far(0, 0)
    far(1, 0)
    scores_zh()
    grads_theirs(0)
    start(exchange(0))
    forward(0, 2)
    forward(0, 3)
    for kind in RS_KINDS:
        for p in range(2):
            for s in range(4):
                rs(kind, p, s).wait_send()
    back_block(0, y)
    near(0, 1)
    near(1, 1)
    far(0, 1)
    far(1, 1)
    grads_theirs(1)
    start(exchange(1))
    near(0, 2)
    near(0, 3)
    back_block(0, yr)
    forward(1, 2)
    forward(1, 3)
    back_block(0, yl)
    far(0, 2)
    far(0, 3)
    back_block(0, yo)
    back_block(1, y)
    back_sum(0, y)
    back_sum(0, yr)
    back_sum(0, yl)
    back_sum(0, yo)
    near(1, 2)
    near(1, 3)
    back_block(1, yr)
    back_block(1, yl)
    far(1, 2)
    far(1, 3)
    back_block(1, yo)
    ring_relay(0)
    back_sum(1, y)
    back_sum(1, yr)
    back_sum(1, yl)
    back_sum(1, yo)
    grads_theirs(2)
    start(exchange(2))
    ring_end(0)
    grads_theirs(3)
    start(exchange(3, 0))
    ring_relay(1)
    last_relay(0)
    grads_mine(0)
    ring_end(1)
    start(exchange(3, 1))
    scores_x()
    go_home(0)
    last_relay(1)
    grads_mine(1)
    add_grads(0)
    add_grads(1)
    go_home(1)
    grads_mine(2)
    grads_mine(3)
    scores_end()
    add_grads(2)

    @pl.when(moves)
    def _():
        home(0).wait_recv()
        home(1).wait_recv()

    add_grads(3, 0)
    add_grads(3, 1)

    @pl.when(moves)
    def _():
        for p in range(2):
            move(p).wait_send()
            home(p).wait_send()

    for kind in AG_KINDS:
        for p in range(2):
            for s in range(4):
                ag(kind, p, s).wait_send()
    for key in number:
        if key[0] == "bx":
            ring(*key[1:]).wait_send()
    for p in range(2):
        for i in range(8):
            pair(p, i).wait_send()
    for cp in started:
        cp.wait_send()


def finish(meta, fin, score, d_gu, d_down):
    total = meta.shape[1]
    steps = 6
    tile = total // steps
    vm = pltpu.VMEM

    def body(meta_ref, fin_ref, score_ref, gu_ref, down_ref, gtok_ref, comb_ref, gu_out, down_out):
        gu_out[...] = gu_ref[...]
        down_out[...] = down_ref[...]
        slots = lax.broadcasted_iota(jnp.int32, (CAP, tile), 0)
        select = jnp.where(slots == meta_ref[0:1, :], 1.0, 0.0).astype(BF16)
        gtok_ref[...] = dot_f32(select, fin_ref[...], ((0,), (0,))).astype(BF16)
        exact = score_ref[0:1, :CAP]
        high = exact.astype(BF16)
        rest = exact - high.astype(F32)
        middle = rest.astype(BF16)
        low = (rest - middle.astype(F32)).astype(BF16)
        at = lax.broadcasted_iota(jnp.int32, (16, CAP), 0)
        split = jnp.where(at == 0, high.astype(F32), jnp.where(at == 1, middle.astype(F32), low.astype(F32)))
        split = jnp.where(at < 3, split, 0.0).astype(BF16)
        parts = dot_f32(split, select, ((1,), (0,)))
        value = parts[0:1] + (parts[1:2] + parts[2:3])
        column = lax.broadcasted_iota(jnp.int32, (8, tile), 0)
        chosen = jnp.where(column == 0, meta_ref[2:3, :], meta_ref[3:4, :])
        comb_ref[...] = jnp.where(chosen > 0, value, 0.0)

    whole = lambda a: pl.BlockSpec(a.shape, lambda i: (0, 0))
    rows = lambda a: pl.BlockSpec((a.shape[0] // steps, a.shape[1]), lambda i: (i, 0))
    cols = pl.BlockSpec((8, tile), lambda i: (0, i))
    return pl.pallas_call(
        body,
        grid=(steps,),
        out_shape=(
            jax.ShapeDtypeStruct((total, SUB), BF16),
            jax.ShapeDtypeStruct((8, total), F32),
            jax.ShapeDtypeStruct(d_gu.shape, F32),
            jax.ShapeDtypeStruct(d_down.shape, F32),
        ),
        in_specs=[cols, whole(fin), whole(score), rows(d_gu), rows(d_down)],
        out_specs=[pl.BlockSpec((tile, SUB), lambda i: (i, 0)), cols, rows(d_gu), rows(d_down)],
        cost_estimate=pl.CostEstimate(flops=2 * total * CAP * SUB, bytes_accessed=12 << 20, transcendentals=0),
    )(meta, fin, score, d_gu, d_down)


def exchange_and_compute(tokens, cotangent, gate_w, up_w, down_w, router, meta):
    own = down_w.shape[0]
    rows_all = 4 * CAP
    vm = pltpu.VMEM
    piece = (CAP, SUB)
    flops = 2 * rows_all * 2 * own * 4 * SUB * 8 // 3
    return pl.pallas_call(
        kernel,
        out_shape=(
            jax.ShapeDtypeStruct(piece, BF16),
            jax.ShapeDtypeStruct((8, 512), F32),
            jax.ShapeDtypeStruct((own * 8, PART), F32),
            jax.ShapeDtypeStruct((own, 512), F32),
        ),
        in_specs=[pl.BlockSpec(memory_space=vm)] * 7,
        out_specs=[pl.BlockSpec(memory_space=vm)] * 4,
        scratch_shapes=[
            vm((CAP, tokens.shape[0]), BF16),
            vm((2,) + piece, BF16),
            vm((2, rows_all, 2 * own), BF16),
            vm((4, 2 * own, SUB), BF16),
            vm((3, 4) + piece, BF16),
            vm((4,) + piece, F32),
            vm((4,) + piece, BF16),
            vm((2, 4) + piece, BF16),
            vm((4, 8, 512), F32),
            vm((3, 8, 512), F32),
            vm((512, PART), F32),
            vm((512, PART), F32),
            vm((4, rows_all, SUB), BF16),
            vm((4, own, SUB), BF16),
            vm((4, own, SUB), BF16),
            vm((4, 2) + piece, BF16),
            vm((8,) + piece, BF16),
            vm((2,) + piece, BF16),
            vm((2, 2) + piece, BF16),
            vm(piece, BF16),
            vm(piece, BF16),
            vm(piece, BF16),
            vm((2,) + piece, BF16),
            vm(piece, BF16),
            vm((3, 8, 512), F32),
            vm((5, 8, 512), F32),
            vm((16, 512), F32),
            pltpu.SemaphoreType.DMA((192,)),
            pltpu.SemaphoreType.DMA((192,)),
        ],
        cost_estimate=pl.CostEstimate(flops=flops, bytes_accessed=20 << 20, transcendentals=CAP * 512),
        compiler_params=pltpu.CompilerParams(
            collective_id=0, has_side_effects=True, vmem_limit_bytes=67043328
        ),
    )(tokens, cotangent, gate_w, up_w, down_w, router, meta)


def local(tokens, cotangent, expert_choice, router, gate_up, w_down):
    own, hid = w_down.shape
    first = expert_choice[:, 0]
    second = expert_choice[:, 1]
    in_first = first == 0
    in_second = second == 0
    routed = jnp.logical_or(in_first, in_second)
    flags = routed.astype(jnp.int32)
    slot_rank = jnp.where(routed, jnp.cumsum(flags) - flags, -1)
    meta = [slot_rank, first + second + 1, in_first.astype(jnp.int32), in_second.astype(jnp.int32)]
    meta = jnp.stack(meta + [flags] * 4)
    fin, score, d_gu, d_down = exchange_and_compute(
        tokens, cotangent, gate_up[:, 0, :], gate_up[:, 1, :], w_down, router, meta
    )
    grad_tokens, combine, d_gu, d_down = finish(meta, fin, score, d_gu, d_down)
    d_gate_up = d_gu.reshape(own, hid // PART, 2, PART).transpose(0, 2, 1, 3).reshape(own, 2, hid)
    return (grad_tokens, combine[:2].T, d_gate_up, d_down)


def solution(mesh):
    split = Mesh(mesh.devices.reshape(4, 2, 2, 4, 2), ALL)
    return jax.shard_map(
        local,
        mesh=split,
        in_specs=(
            P(TOK, HID),
            P(TOK, HID),
            P(TOK, None),
            P(),
            P(TOK, None, HID),
            P(TOK, HID),
        ),
        out_specs=(P(TOK, HID), P(TOK, None), P(TOK, None, HID), P(TOK, HID)),
        check_vma=False,
    )
```

time: 528 us -> 255 us (0.48)
  waiting for transfers between devices: 297 us -> 0 us
  Pallas kernels: 0 us -> 239 us
  blocking collectives: 71.2 us -> 0 us
  local copies, waits for them, and re-layouts: 63.7 us -> 8.39 us
  matrix products: 46.2 us -> 0 us
  other arithmetic: 19.1 us -> 2.04 us
  starting transfers between devices: 15.7 us -> 0 us
  between operations: 14.1 us -> 0.67 us
    pallas_call x0 -> x2, Pallas kernels: none -> 239 us  [the longest x1 232 us: exchange_and_compute(): pl.pallas_call(kernel, out_shape=(jax.ShapeDtypeStruct(piece, BF16), jax....]
    reduce_scatter x2 -> x0, waiting for transfers between devices: 128 us -> none  [the longest x1 75.8 us: local(): back = lax.psum_scatter(back, 'hid', scatter_dimension=0, tiled=False)]
    ppermute x4 -> x0, waiting for transfers between devices: 97.2 us -> none  [the longest x1 76.6 us: local(): other_weights = lax.ppermute(weights, 'zl', [(0, 1), (1, 0)])]
    psum x2 -> x0, blocking collectives: 71.2 us -> none  [the longest x1 37.8 us: local(): scores = lax.psum(score_part, 'hid')]
    all_gather x2 -> x0, waiting for transfers between devices: 71 us -> none  [the longest x1 53 us: local(): mids = lax.all_gather(mids, 'y', axis=0, tiled=True)]
    reshape x5 -> x0, local copies, waits for them, and re-layouts: 48.1 us -> none  [the longest x2 29.2 us: local(): parts = gathered.reshape(4, 4, CAP, 2, cols).transpose(3, 0, 2, 1, 4)]
    dot_general x10 -> x0, matrix products: 46.2 us -> none  [dot_f32(): lax.dot_general(left, right, ((dims[0], dims[1]), ((), ())), preferred_el...]
    ppermute x4 -> x0, starting transfers between devices: 15.5 us -> none  [the longest x1 7.9 us: local(): moved = lax.ppermute(dispatched.astype(jnp.bfloat16), ALL, swap_pairs())]
  transfers between devices with their start and end apart: 8 -> 0, of which waited for: 7 -> 0; matrix products, arithmetic and copies ran while one was open for 7% -> 0% of each run, Pallas kernels for 0% -> 0%
where the time goes in v4:
time: 255 us; the launch traced here: 251 us
  Pallas kernels  239 us (94%)
  local copies, waits for them, and re-layouts  8.39 us (3%)
    pallas_call x1, Pallas kernels, exchange_and_compute(): pl.pallas_call(kernel, out_shape=(jax.ShapeDtypeStruct(piece, BF16), jax....  232 us
    pallas_call x1, Pallas kernels, finish(): pl.pallas_call(body, grid=(steps,), out_shape=(jax.ShapeDtypeStruct((tota...  7.32 us

profile of v4, /device:TPU:24, one launch (start us, length us, event | category | flops | bytes accessed | tf_op | source)
XLA Modules:
  0.0 250.6 jit_solution(6914433273547193286)
XLA Ops:
  0.6 0.8 add_bitcast_fusion.1
  1.4 0.8 bitcast_convert_fusion
  2.3 0.3 reduce-window.9
  2.6 0.1 slice.29
  2.7 0.1 slice_reduce_fusion
  2.8 0.1 add_bitcast_fusion
  2.9 0.7 stack.2.meta.meta_ref
  3.6 4.5 %fusion.2 = (bf16[768,1,512]{2,1,0:T(2,128)(2,1)S(1)}, bf16[768,1,512]{2,1,0:T(2,128)(2,1)S(1)}) fusion(bf16[768,2,512]{2,1,0:T(2,128)(2,1)} %param.10), kind=kLoop, calls=%fused_computation.15 | loop fusion | bytes 3145728 | tf_op jit(solution)/shard_map/slice | solution.py:752
  8.1 1.6 copy_bitcast_fusion
  9.7 232.1 %shard_map.93 = (bf16[432,384]{1,0:T(8,128)(2,1)}, f32[8,512]{1,0:T(8,128)}, f32[6144,128]{1,0:T(8,128)}, f32[768,512]{1,0:T(8,128)}) custom-call(bf16[1536,384]{1,0:T(8,128)(2,1)} %tokens.1, bf16[1536,384]{1,0:T(8,128)(2,1)} %cotangent.1, bf16[768,512]{1,0:T(8,128)(2,1)} %get-tuple-element.27.gate_w, bf16[768,512]{1,0:T(8,128)(2,1)} %get-tuple-element.26.up_w, ...), custom_call_target="tpu_custom_call" | custom-call | flops 21743271936 | bytes 20971520 | tf_op jit(solution)/shard_map/pallas_call | solution.py:692
  241.8 7.3 %shard_map.94 = (bf16[1536,384]{1,0:T(8,128)(2,1)}, f32[8,1536]{1,0:T(8,128)}, f32[6144,128]{1,0:T(8,128)}, f32[768,512]{1,0:T(8,128)}) custom-call(s32[8,1536]{1,0:T(8,128)} %stack.2.meta.meta_ref, bf16[432,384]{1,0:T(8,128)(2,1)} %get-tuple-element.12.fin_ref, f32[8,512]{1,0:T(8,128)} %get-tuple-element.13.score_ref, ...), custom_call_target="tpu_custom_call" | custom-call | flops 509607936 | bytes 12582912 | tf_op jit(solution)/shard_map/pallas_call | solution.py:671
  249.2 1.4 slice_bitcast_fusion
  (3 shorter events, 0.1 us)

commit v5 on v4

--- a/solution.py
+++ b/solution.py
@@ -28,10 +28,10 @@
 
 
 def kernel(
-    tokens, cotangent, gate_w, up_w, down_w, router, meta,
-    fin, score_out, dgu_out, dd_out,
+    tokens, cotangent, gate_up, down_w, router, choice,
+    fin, comb_out, rank_out, dgu_out, dd_out,
     select, xin, rows, wgt, psend, pown, prelay, precv, lsend, lrecv, gate, sacc, mids,
-    gsend, grecv, bown, brecv, xrelay, xrecv, zsend, zrecv, fsend, stage, zstage, srow, srecv, labels,
+    gsend, grecv, bown, brecv, xrelay, xrecv, zsend, zrecv, fsend, srow, srecv, labels, meta, flags,
     ssem, rsem,
 ):
     y, zl, zh, x, c = (lax.axis_index(a) for a in ALL)
@@ -70,7 +70,7 @@
     barrier = pltpu.get_barrier_semaphore()
     peers = (
         dict(y=yr), dict(y=yl), dict(y=yo), dict(zl=1 - zl), dict(zh=1 - zh),
-        dict(x=xr), dict(x=xl), dict(x=xo), dict(c=1 - c), dict(zl=1 - zl, zh=1 - zh),
+        dict(x=xr), dict(x=xl), dict(x=xo), dict(c=1 - c),
     )
     for peer in peers:
         pl.semaphore_signal(barrier, inc=1, device_id=peer, device_id_type=MESH)
@@ -96,6 +96,31 @@
 
     def move(p):
         return copy(("move", p), xin.at[:, part(p), :], place(p, swap_zh, swap_x, c), **swap)
+
+    total = tokens.shape[0]
+    first, second = choice[0:1, :], choice[1:2, :]
+    routed = jnp.logical_or(first == 0, second == 0)
+    hits = jnp.where(routed, 1.0, 0.0)
+    flags[...] = jnp.zeros_like(flags)
+    for i in range(total // PART):
+        flags[i : i + 1, :] = hits[:, PART * i : PART * (i + 1)]
+    lane = lax.broadcasted_iota(jnp.int32, (PART, PART), 0)
+    before = jnp.where(lane < lax.broadcasted_iota(jnp.int32, (PART, PART), 1), 1.0, 0.0)
+    line = lax.broadcasted_iota(jnp.int32, (16, 16), 0)
+    above = jnp.where(line > lax.broadcasted_iota(jnp.int32, (16, 16), 1), 1.0, 0.0)
+    marks = flags[...].astype(BF16)
+    within = dot_f32(marks, before.astype(BF16), ((1,), (0,)))
+    counts = dot_f32(marks, jnp.ones((PART, PART), BF16), ((1,), (0,)))
+    flags[...] = within + dot_f32(above.astype(BF16), counts.astype(BF16), ((1,), (0,)))
+    for i in range(total // PART):
+        at = slice(PART * i, PART * (i + 1))
+        rank = flags[i : i + 1, :].astype(jnp.int32)
+        meta[0:1, at] = jnp.where(routed[:, at], rank, -1)
+    meta[1:2, :] = first + second + 1
+    meta[2:3, :] = jnp.where(first == 0, 1, 0)
+    meta[3:4, :] = jnp.where(second == 0, 1, 0)
+    meta[4:8, :] = jnp.zeros((4, total), jnp.int32)
+    rank_out[...] = meta[...]
 
     for p in range(2):
         slots = lax.broadcasted_iota(jnp.int32, (PN[p], tokens.shape[0]), 0) + P0[p]
@@ -107,8 +132,8 @@
         at = pl.ds(pl.multiple_of(zl * own + i * 96, 16), 96)
         of = pl.ds(pl.multiple_of(i * 96, 16), 96)
         for sub in range(4):
-            for n, ref in enumerate((gate_w, up_w, down_w)):
-                wgt[sub, at, PART * n : PART * (n + 1)] = ref[of, PART * sub : PART * (sub + 1)]
+            for n, (ref, base) in enumerate(((gate_up, 0), (gate_up, 512), (down_w, 0))):
+                wgt[sub, at, PART * n : PART * (n + 1)] = ref[of, base + PART * sub : base + PART * (sub + 1)]
         return carry
 
     lax.fori_loop(0, own // 96, put_weights, 0)
@@ -136,8 +161,7 @@
     labels[:, :CAP] = dot_f32(named, select[...], ((1,), (1,)))
 
     steps = {
-        "za": (lambda p: (place(p, zh, x, c), stage.at[:, part(p), :]), dict(zl=1 - zl)),
-        "zb": (lambda p: (stage.at[:, part(p), :], place(p, zh, x, c)), dict(zl=1 - zl, zh=1 - zh)),
+        "zh": (lambda p: place(p, zh, x, c), dict(zh=1 - zh)),
         "xr0": (lambda p: place(p, zh, x, c), dict(x=xr)),
         "xl0": (lambda p: place(p, zh, x, c), dict(x=xl)),
         "xro": (lambda p: place(p, zh, xl, c), dict(x=xr)),
@@ -156,9 +180,7 @@
 
     def hop(name, p):
         at, to = steps[name]
-        ends = at(p)
-        src, dst = ends if isinstance(ends, tuple) else (ends, ends)
-        return copy((name, p), src, dst, **to)
+        return copy((name, p), at(p), at(p), **to)
 
     def arrive(name, p, *then):
         hop(name, p).wait_recv()
@@ -176,10 +198,10 @@
         def _():
             move(p).wait_recv()
 
-        for name in ("za", "xr0", "xl0", "c_own"):
+        for name in ("zh", "xr0", "xl0", "c_own"):
             start(hop(name, p))
-        start(weights(p + 1))
-    start(weights(3))
+    for sub in range(1, 4):
+        start(weights(sub))
 
     rs_base = index("rs", 48)
     ag_base = index("ag", 48)
@@ -370,8 +392,8 @@
         return copy(("sc", key), srow.at[src], srecv.at[dst], **to)
 
     def scores():
-        total = jnp.sum(jnp.transpose(sacc[...]), axis=0, keepdims=True)
-        srow[0] = jnp.broadcast_to(total, (8, 512))
+        summed = jnp.sum(jnp.transpose(sacc[...]), axis=0, keepdims=True)
+        srow[0] = jnp.broadcast_to(summed, (8, 512))
         start(score("c"))
 
     def scores_zh():
@@ -388,7 +410,17 @@
     def scores_end():
         for key in ("x0", "x1", "x2"):
             score(key).wait_recv()
-        score_out[...] = (srow[2] + srecv[2]) + (srecv[3] + srecv[4])
+        exact = ((srow[2] + srecv[2]) + (srecv[3] + srecv[4]))[0:1, :CAP]
+        high = exact.astype(BF16).astype(F32)
+        middle = (exact - high).astype(BF16).astype(F32)
+        at = lax.broadcasted_iota(jnp.int32, (16, CAP), 0)
+        split = jnp.where(at == 0, high, jnp.where(at == 1, middle, exact - high - middle))
+        split = jnp.where(at < 3, split, 0.0).astype(BF16)
+        parts = dot_f32(split, select[...], ((1,), (0,)))
+        value = parts[0:1] + (parts[1:2] + parts[2:3])
+        column = lax.broadcasted_iota(jnp.int32, (8, total), 0)
+        chosen = jnp.where(column == 0, meta[2:3, :], meta[3:4, :])
+        comb_out[...] = jnp.where(chosen > 0, value, 0.0)
 
     pair_base = index("pair", 16)
 
@@ -406,15 +438,8 @@
         }[kind]()
         return copy(("bx", kind, half, p), src, dst, x=to)
 
-    def last_a(p):
-        return copy(("bza", p), zsend.at[part(p), :], zstage.at[part(p), :], zl=1 - zl)
-
-    def last_b(p):
-        return copy(("bzb", p), zstage.at[part(p), :], zrecv.at[part(p), :], zl=1 - zl, zh=1 - zh)
-
-    def last_relay(p):
-        last_a(p).wait_recv()
-        start(last_b(p))
+    def last(p):
+        return copy(("bz", p), zsend.at[part(p), :], zrecv.at[part(p), :], zh=1 - zh)
 
     def home(p):
         return copy(("home", p), fsend.at[part(p), :], fin.at[part(p), :], **swap)
@@ -480,10 +505,10 @@
             for kind in ("near_r", "near_l"):
                 ring(kind, half, p).wait_recv()
         add_rows(p, zsend, [bown.at[x, 1 - zh], xrecv.at[0, 1 - zh], xrecv.at[1, 1 - zh]])
-        start(last_a(p))
+        start(last(p))
 
     def go_home(p):
-        last_b(p).wait_recv()
+        last(p).wait_recv()
         add_rows(p, fsend, [bown.at[x, zh], xrecv.at[0, zh], xrecv.at[1, zh], zrecv])
 
         @pl.when(fixed)
@@ -496,13 +521,11 @@
 
     arrive("xr0", 0, "xro", "c_xr0")
     arrive("xl0", 0, "c_xl0")
-    arrive("za", 0, "zb")
-    arrive("zb", 0, "xr1", "xl1", "c_zh")
+    arrive("zh", 0, "xr1", "xl1", "c_zh")
     arrive("xr0", 1, "xro", "c_xr0")
     arrive("xl0", 1, "c_xl0")
-    arrive("za", 1, "zb")
+    arrive("zh", 1, "xr1", "xl1", "c_zh")
     arrive("xl1", 0, "xlo", "c_xl1")
-    arrive("zb", 1, "xr1", "xl1", "c_zh")
     arrive("xro", 0, "c_xro")
     arrive("xr1", 0, "c_xr1")
     arrive("xl1", 1, "xlo", "c_xl1")
@@ -516,9 +539,9 @@
     arrive("xlo", 1, "c_xlo")
     all_cores(1)
     pre(1, 0)
+    logits()
     relay(0, 0)
     relay(0, 1)
-    logits()
     weights(2).wait_recv()
     weights(3).wait_recv()
     pre(0, 1)
@@ -526,90 +549,86 @@
     relay(1, 1)
     pre(1, 1)
     gates()
+    relay(0, 2)
+    relay(0, 3)
     pointwise(0, 0)
     pointwise(1, 0)
-    relay(0, 2)
-    relay(0, 3)
-    pointwise(0, 1)
-    pointwise(1, 1)
     relay(1, 2)
     relay(1, 3)
     forward(0, 0)
+    pointwise(0, 1)
     forward(1, 0)
+    pointwise(1, 1)
+    forward(0, 1)
+    for p in range(2):
+        near(p, 0)
+        far(p, 0)
     pointwise(0, 2)
-    pointwise(0, 3)
-    forward(0, 1)
     forward(1, 1)
-    pointwise(1, 2)
-    pointwise(1, 3)
-    scores()
-    near(0, 0)
-    near(1, 0)
-    far(0, 0)
-    far(1, 0)
-    scores_zh()
     grads_theirs(0)
     start(exchange(0))
+    pointwise(0, 3)
     forward(0, 2)
+    pointwise(1, 2)
     forward(0, 3)
+    pointwise(1, 3)
     for kind in RS_KINDS:
         for p in range(2):
             for s in range(4):
                 rs(kind, p, s).wait_send()
     back_block(0, y)
-    near(0, 1)
-    near(1, 1)
-    far(0, 1)
-    far(1, 1)
+    scores()
+    for p in range(2):
+        near(p, 1)
+        far(p, 1)
     grads_theirs(1)
     start(exchange(1))
-    near(0, 2)
-    near(0, 3)
+    forward(1, 2)
+    for s in range(2, 4):
+        near(0, s)
     back_block(0, yr)
-    forward(1, 2)
     forward(1, 3)
     back_block(0, yl)
-    far(0, 2)
-    far(0, 3)
+    for s in range(2, 4):
+        far(0, s)
     back_block(0, yo)
-    back_block(1, y)
     back_sum(0, y)
     back_sum(0, yr)
     back_sum(0, yl)
     back_sum(0, yo)
+    scores_zh()
     near(1, 2)
+    far(1, 2)
+    grads_theirs(2)
+    start(exchange(2))
+    back_block(1, y)
     near(1, 3)
     back_block(1, yr)
+    ring_relay(0)
     back_block(1, yl)
-    far(1, 2)
     far(1, 3)
     back_block(1, yo)
-    ring_relay(0)
     back_sum(1, y)
     back_sum(1, yr)
     back_sum(1, yl)
     back_sum(1, yo)
-    grads_theirs(2)
-    start(exchange(2))
+    grads_theirs(3)
     ring_end(0)
-    grads_theirs(3)
     start(exchange(3, 0))
     ring_relay(1)
-    last_relay(0)
+    scores_x()
     grads_mine(0)
+    add_grads(0)
     ring_end(1)
     start(exchange(3, 1))
-    scores_x()
     go_home(0)
-    last_relay(1)
     grads_mine(1)
-    add_grads(0)
     add_grads(1)
+    grads_mine(2)
     go_home(1)
-    grads_mine(2)
     grads_mine(3)
+    add_grads(2)
     scores_end()
-    add_grads(2)
 
     @pl.when(moves)
     def _():
@@ -639,51 +658,35 @@
         cp.wait_send()
 
 
-def finish(meta, fin, score, d_gu, d_down):
-    total = meta.shape[1]
-    steps = 6
+def finish(ranks, fin, d_gu, d_down):
+    total = ranks.shape[1]
+    steps = 3
     tile = total // steps
-    vm = pltpu.VMEM
-
-    def body(meta_ref, fin_ref, score_ref, gu_ref, down_ref, gtok_ref, comb_ref, gu_out, down_out):
+
+    def body(ranks_ref, fin_ref, gu_ref, down_ref, gtok_ref, gu_out, down_out):
         gu_out[...] = gu_ref[...]
         down_out[...] = down_ref[...]
         slots = lax.broadcasted_iota(jnp.int32, (CAP, tile), 0)
-        select = jnp.where(slots == meta_ref[0:1, :], 1.0, 0.0).astype(BF16)
+        select = jnp.where(slots == ranks_ref[0:1, :], 1.0, 0.0).astype(BF16)
         gtok_ref[...] = dot_f32(select, fin_ref[...], ((0,), (0,))).astype(BF16)
-        exact = score_ref[0:1, :CAP]
-        high = exact.astype(BF16)
-        rest = exact - high.astype(F32)
-        middle = rest.astype(BF16)
-        low = (rest - middle.astype(F32)).astype(BF16)
-        at = lax.broadcasted_iota(jnp.int32, (16, CAP), 0)
-        split = jnp.where(at == 0, high.astype(F32), jnp.where(at == 1, middle.astype(F32), low.astype(F32)))
-        split = jnp.where(at < 3, split, 0.0).astype(BF16)
-        parts = dot_f32(split, select, ((1,), (0,)))
-        value = parts[0:1] + (parts[1:2] + parts[2:3])
-        column = lax.broadcasted_iota(jnp.int32, (8, tile), 0)
-        chosen = jnp.where(column == 0, meta_ref[2:3, :], meta_ref[3:4, :])
-        comb_ref[...] = jnp.where(chosen > 0, value, 0.0)
 
     whole = lambda a: pl.BlockSpec(a.shape, lambda i: (0, 0))
     rows = lambda a: pl.BlockSpec((a.shape[0] // steps, a.shape[1]), lambda i: (i, 0))
-    cols = pl.BlockSpec((8, tile), lambda i: (0, i))
     return pl.pallas_call(
         body,
         grid=(steps,),
         out_shape=(
             jax.ShapeDtypeStruct((total, SUB), BF16),
-            jax.ShapeDtypeStruct((8, total), F32),
             jax.ShapeDtypeStruct(d_gu.shape, F32),
             jax.ShapeDtypeStruct(d_down.shape, F32),
         ),
-        in_specs=[cols, whole(fin), whole(score), rows(d_gu), rows(d_down)],
-        out_specs=[pl.BlockSpec((tile, SUB), lambda i: (i, 0)), cols, rows(d_gu), rows(d_down)],
+        in_specs=[pl.BlockSpec((8, tile), lambda i: (0, i)), whole(fin), rows(d_gu), rows(d_down)],
+        out_specs=[pl.BlockSpec((tile, SUB), lambda i: (i, 0)), rows(d_gu), rows(d_down)],
         cost_estimate=pl.CostEstimate(flops=2 * total * CAP * SUB, bytes_accessed=12 << 20, transcendentals=0),
-    )(meta, fin, score, d_gu, d_down)
-
-
-def exchange_and_compute(tokens, cotangent, gate_w, up_w, down_w, router, meta):
+    )(ranks, fin, d_gu, d_down)
+
+
+def exchange_and_compute(tokens, cotangent, gate_up, down_w, router, choice):
     own = down_w.shape[0]
     rows_all = 4 * CAP
     vm = pltpu.VMEM
@@ -693,12 +696,13 @@
         kernel,
         out_shape=(
             jax.ShapeDtypeStruct(piece, BF16),
-            jax.ShapeDtypeStruct((8, 512), F32),
+            jax.ShapeDtypeStruct((8, tokens.shape[0]), F32),
+            jax.ShapeDtypeStruct((8, tokens.shape[0]), jnp.int32),
             jax.ShapeDtypeStruct((own * 8, PART), F32),
             jax.ShapeDtypeStruct((own, 512), F32),
         ),
-        in_specs=[pl.BlockSpec(memory_space=vm)] * 7,
-        out_specs=[pl.BlockSpec(memory_space=vm)] * 4,
+        in_specs=[pl.BlockSpec(memory_space=vm)] * 6,
+        out_specs=[pl.BlockSpec(memory_space=vm)] * 5,
         scratch_shapes=[
             vm((CAP, tokens.shape[0]), BF16),
             vm((2,) + piece, BF16),
@@ -722,11 +726,11 @@
             vm(piece, BF16),
             vm(piece, BF16),
             vm(piece, BF16),
-            vm((2,) + piece, BF16),
-            vm(piece, BF16),
             vm((3, 8, 512), F32),
             vm((5, 8, 512), F32),
             vm((16, 512), F32),
+            vm((8, tokens.shape[0]), jnp.int32),
+            vm((16, PART), F32),
             pltpu.SemaphoreType.DMA((192,)),
             pltpu.SemaphoreType.DMA((192,)),
         ],
@@ -734,24 +738,15 @@
         compiler_params=pltpu.CompilerParams(
             collective_id=0, has_side_effects=True, vmem_limit_bytes=67043328
         ),
-    )(tokens, cotangent, gate_w, up_w, down_w, router, meta)
+    )(tokens, cotangent, gate_up, down_w, router, choice)
 
 
 def local(tokens, cotangent, expert_choice, router, gate_up, w_down):
     own, hid = w_down.shape
-    first = expert_choice[:, 0]
-    second = expert_choice[:, 1]
-    in_first = first == 0
-    in_second = second == 0
-    routed = jnp.logical_or(in_first, in_second)
-    flags = routed.astype(jnp.int32)
-    slot_rank = jnp.where(routed, jnp.cumsum(flags) - flags, -1)
-    meta = [slot_rank, first + second + 1, in_first.astype(jnp.int32), in_second.astype(jnp.int32)]
-    meta = jnp.stack(meta + [flags] * 4)
-    fin, score, d_gu, d_down = exchange_and_compute(
-        tokens, cotangent, gate_up[:, 0, :], gate_up[:, 1, :], w_down, router, meta
+    fin, combine, ranks, d_gu, d_down = exchange_and_compute(
+        tokens, cotangent, gate_up.reshape(own, 2 * hid), w_down, router, expert_choice.T
     )
-    grad_tokens, combine, d_gu, d_down = finish(meta, fin, score, d_gu, d_down)
+    grad_tokens, d_gu, d_down = finish(ranks, fin, d_gu, d_down)
     d_gate_up = d_gu.reshape(own, hid // PART, 2, PART).transpose(0, 2, 1, 3).reshape(own, 2, hid)
     return (grad_tokens, combine[:2].T, d_gate_up, d_down)
 

time: 255 us -> 223 us (0.87); the launches traced: 251 us -> 222 us
  Pallas kernels: 239 us -> 217 us
  local copies, waits for them, and re-layouts: 8.39 us -> 4.37 us
    pallas_call x1, Pallas kernels: 232 us -> 210 us  [exchange_and_compute(): pl.pallas_call(kernel, out_shape=(jax.ShapeDtypeStruct(piece, BF16), jax....]
    slice x2 -> x0, local copies, waits for them, and re-layouts: 4.6 us -> none  [the longest x1 4.53 us: local(): gate_up[:, 1, :]]
    unnamed x0 -> x1, local copies, waits for them, and re-layouts: none -> 2.97 us
where the time goes in v5:
time: 223 us; the launch traced here: 222 us
  Pallas kernels  217 us (97%)
  local copies, waits for them, and re-layouts  4.37 us (2%)
    pallas_call x1, Pallas kernels, exchange_and_compute(): pl.pallas_call(kernel, out_shape=(jax.ShapeDtypeStruct(piece, BF16), jax....  210 us
    pallas_call x1, Pallas kernels, finish(): pl.pallas_call(body, grid=(steps,), out_shape=(jax.ShapeDtypeStruct((tota...  6.64 us

profile of v5, /device:TPU:24, one launch (start us, length us, event | category | flops | bytes accessed | tf_op | source)
XLA Modules:
  0.0 221.5 jit_solution(11531383855452596100)
XLA Ops:
  0.6 3.0 %copy.11 = bf16[96,8,2,512]{3,1,2,0:T(8,128)(2,1)} copy(bf16[96,8,2,512]{3,2,1,0:T(2,128)(2,1)} %bitcast.10) | data formatting | bytes 3145728
  3.6 209.9 %shard_map.93 = (bf16[432,384]{1,0:T(8,128)(2,1)}, f32[8,1536]{1,0:T(8,128)}, s32[8,1536]{1,0:T(8,128)}, f32[6144,128]{1,0:T(8,128)}, f32[768,512]{1,0:T(8,128)}) custom-call(bf16[1536,384]{1,0:T(8,128)(2,1)} %tokens.1, bf16[1536,384]{1,0:T(8,128)(2,1)} %cotangent.1, bf16[768,1024]{1,0:T(8,128)(2,1)} %bitcast.11, bf16[768,512]{1,0:T(8,128)(2,1)} %down_w.1, ...), custom_call_target="tpu_custom_call" | custom-call | flops 21743271936 | bytes 20971520 | tf_op jit(solution)/shard_map/pallas_call | solution.py:695
  213.5 1.4 slice_bitcast_fusion
  214.9 6.6 %shard_map.94 = (bf16[1536,384]{1,0:T(8,128)(2,1)}, f32[6144,128]{1,0:T(8,128)}, f32[768,512]{1,0:T(8,128)}) custom-call(s32[8,1536]{1,0:T(8,128)} %get-tuple-element.12.ranks_ref, bf16[432,384]{1,0:T(8,128)(2,1)} %get-tuple-element.13.fin_ref, f32[6144,128]{1,0:T(8,128)} %get-tuple-element.14.gu_ref, f32[768,512]{1,0:T(8,128)} %get-tuple-element.15.down_ref), custom_call_target="tpu_custom_call" | custom-call | flops 509607936 | bytes 12582912 | tf_op jit(solution)/shard_map/pallas_call | solution.py:675

commit v6 on v5

--- a/solution.py
+++ b/solution.py
@@ -29,10 +29,10 @@
 
 def kernel(
     tokens, cotangent, gate_up, down_w, router, choice,
-    fin, comb_out, rank_out, dgu_out, dd_out,
+    fin_out, comb_out, rank_out, acc_out,
     select, xin, rows, wgt, psend, pown, prelay, precv, lsend, lrecv, gate, sacc, mids,
-    gsend, grecv, bown, brecv, xrelay, xrecv, zsend, zrecv, fsend, srow, srecv, labels, meta, flags,
-    ssem, rsem,
+    gsend, grecv, bown, brecv, xrelay, xrecv, zsend, zrecv, fsend, fin, srow, srecv, labels, meta, flags, comb, acc,
+    ssem, rsem, osem,
 ):
     y, zl, zh, x, c = (lax.axis_index(a) for a in ALL)
     yr, yl, yo = (y + 1) % 4, (y + 3) % 4, (y + 2) % 4
@@ -120,13 +120,43 @@
     meta[2:3, :] = jnp.where(first == 0, 1, 0)
     meta[3:4, :] = jnp.where(second == 0, 1, 0)
     meta[4:8, :] = jnp.zeros((4, total), jnp.int32)
-    rank_out[...] = meta[...]
-
-    for p in range(2):
-        slots = lax.broadcasted_iota(jnp.int32, (PN[p], tokens.shape[0]), 0) + P0[p]
+    leave = []
+
+    def put_out(src, dst):
+        cp = pltpu.make_async_copy(src, dst, osem.at[len(leave)])
+        cp.start()
+        leave.append(cp)
+
+    put_out(meta, rank_out)
+
+    def dispatch(p):
+        slots = lax.broadcasted_iota(jnp.int32, (PN[p], total), 0) + P0[p]
         select[part(p), :] = jnp.where(slots == meta[0:1, :], 1.0, 0.0).astype(BF16)
         xin[0, part(p), :] = dot_f32(select[part(p), :], tokens[...], ((1,), (0,))).astype(BF16)
         xin[1, part(p), :] = dot_f32(select[part(p), :], cotangent[...], ((1,), (0,))).astype(BF16)
+
+    def send(p):
+        @pl.when(fixed)
+        def _():
+            place(p, zh, x, c)[...] = xin[:, part(p), :]
+
+        @pl.when(moves)
+        def _():
+            move(p).start()
+
+    dispatch(0)
+
+    @pl.when(moves)
+    def _():
+        pl.semaphore_wait(barrier, len(peers) + 1)
+
+    @pl.when(fixed)
+    def _():
+        pl.semaphore_wait(barrier, len(peers))
+
+    send(0)
+    dispatch(1)
+    send(1)
 
     def put_weights(i, carry):
         at = pl.ds(pl.multiple_of(zl * own + i * 96, 16), 96)
@@ -137,25 +167,6 @@
         return carry
 
     lax.fori_loop(0, own // 96, put_weights, 0)
-
-    @pl.when(moves)
-    def _():
-        pl.semaphore_wait(barrier, len(peers) + 1)
-
-    @pl.when(fixed)
-    def _():
-        pl.semaphore_wait(barrier, len(peers))
-
-    for p in range(2):
-
-        @pl.when(fixed)
-        def _():
-            place(p, zh, x, c)[...] = xin[:, part(p), :]
-
-        @pl.when(moves)
-        def _():
-            move(p).start()
-
     start(weights(0))
     named = jnp.broadcast_to(meta[1:2, :].astype(F32).astype(BF16), (16, tokens.shape[0]))
     labels[:, :CAP] = dot_f32(named, select[...], ((1,), (1,)))
@@ -338,9 +349,6 @@
         at = pl.ds(0, own) if half is None else pl.ds(half * (own // 2), own // 2)
         return copy(("gz", s, half), gsend.at[s, at, :], grecv.at[s, at, :], zl=1 - zl)
 
-    def out_rows(first, count, sub, g):
-        return pl.ds(first * 8 + 2 * sub + g, count, stride=8)
-
     def grads_tile(s, at):
         gu = dot_f32(rows[0, :, pl.ds(at, 256)], mids[s, :, : 2 * PART], ((0,), (0,)))
         return gu, dot_f32(rows[1, :, pl.ds(at, 256)], mids[s, :, 2 * PART :], ((0,), (0,)))
@@ -358,10 +366,10 @@
     def grads_mine(s):
         def one(i, carry):
             gu, d = grads_tile(s, pl.multiple_of(zl * own + i * 256, 256))
+            to = pl.ds(pl.multiple_of(i * 256, 256), 256)
             for g in range(2):
-                dgu_out[out_rows(i * 256, 256, s, g), :] = gu[:, PART * g : PART * (g + 1)]
-            to = pl.ds(pl.multiple_of(i * 256, 256), 256)
-            dd_out[to, s * PART : (s + 1) * PART] = d
+                acc[3 * s + g, to, :] = gu[:, PART * g : PART * (g + 1)]
+            acc[3 * s + 2, to, :] = d
             return carry
 
         lax.fori_loop(0, own // 256, one, 0)
@@ -372,10 +380,8 @@
         def one(i, carry):
             at = pl.ds(pl.multiple_of(i * 64, 16), 64)
             got = grecv[s, at, :].astype(F32)
-            for g in range(2):
-                to = out_rows(i * 64, 64, s, g)
-                dgu_out[to, :] = dgu_out[to, :] + got[:, PART * g : PART * (g + 1)]
-            dd_out[at, s * PART : (s + 1) * PART] += got[:, 2 * PART :]
+            for g in range(3):
+                acc[3 * s + g, at, :] += got[:, PART * g : PART * (g + 1)]
             return carry
 
         count = own // 64
@@ -383,6 +389,8 @@
             lax.fori_loop(0, count, one, 0)
         else:
             lax.fori_loop(half * (count // 2), (half + 1) * (count // 2), one, 0)
+        at = pl.ds(0, own) if half is None else pl.ds(half * (own // 2), own // 2)
+        put_out(acc.at[pl.ds(3 * s, 3), at, :], acc_out.at[pl.ds(3 * s, 3), at, :])
 
     def score(key):
         src, dst, to = {
@@ -420,7 +428,8 @@
         value = parts[0:1] + (parts[1:2] + parts[2:3])
         column = lax.broadcasted_iota(jnp.int32, (8, total), 0)
         chosen = jnp.where(column == 0, meta[2:3, :], meta[3:4, :])
-        comb_out[...] = jnp.where(chosen > 0, value, 0.0)
+        comb[...] = jnp.where(chosen > 0, value, 0.0)
+        put_out(comb, comb_out)
 
     pair_base = index("pair", 16)
 
@@ -540,71 +549,70 @@
     all_cores(1)
     pre(1, 0)
     logits()
-    relay(0, 0)
-    relay(0, 1)
+    for p in range(2):
+        for s in range(2):
+            relay(p, s)
+    gates()
+    pointwise(0, 0)
+    pointwise(0, 1)
     weights(2).wait_recv()
     weights(3).wait_recv()
     pre(0, 1)
-    relay(1, 0)
-    relay(1, 1)
+    pointwise(1, 0)
+    pointwise(1, 1)
+    forward(0, 0)
+    forward(0, 1)
     pre(1, 1)
-    gates()
     relay(0, 2)
     relay(0, 3)
-    pointwise(0, 0)
-    pointwise(1, 0)
+    forward(1, 0)
+    forward(1, 1)
     relay(1, 2)
     relay(1, 3)
-    forward(0, 0)
-    pointwise(0, 1)
-    forward(1, 0)
-    pointwise(1, 1)
-    forward(0, 1)
     for p in range(2):
         near(p, 0)
         far(p, 0)
-    pointwise(0, 2)
-    forward(1, 1)
     grads_theirs(0)
     start(exchange(0))
+    pointwise(0, 2)
+    for p in range(2):
+        near(p, 1)
+        far(p, 1)
+    grads_theirs(1)
+    start(exchange(1))
+    pointwise(1, 2)
+    forward(0, 2)
     pointwise(0, 3)
-    forward(0, 2)
-    pointwise(1, 2)
-    forward(0, 3)
+    forward(1, 2)
     pointwise(1, 3)
     for kind in RS_KINDS:
         for p in range(2):
             for s in range(4):
                 rs(kind, p, s).wait_send()
+    scores()
+    grads_mine(0)
     back_block(0, y)
-    scores()
+    forward(0, 3)
+    grads_mine(1)
+    scores_zh()
     for p in range(2):
-        near(p, 1)
-        far(p, 1)
-    grads_theirs(1)
-    start(exchange(1))
-    forward(1, 2)
-    for s in range(2, 4):
-        near(0, s)
+        near(p, 2)
+        far(p, 2)
+    grads_theirs(2)
+    start(exchange(2))
+    forward(1, 3)
+    near(0, 3)
     back_block(0, yr)
-    forward(1, 3)
     back_block(0, yl)
-    for s in range(2, 4):
-        far(0, s)
+    far(0, 3)
     back_block(0, yo)
     back_sum(0, y)
     back_sum(0, yr)
     back_sum(0, yl)
     back_sum(0, yo)
-    scores_zh()
-    near(1, 2)
-    far(1, 2)
-    grads_theirs(2)
-    start(exchange(2))
     back_block(1, y)
     near(1, 3)
     back_block(1, yr)
-    ring_relay(0)
     back_block(1, yl)
     far(1, 3)
     back_block(1, yo)
@@ -612,28 +620,29 @@
     back_sum(1, yr)
     back_sum(1, yl)
     back_sum(1, yo)
+    ring_relay(0)
     grads_theirs(3)
-    ring_end(0)
     start(exchange(3, 0))
     ring_relay(1)
+    ring_end(0)
+    start(exchange(3, 1))
     scores_x()
-    grads_mine(0)
     add_grads(0)
-    ring_end(1)
-    start(exchange(3, 1))
-    go_home(0)
-    grads_mine(1)
     add_grads(1)
     grads_mine(2)
-    go_home(1)
+    ring_end(1)
+    go_home(0)
     grads_mine(3)
     add_grads(2)
     scores_end()
+    go_home(1)
 
     @pl.when(moves)
     def _():
         home(0).wait_recv()
         home(1).wait_recv()
+
+    put_out(fin, fin_out)
 
     add_grads(3, 0)
     add_grads(3, 1)
@@ -656,34 +665,45 @@
             pair(p, i).wait_send()
     for cp in started:
         cp.wait_send()
-
-
-def finish(ranks, fin, d_gu, d_down):
-    total = ranks.shape[1]
-    steps = 3
-    tile = total // steps
-
-    def body(ranks_ref, fin_ref, gu_ref, down_ref, gtok_ref, gu_out, down_out):
-        gu_out[...] = gu_ref[...]
-        down_out[...] = down_ref[...]
+    for cp in leave:
+        cp.wait()
+
+
+def finish(ranks, fin, combine, sums):
+    total, own = ranks.shape[1], sums.shape[1]
+    steps = 4
+    tile, deep = total // steps, own // steps
+
+    def body(ranks_ref, fin_ref, comb_ref, sums_ref, gtok_ref, comb_out, gu_out, down_out):
+        for s in range(4):
+            for g in range(2):
+                gu_out[pl.ds(2 * s + g, deep, stride=8), :] = sums_ref[3 * s + g]
+            down_out[:, PART * s : PART * (s + 1)] = sums_ref[3 * s + 2]
+        comb_out[...] = comb_ref[0:2, :]
         slots = lax.broadcasted_iota(jnp.int32, (CAP, tile), 0)
         select = jnp.where(slots == ranks_ref[0:1, :], 1.0, 0.0).astype(BF16)
         gtok_ref[...] = dot_f32(select, fin_ref[...], ((0,), (0,))).astype(BF16)
 
-    whole = lambda a: pl.BlockSpec(a.shape, lambda i: (0, 0))
-    rows = lambda a: pl.BlockSpec((a.shape[0] // steps, a.shape[1]), lambda i: (i, 0))
+    cols = lambda n: pl.BlockSpec((n, tile), lambda i: (0, i))
+    rows = lambda n, m: pl.BlockSpec((n, m), lambda i: (i, 0))
     return pl.pallas_call(
         body,
         grid=(steps,),
         out_shape=(
             jax.ShapeDtypeStruct((total, SUB), BF16),
-            jax.ShapeDtypeStruct(d_gu.shape, F32),
-            jax.ShapeDtypeStruct(d_down.shape, F32),
+            jax.ShapeDtypeStruct((2, total), F32),
+            jax.ShapeDtypeStruct((own * 8, PART), F32),
+            jax.ShapeDtypeStruct((own, 4 * PART), F32),
         ),
-        in_specs=[pl.BlockSpec((8, tile), lambda i: (0, i)), whole(fin), rows(d_gu), rows(d_down)],
-        out_specs=[pl.BlockSpec((tile, SUB), lambda i: (i, 0)), rows(d_gu), rows(d_down)],
+        in_specs=[
+            cols(8),
+            pl.BlockSpec(fin.shape, lambda i: (0, 0)),
+            cols(8),
+            pl.BlockSpec((12, deep, PART), lambda i: (0, i, 0)),
+        ],
+        out_specs=[rows(tile, SUB), cols(2), rows(deep * 8, PART), rows(deep, 4 * PART)],
         cost_estimate=pl.CostEstimate(flops=2 * total * CAP * SUB, bytes_accessed=12 << 20, transcendentals=0),
-    )(ranks, fin, d_gu, d_down)
+    )(ranks, fin, combine, sums)
 
 
 def exchange_and_compute(tokens, cotangent, gate_up, down_w, router, choice):
@@ -698,11 +718,10 @@
             jax.ShapeDtypeStruct(piece, BF16),
             jax.ShapeDtypeStruct((8, tokens.shape[0]), F32),
             jax.ShapeDtypeStruct((8, tokens.shape[0]), jnp.int32),
-            jax.ShapeDtypeStruct((own * 8, PART), F32),
-            jax.ShapeDtypeStruct((own, 512), F32),
+            jax.ShapeDtypeStruct((12, own, PART), F32),
         ),
         in_specs=[pl.BlockSpec(memory_space=vm)] * 6,
-        out_specs=[pl.BlockSpec(memory_space=vm)] * 5,
+        out_specs=[pl.BlockSpec(memory_space=pl.ANY)] * 4,
         scratch_shapes=[
             vm((CAP, tokens.shape[0]), BF16),
             vm((2,) + piece, BF16),
@@ -726,13 +745,17 @@
             vm(piece, BF16),
             vm(piece, BF16),
             vm(piece, BF16),
+            vm(piece, BF16),
             vm((3, 8, 512), F32),
             vm((5, 8, 512), F32),
             vm((16, 512), F32),
             vm((8, tokens.shape[0]), jnp.int32),
             vm((16, PART), F32),
+            vm((8, tokens.shape[0]), F32),
+            vm((12, own, PART), F32),
             pltpu.SemaphoreType.DMA((192,)),
             pltpu.SemaphoreType.DMA((192,)),
+            pltpu.SemaphoreType.DMA((8,)),
         ],
         cost_estimate=pl.CostEstimate(flops=flops, bytes_accessed=20 << 20, transcendentals=CAP * 512),
         compiler_params=pltpu.CompilerParams(
@@ -743,12 +766,12 @@
 
 def local(tokens, cotangent, expert_choice, router, gate_up, w_down):
     own, hid = w_down.shape
-    fin, combine, ranks, d_gu, d_down = exchange_and_compute(
+    fin, combine, ranks, sums = exchange_and_compute(
         tokens, cotangent, gate_up.reshape(own, 2 * hid), w_down, router, expert_choice.T
     )
-    grad_tokens, d_gu, d_down = finish(ranks, fin, d_gu, d_down)
+    grad_tokens, combine, d_gu, d_down = finish(ranks, fin, combine, sums)
     d_gate_up = d_gu.reshape(own, hid // PART, 2, PART).transpose(0, 2, 1, 3).reshape(own, 2, hid)
-    return (grad_tokens, combine[:2].T, d_gate_up, d_down)
+    return (grad_tokens, combine.T, d_gate_up, d_down)
 
 
 def solution(mesh):

time: 223 us -> 224 us (level)
  Pallas kernels: 217 us -> 220 us
    pallas_call x1, Pallas kernels: 210 us -> 213 us  [exchange_and_compute(): pl.pallas_call(kernel, out_shape=(jax.ShapeDtypeStruct(piece, BF16), jax....]
where the time goes in v6:
time: 224 us; the launch traced here: 223 us
  Pallas kernels  220 us (98%)
  local copies, waits for them, and re-layouts  2.97 us (1%)
    pallas_call x1, Pallas kernels, exchange_and_compute(): pl.pallas_call(kernel, out_shape=(jax.ShapeDtypeStruct(piece, BF16), jax....  213 us
    pallas_call x1, Pallas kernels, finish(): pl.pallas_call(body, grid=(steps,), out_shape=(jax.ShapeDtypeStruct((tota...  6.53 us

profile of v6, /device:TPU:24, one launch (start us, length us, event | category | flops | bytes accessed | tf_op | source)
XLA Modules:
  0.0 223.4 jit_solution(12519749691606943493)
XLA Ops:
  0.6 3.0 %copy.11 = bf16[96,8,2,512]{3,1,2,0:T(8,128)(2,1)} copy(bf16[96,8,2,512]{3,2,1,0:T(2,128)(2,1)} %bitcast.9) | data formatting | bytes 3145728
  3.6 213.1 %shard_map.93 = (bf16[432,384]{1,0:T(8,128)(2,1)}, f32[8,1536]{1,0:T(8,128)}, s32[8,1536]{1,0:T(8,128)}, f32[12,768,128]{2,1,0:T(8,128)}) custom-call(bf16[1536,384]{1,0:T(8,128)(2,1)} %tokens.1, bf16[1536,384]{1,0:T(8,128)(2,1)} %cotangent.1, bf16[768,1024]{1,0:T(8,128)(2,1)} %bitcast.10, bf16[768,512]{1,0:T(8,128)(2,1)} %down_w.1, bf16[8,6144]{1,0:T(8,128)(2,1)} %router.1, ...), custom_call_target="tpu_custom_call" | custom-call | flops 21743271936 | bytes 20971520 | tf_op jit(solution)/shard_map/pallas_call | solution.py:715
  216.7 6.5 %shard_map.94 = (bf16[1536,384]{1,0:T(8,128)(2,1)}, f32[2,1536]{1,0:T(2,128)}, f32[6144,128]{1,0:T(8,128)}, f32[768,512]{1,0:T(8,128)}) custom-call(s32[8,1536]{1,0:T(8,128)} %get-tuple-element.12.ranks_ref, bf16[432,384]{1,0:T(8,128)(2,1)} %get-tuple-element.13.fin_ref, f32[8,1536]{1,0:T(8,128)} %get-tuple-element.14.comb_ref, ...), custom_call_target="tpu_custom_call" | custom-call | flops 509607936 | bytes 12582912 | tf_op jit(solution)/shard_map/pallas_call | solution.py:689

commit v7 on v6

--- a/solution.py
+++ b/solution.py
@@ -167,7 +167,6 @@
         return carry
 
     lax.fori_loop(0, own // 96, put_weights, 0)
-    start(weights(0))
     named = jnp.broadcast_to(meta[1:2, :].astype(F32).astype(BF16), (16, tokens.shape[0]))
     labels[:, :CAP] = dot_f32(named, select[...], ((1,), (1,)))
 
@@ -211,7 +210,7 @@
 
         for name in ("zh", "xr0", "xl0", "c_own"):
             start(hop(name, p))
-    for sub in range(1, 4):
+    for sub in range(4):
         start(weights(sub))
 
     rs_base = index("rs", 48)
@@ -231,7 +230,12 @@
         to = (yo, yr, yl)[r]
         return copy(("lg", r), lsend.at[r], lrecv.at[r], y=to)
 
-    def pre(p, j):
+    def pre_send(p, j):
+        for kind in RS_KINDS[:4]:
+            for s in (2 * j, 2 * j + 1):
+                rs(kind, p, s).start()
+
+    def pre(p, j, held=False):
         s0, s1 = 2 * j, 2 * j + 1
 
         def one(n, carry):
@@ -258,7 +262,7 @@
                 pown[s0, part(p), 2 * PART :] = d[:, :PART]
                 pown[s1, part(p), 2 * PART :] = d[:, PART:]
 
-            for m, kinds in ((0, ("far_r", "far_l")), (1, ("nr_raw",)), (2, ("nl_raw",))):
+            for m, kinds in () if held else ((0, ("far_r", "far_l")), (1, ("nr_raw",)), (2, ("nl_raw",))):
 
                 @pl.when(n == m)
                 def _():
@@ -346,7 +350,7 @@
         ag("fwd_l", p, s).wait_recv()
 
     def exchange(s, half=None):
-        at = pl.ds(0, own) if half is None else pl.ds(half * (own // 2), own // 2)
+        at = pl.ds(0, own) if half is None else pl.ds(half * (own // 4), own // 4)
         return copy(("gz", s, half), gsend.at[s, at, :], grecv.at[s, at, :], zl=1 - zl)
 
     def grads_tile(s, at):
@@ -388,8 +392,8 @@
         if half is None:
             lax.fori_loop(0, count, one, 0)
         else:
-            lax.fori_loop(half * (count // 2), (half + 1) * (count // 2), one, 0)
-        at = pl.ds(0, own) if half is None else pl.ds(half * (own // 2), own // 2)
+            lax.fori_loop(half * (count // 4), (half + 1) * (count // 4), one, 0)
+        at = pl.ds(0, own) if half is None else pl.ds(half * (own // 4), own // 4)
         put_out(acc.at[pl.ds(3 * s, 3), at, :], acc_out.at[pl.ds(3 * s, 3), at, :])
 
     def score(key):
@@ -461,23 +465,28 @@
                 total = total + ref[at, :].astype(F32)
             out[at, :] = total.astype(out.dtype)
 
-    def back_block(p, t):
-        k = t // 2
-
+    def back_blocks(*blocks):
         def one(b, carry):
-            x_ = 2 * (t % 2) + b
             col = pl.multiple_of(b * 2 * SUB, 128)
-            acc = None
-            for sub in range(4):
-                m = mids[sub, pl.ds(pl.multiple_of(t * CAP + P0[p], 16), PN[p]), : 2 * PART]
-                w = wgt[sub, pl.ds(col, 2 * SUB), : 2 * PART]
-                piece = dot_f32(m, w, ((1,), (1,)))
-                acc = piece if acc is None else acc + piece
-            low, high = acc[:, :SUB], acc[:, SUB:]
-            i = x_ * 2 + k
-            bown[x_, k, part(p), :] = jnp.where(c == 0, low, high).astype(BF16)
-            psend[i // 4, i % 4, part(p), :] = jnp.where(c == 0, high, low).astype(BF16)
-            pair(p, i).start()
+            lines = []
+            for p, t in blocks:
+                at = pl.ds(pl.multiple_of(t * CAP + P0[p], 16), PN[p])
+                lines.append(jnp.concatenate([mids[sub, at, : 2 * PART] for sub in range(4)], axis=1))
+            m = jnp.concatenate(lines, axis=0)
+            w = jnp.concatenate([wgt[sub, pl.ds(col, 2 * SUB), : 2 * PART] for sub in range(4)], axis=1)
+            piece = dot_f32(m, w, ((1,), (1,)))
+            low, high = piece[:, :SUB], piece[:, SUB:]
+            mine = jnp.where(c == 0, low, high).astype(BF16)
+            theirs = jnp.where(c == 0, high, low).astype(BF16)
+            base = 0
+            for p, t in blocks:
+                k = t // 2
+                x_ = 2 * (t % 2) + b
+                i = x_ * 2 + k
+                bown[x_, k, part(p), :] = mine[base : base + PN[p]]
+                psend[i // 4, i % 4, part(p), :] = theirs[base : base + PN[p]]
+                base += PN[p]
+                pair(p, i).start()
             return carry
 
         lax.fori_loop(0, 2, one, 0)
@@ -555,31 +564,33 @@
     gates()
     pointwise(0, 0)
     pointwise(0, 1)
-    weights(2).wait_recv()
-    weights(3).wait_recv()
-    pre(0, 1)
     pointwise(1, 0)
     pointwise(1, 1)
     forward(0, 0)
     forward(0, 1)
-    pre(1, 1)
-    relay(0, 2)
-    relay(0, 3)
+    weights(2).wait_recv()
+    weights(3).wait_recv()
+    pre(0, 1, held=True)
     forward(1, 0)
     forward(1, 1)
-    relay(1, 2)
-    relay(1, 3)
+    pre_send(0, 1)
+    pre(1, 1)
     for p in range(2):
         near(p, 0)
         far(p, 0)
     grads_theirs(0)
     start(exchange(0))
-    pointwise(0, 2)
+    relay(0, 2)
+    relay(0, 3)
     for p in range(2):
         near(p, 1)
         far(p, 1)
     grads_theirs(1)
     start(exchange(1))
+    relay(1, 2)
+    relay(1, 3)
+    grads_mine(0)
+    pointwise(0, 2)
     pointwise(1, 2)
     forward(0, 2)
     pointwise(0, 3)
@@ -590,52 +601,52 @@
             for s in range(4):
                 rs(kind, p, s).wait_send()
     scores()
-    grads_mine(0)
-    back_block(0, y)
+    back_blocks((0, y), (1, y))
     forward(0, 3)
-    grads_mine(1)
-    scores_zh()
     for p in range(2):
         near(p, 2)
         far(p, 2)
     grads_theirs(2)
     start(exchange(2))
+    scores_zh()
     forward(1, 3)
     near(0, 3)
-    back_block(0, yr)
-    back_block(0, yl)
+    back_blocks((0, yr), (0, yl))
     far(0, 3)
-    back_block(0, yo)
+    back_blocks((0, yo),)
     back_sum(0, y)
     back_sum(0, yr)
     back_sum(0, yl)
     back_sum(0, yo)
-    back_block(1, y)
     near(1, 3)
-    back_block(1, yr)
-    back_block(1, yl)
+    back_blocks((1, yr), (1, yl))
     far(1, 3)
-    back_block(1, yo)
+    grads_theirs(3)
+    start(exchange(3, 0))
+    start(exchange(3, 1))
+    back_blocks((1, yo),)
     back_sum(1, y)
     back_sum(1, yr)
     back_sum(1, yl)
     back_sum(1, yo)
     ring_relay(0)
-    grads_theirs(3)
-    start(exchange(3, 0))
     ring_relay(1)
     ring_end(0)
-    start(exchange(3, 1))
+    start(exchange(3, 2))
     scores_x()
+    grads_mine(1)
+    ring_end(1)
+    start(exchange(3, 3))
     add_grads(0)
     add_grads(1)
+    go_home(0)
     grads_mine(2)
-    ring_end(1)
-    go_home(0)
-    grads_mine(3)
     add_grads(2)
     scores_end()
     go_home(1)
+    grads_mine(3)
+    for quarter_ in range(4):
+        add_grads(3, quarter_)
 
     @pl.when(moves)
     def _():
@@ -643,9 +654,6 @@
         home(1).wait_recv()
 
     put_out(fin, fin_out)
-
-    add_grads(3, 0)
-    add_grads(3, 1)
 
     @pl.when(moves)
     def _():
@@ -755,7 +763,7 @@
             vm((12, own, PART), F32),
             pltpu.SemaphoreType.DMA((192,)),
             pltpu.SemaphoreType.DMA((192,)),
-            pltpu.SemaphoreType.DMA((8,)),
+            pltpu.SemaphoreType.DMA((12,)),
         ],
         cost_estimate=pl.CostEstimate(flops=flops, bytes_accessed=20 << 20, transcendentals=CAP * 512),
         compiler_params=pltpu.CompilerParams(

time: 224 us -> 216 us (0.964); the launches traced: 223 us -> 213 us
  Pallas kernels: 220 us -> 209 us
    pallas_call x1, Pallas kernels: 213 us -> 203 us  [exchange_and_compute(): pl.pallas_call(kernel, out_shape=(jax.ShapeDtypeStruct(piece, BF16), jax....]
where the time goes in v7:
time: 216 us; the launch traced here: 213 us
  Pallas kernels  209 us (97%)
  local copies, waits for them, and re-layouts  2.97 us (1%)
    pallas_call x1, Pallas kernels, exchange_and_compute(): pl.pallas_call(kernel, out_shape=(jax.ShapeDtypeStruct(piece, BF16), jax....  203 us
    pallas_call x1, Pallas kernels, finish(): pl.pallas_call(body, grid=(steps,), out_shape=(jax.ShapeDtypeStruct((tota...  6.53 us

profile of v7, /device:TPU:24, one launch (start us, length us, event | category | flops | bytes accessed | tf_op | source)
XLA Modules:
  0.0 212.8 jit_solution(11121493242440117062)
XLA Ops:
  0.6 3.0 %copy.11 = bf16[96,8,2,512]{3,1,2,0:T(8,128)(2,1)} copy(bf16[96,8,2,512]{3,2,1,0:T(2,128)(2,1)} %bitcast.9) | data formatting | bytes 3145728
  3.6 202.5 %shard_map.93 = (bf16[432,384]{1,0:T(8,128)(2,1)}, f32[8,1536]{1,0:T(8,128)}, s32[8,1536]{1,0:T(8,128)}, f32[12,768,128]{2,1,0:T(8,128)}) custom-call(bf16[1536,384]{1,0:T(8,128)(2,1)} %tokens.1, bf16[1536,384]{1,0:T(8,128)(2,1)} %cotangent.1, bf16[768,1024]{1,0:T(8,128)(2,1)} %bitcast.10, bf16[768,512]{1,0:T(8,128)(2,1)} %down_w.1, bf16[8,6144]{1,0:T(8,128)(2,1)} %router.1, ...), custom_call_target="tpu_custom_call" | custom-call | flops 21743271936 | bytes 20971520 | tf_op jit(solution)/shard_map/pallas_call | solution.py:723
  206.1 6.5 %shard_map.94 = (bf16[1536,384]{1,0:T(8,128)(2,1)}, f32[2,1536]{1,0:T(2,128)}, f32[6144,128]{1,0:T(8,128)}, f32[768,512]{1,0:T(8,128)}) custom-call(s32[8,1536]{1,0:T(8,128)} %get-tuple-element.12.ranks_ref, bf16[432,384]{1,0:T(8,128)(2,1)} %get-tuple-element.13.fin_ref, f32[8,1536]{1,0:T(8,128)} %get-tuple-element.14.comb_ref, ...), custom_call_target="tpu_custom_call" | custom-call | flops 509607936 | bytes 12582912 | tf_op jit(solution)/shard_map/pallas_call | solution.py:697

commit v8 on v7

--- a/solution.py
+++ b/solution.py
@@ -31,7 +31,7 @@
     tokens, cotangent, gate_up, down_w, router, choice,
     fin_out, comb_out, rank_out, acc_out,
     select, xin, rows, wgt, psend, pown, prelay, precv, lsend, lrecv, gate, sacc, mids,
-    gsend, grecv, bown, brecv, xrelay, xrecv, zsend, zrecv, fsend, fin, srow, srecv, labels, meta, flags, comb, acc,
+    gsend, grecv, bown, brecv, xrelay, xrecv, fsend, fin2, fin, srow, srecv, labels, meta, flags, comb, acc,
     ssem, rsem, osem,
 ):
     y, zl, zh, x, c = (lax.axis_index(a) for a in ALL)
@@ -71,6 +71,7 @@
     peers = (
         dict(y=yr), dict(y=yl), dict(y=yo), dict(zl=1 - zl), dict(zh=1 - zh),
         dict(x=xr), dict(x=xl), dict(x=xo), dict(c=1 - c),
+        dict(y=2 * (1 - zh) + x // 2, zh=swap_zh, x=swap_x), dict(y=swap_y, zh=1 - swap_zh, x=swap_x),
     )
     for peer in peers:
         pl.semaphore_signal(barrier, inc=1, device_id=peer, device_id_type=MESH)
@@ -230,45 +231,34 @@
         to = (yo, yr, yl)[r]
         return copy(("lg", r), lsend.at[r], lrecv.at[r], y=to)
 
-    def pre_send(p, j):
+    def pre_send(p, s):
         for kind in RS_KINDS[:4]:
-            for s in (2 * j, 2 * j + 1):
-                rs(kind, p, s).start()
-
-    def pre(p, j, held=False):
-        s0, s1 = 2 * j, 2 * j + 1
-
+            rs(kind, p, s).start()
+
+    def pre(p, s, held=False):
         def one(n, carry):
             r = jnp.where(n == 0, 2, jnp.where(n == 1, 1, jnp.where(n == 2, 3, 0)))
             t = (y + r) % 4
             at = pl.ds(pl.multiple_of(t * CAP + P0[p], 16), PN[p])
-            x_in = rows[0, at, :]
-            g0 = dot_f32(x_in, wgt[s0, :, : 2 * PART], ((1,), (0,)))
-            g1 = dot_f32(x_in, wgt[s1, :, : 2 * PART], ((1,), (0,)))
-            w_d = jnp.concatenate([wgt[s0, :, 2 * PART :], wgt[s1, :, 2 * PART :]], axis=1)
-            d = dot_f32(rows[1, at, :], w_d, ((1,), (0,)))
+            g = dot_f32(rows[0, at, :], wgt[s, :, : 2 * PART], ((1,), (0,)))
+            d = dot_f32(rows[1, at, :], wgt[s, :, 2 * PART :], ((1,), (0,)))
 
             @pl.when(n < 3)
             def _():
-                psend[n, s0, part(p), : 2 * PART] = g0.astype(BF16)
-                psend[n, s1, part(p), : 2 * PART] = g1.astype(BF16)
-                psend[n, s0, part(p), 2 * PART :] = d[:, :PART].astype(BF16)
-                psend[n, s1, part(p), 2 * PART :] = d[:, PART:].astype(BF16)
+                psend[n, s, part(p), : 2 * PART] = g.astype(BF16)
+                psend[n, s, part(p), 2 * PART :] = d.astype(BF16)
 
             @pl.when(n == 3)
             def _():
-                pown[s0, part(p), : 2 * PART] = g0
-                pown[s1, part(p), : 2 * PART] = g1
-                pown[s0, part(p), 2 * PART :] = d[:, :PART]
-                pown[s1, part(p), 2 * PART :] = d[:, PART:]
+                pown[s, part(p), : 2 * PART] = g
+                pown[s, part(p), 2 * PART :] = d
 
             for m, kinds in () if held else ((0, ("far_r", "far_l")), (1, ("nr_raw",)), (2, ("nl_raw",))):
 
                 @pl.when(n == m)
                 def _():
-                    for s in (s0, s1):
-                        for kind in kinds:
-                            rs(kind, p, s).start()
+                    for kind in kinds:
+                        rs(kind, p, s).start()
 
             return carry
 
@@ -451,11 +441,19 @@
         }[kind]()
         return copy(("bx", kind, half, p), src, dst, x=to)
 
-    def last(p):
-        return copy(("bz", p), zsend.at[part(p), :], zrecv.at[part(p), :], zh=1 - zh)
-
-    def home(p):
-        return copy(("home", p), fsend.at[part(p), :], fin.at[part(p), :], **swap)
+    def home(p, near_plane):
+        to = swap if near_plane else dict(y=2 * (1 - zh) + x // 2, zh=swap_zh, x=swap_x)
+        src = fsend.at[0 if near_plane else 1, part(p), :]
+        return copy(("home", p, near_plane), src, fin2.at[zh, part(p), :], **to)
+
+    def owned(p):
+        home(p, False).wait_recv()
+
+        @pl.when(moves)
+        def _():
+            home(p, True).wait_recv()
+
+        add_rows(p, fin, [fin2.at[0], fin2.at[1]])
 
     def add_rows(p, out, refs):
         for q in (2 * p, 2 * p + 1):
@@ -522,20 +520,19 @@
         for half in range(2):
             for kind in ("near_r", "near_l"):
                 ring(kind, half, p).wait_recv()
-        add_rows(p, zsend, [bown.at[x, 1 - zh], xrecv.at[0, 1 - zh], xrecv.at[1, 1 - zh]])
-        start(last(p))
+        add_rows(p, fsend.at[1], [bown.at[x, 1 - zh], xrecv.at[0, 1 - zh], xrecv.at[1, 1 - zh]])
+        add_rows(p, fsend.at[0], [bown.at[x, zh], xrecv.at[0, zh], xrecv.at[1, zh]])
 
     def go_home(p):
-        last(p).wait_recv()
-        add_rows(p, fsend, [bown.at[x, zh], xrecv.at[0, zh], xrecv.at[1, zh], zrecv])
+        start(home(p, False))
 
         @pl.when(fixed)
         def _():
-            fin[part(p), :] = fsend[part(p), :]
+            fin2[zh, part(p), :] = fsend[0, part(p), :]
 
         @pl.when(moves)
         def _():
-            home(p).start()
+            home(p, True).start()
 
     arrive("xr0", 0, "xro", "c_xr0")
     arrive("xl0", 0, "c_xl0")
@@ -548,15 +545,17 @@
     arrive("xr1", 0, "c_xr1")
     arrive("xl1", 1, "xlo", "c_xl1")
     arrive("xlo", 0, "c_xlo")
+    all_cores(0)
     weights(0).wait_recv()
+    pre(0, 0)
     weights(1).wait_recv()
-    all_cores(0)
-    pre(0, 0)
+    pre(0, 1)
     arrive("xro", 1, "c_xro")
     arrive("xr1", 1, "c_xr1")
     arrive("xlo", 1, "c_xlo")
     all_cores(1)
     pre(1, 0)
+    pre(1, 1)
     logits()
     for p in range(2):
         for s in range(2):
@@ -569,12 +568,14 @@
     forward(0, 0)
     forward(0, 1)
     weights(2).wait_recv()
-    weights(3).wait_recv()
-    pre(0, 1, held=True)
+    pre(0, 2, held=True)
     forward(1, 0)
     forward(1, 1)
-    pre_send(0, 1)
-    pre(1, 1)
+    pre_send(0, 2)
+    weights(3).wait_recv()
+    pre(0, 3)
+    pre(1, 2)
+    pre(1, 3)
     for p in range(2):
         near(p, 0)
         far(p, 0)
@@ -591,75 +592,68 @@
     relay(1, 3)
     grads_mine(0)
     pointwise(0, 2)
+    pointwise(0, 3)
+    forward(0, 2)
     pointwise(1, 2)
-    forward(0, 2)
-    pointwise(0, 3)
-    forward(1, 2)
+    forward(0, 3)
     pointwise(1, 3)
+    scores()
     for kind in RS_KINDS:
         for p in range(2):
             for s in range(4):
                 rs(kind, p, s).wait_send()
-    scores()
     back_blocks((0, y), (1, y))
-    forward(0, 3)
-    for p in range(2):
-        near(p, 2)
-        far(p, 2)
-    grads_theirs(2)
-    start(exchange(2))
     scores_zh()
-    forward(1, 3)
-    near(0, 3)
+    for s in range(2, 4):
+        near(0, s)
     back_blocks((0, yr), (0, yl))
-    far(0, 3)
+    forward(1, 2)
+    for s in range(2, 4):
+        far(0, s)
     back_blocks((0, yo),)
     back_sum(0, y)
     back_sum(0, yr)
     back_sum(0, yl)
+    forward(1, 3)
     back_sum(0, yo)
+    near(1, 2)
+    far(1, 2)
+    grads_theirs(2)
+    start(exchange(2))
     near(1, 3)
     back_blocks((1, yr), (1, yl))
+    ring_relay(0)
     far(1, 3)
     grads_theirs(3)
-    start(exchange(3, 0))
-    start(exchange(3, 1))
+    start(exchange(3))
     back_blocks((1, yo),)
     back_sum(1, y)
     back_sum(1, yr)
     back_sum(1, yl)
     back_sum(1, yo)
-    ring_relay(0)
+    scores_x()
     ring_relay(1)
+    grads_mine(1)
     ring_end(0)
-    start(exchange(3, 2))
-    scores_x()
-    grads_mine(1)
     ring_end(1)
-    start(exchange(3, 3))
+    go_home(0)
+    go_home(1)
+    grads_mine(2)
     add_grads(0)
     add_grads(1)
-    go_home(0)
-    grads_mine(2)
     add_grads(2)
+    grads_mine(3)
     scores_end()
-    go_home(1)
-    grads_mine(3)
-    for quarter_ in range(4):
-        add_grads(3, quarter_)
-
-    @pl.when(moves)
-    def _():
-        home(0).wait_recv()
-        home(1).wait_recv()
-
+    owned(0)
+    add_grads(3)
+    owned(1)
     put_out(fin, fin_out)
 
     @pl.when(moves)
     def _():
         for p in range(2):
             move(p).wait_send()
-            home(p).wait_send()
+            home(p, True).wait_send()
 
     for kind in AG_KINDS:
         for p in range(2):
@@ -679,7 +673,7 @@
 
 def finish(ranks, fin, combine, sums):
     total, own = ranks.shape[1], sums.shape[1]
-    steps = 4
+    steps = 2
     tile, deep = total // steps, own // steps
 
     def body(ranks_ref, fin_ref, comb_ref, sums_ref, gtok_ref, comb_out, gu_out, down_out):
@@ -750,9 +744,8 @@
             vm((8,) + piece, BF16),
             vm((2,) + piece, BF16),
             vm((2, 2) + piece, BF16),
-            vm(piece, BF16),
-            vm(piece, BF16),
-            vm(piece, BF16),
+            vm((2,) + piece, BF16),
+            vm((2,) + piece, BF16),
             vm(piece, BF16),
             vm((3, 8, 512), F32),
             vm((5, 8, 512), F32),

time: 216 us -> 208 us (0.963)
  Pallas kernels: 209 us -> 201 us
    pallas_call x1, Pallas kernels: 203 us -> 196 us  [exchange_and_compute(): pl.pallas_call(kernel, out_shape=(jax.ShapeDtypeStruct(piece, BF16), jax....]
where the time goes in v8:
time: 208 us; the launch traced here: 205 us
  Pallas kernels  201 us (97%)
  local copies, waits for them, and re-layouts  2.97 us (1%)
    pallas_call x1, Pallas kernels, exchange_and_compute(): pl.pallas_call(kernel, out_shape=(jax.ShapeDtypeStruct(piece, BF16), jax....  196 us
    pallas_call x1, Pallas kernels, finish(): pl.pallas_call(body, grid=(steps,), out_shape=(jax.ShapeDtypeStruct((tota...  5.44 us

profile of v8, /device:TPU:24, one launch (start us, length us, event | category | flops | bytes accessed | tf_op | source)
XLA Modules:
  0.0 204.9 jit_solution(5838402974044051785)
XLA Ops:
  0.6 3.0 %copy.11 = bf16[96,8,2,512]{3,1,2,0:T(8,128)(2,1)} copy(bf16[96,8,2,512]{3,2,1,0:T(2,128)(2,1)} %bitcast.9) | data formatting | bytes 3145728
  3.6 195.9 %shard_map.93 = (bf16[432,384]{1,0:T(8,128)(2,1)}, f32[8,1536]{1,0:T(8,128)}, s32[8,1536]{1,0:T(8,128)}, f32[12,768,128]{2,1,0:T(8,128)}) custom-call(bf16[1536,384]{1,0:T(8,128)(2,1)} %tokens.1, bf16[1536,384]{1,0:T(8,128)(2,1)} %cotangent.1, bf16[768,1024]{1,0:T(8,128)(2,1)} %bitcast.10, bf16[768,512]{1,0:T(8,128)(2,1)} %down_w.1, bf16[8,6144]{1,0:T(8,128)(2,1)} %router.1, ...), custom_call_target="tpu_custom_call" | custom-call | flops 21743271936 | bytes 20971520 | tf_op jit(solution)/shard_map/pallas_call | solution.py:717
  199.5 5.4 %shard_map.94 = (bf16[1536,384]{1,0:T(8,128)(2,1)}, f32[2,1536]{1,0:T(2,128)}, f32[6144,128]{1,0:T(8,128)}, f32[768,512]{1,0:T(8,128)}) custom-call(s32[8,1536]{1,0:T(8,128)} %get-tuple-element.12.ranks_ref, bf16[432,384]{1,0:T(8,128)(2,1)} %get-tuple-element.13.fin_ref, f32[8,1536]{1,0:T(8,128)} %get-tuple-element.14.comb_ref, ...), custom_call_target="tpu_custom_call" | custom-call | flops 509607936 | bytes 12582912 | tf_op jit(solution)/shard_map/pallas_call | solution.py:691

commit v9 on v8

--- a/solution.py
+++ b/solution.py
@@ -163,8 +163,10 @@
         at = pl.ds(pl.multiple_of(zl * own + i * 96, 16), 96)
         of = pl.ds(pl.multiple_of(i * 96, 16), 96)
         for sub in range(4):
-            for n, (ref, base) in enumerate(((gate_up, 0), (gate_up, 512), (down_w, 0))):
-                wgt[sub, at, PART * n : PART * (n + 1)] = ref[of, base + PART * sub : base + PART * (sub + 1)]
+            cut = slice(PART * sub, PART * (sub + 1))
+            wgt[sub, at, :PART] = gate_up[of, 0, cut]
+            wgt[sub, at, PART : 2 * PART] = gate_up[of, 1, cut]
+            wgt[sub, at, 2 * PART :] = down_w[of, cut]
         return carry
 
     lax.fori_loop(0, own // 96, put_weights, 0)
@@ -524,7 +526,7 @@
         add_rows(p, fsend.at[0], [bown.at[x, zh], xrecv.at[0, zh], xrecv.at[1, zh]])
 
     def go_home(p):
-        start(home(p, False))
+        home(p, False).start()
 
         @pl.when(fixed)
         def _():
@@ -644,16 +646,11 @@
     add_grads(2)
     grads_mine(3)
     scores_end()
-    owned(0)
-    add_grads(3)
-    owned(1)
-    put_out(fin, fin_out)
 
     @pl.when(moves)
     def _():
         for p in range(2):
             move(p).wait_send()
-            home(p, True).wait_send()
 
     for kind in AG_KINDS:
         for p in range(2):
@@ -667,6 +664,19 @@
             pair(p, i).wait_send()
     for cp in started:
         cp.wait_send()
+    owned(0)
+    add_grads(3)
+    owned(1)
+    put_out(fin, fin_out)
+
+    for p in range(2):
+        home(p, False).wait_send()
+
+    @pl.when(moves)
+    def _():
+        for p in range(2):
+            home(p, True).wait_send()
+
     for cp in leave:
         cp.wait()
 
@@ -768,7 +778,7 @@
 def local(tokens, cotangent, expert_choice, router, gate_up, w_down):
     own, hid = w_down.shape
     fin, combine, ranks, sums = exchange_and_compute(
-        tokens, cotangent, gate_up.reshape(own, 2 * hid), w_down, router, expert_choice.T
+        tokens, cotangent, gate_up, w_down, router, expert_choice.T
     )
     grad_tokens, combine, d_gu, d_down = finish(ranks, fin, combine, sums)
     d_gate_up = d_gu.reshape(own, hid // PART, 2, PART).transpose(0, 2, 1, 3).reshape(own, 2, hid)

time: 208 us -> 205 us (0.986)
  local copies, waits for them, and re-layouts: 2.97 us -> 0 us
    unnamed x1 -> x0, local copies, waits for them, and re-layouts: 2.97 us -> none
where the time goes in v9:
time: 205 us; the launch traced here: 202 us
  Pallas kernels  201 us (98%)
    pallas_call x1, Pallas kernels, exchange_and_compute(): pl.pallas_call(kernel, out_shape=(jax.ShapeDtypeStruct(piece, BF16), jax....  196 us
    pallas_call x1, Pallas kernels, finish(): pl.pallas_call(body, grid=(steps,), out_shape=(jax.ShapeDtypeStruct((tota...  5.44 us

profile of v9, /device:TPU:24, one launch (start us, length us, event | category | flops | bytes accessed | tf_op | source)
XLA Modules:
  0.0 201.7 jit_solution(1283173165643256831)
XLA Ops:
  0.6 195.6 %shard_map.93 = (bf16[432,384]{1,0:T(8,128)(2,1)}, f32[8,1536]{1,0:T(8,128)}, s32[8,1536]{1,0:T(8,128)}, f32[12,768,128]{2,1,0:T(8,128)}) custom-call(bf16[1536,384]{1,0:T(8,128)(2,1)} %tokens.1, bf16[1536,384]{1,0:T(8,128)(2,1)} %cotangent.1, bf16[768,2,512]{2,1,0:T(2,128)(2,1)} %gate_up.1, bf16[768,512]{1,0:T(8,128)(2,1)} %down_w.1, ...), custom_call_target="tpu_custom_call" | custom-call | flops 21743271936 | bytes 20971520 | tf_op jit(solution)/shard_map/pallas_call | solution.py:727
  196.3 5.4 %shard_map.94 = (bf16[1536,384]{1,0:T(8,128)(2,1)}, f32[2,1536]{1,0:T(2,128)}, f32[6144,128]{1,0:T(8,128)}, f32[768,512]{1,0:T(8,128)}) custom-call(s32[8,1536]{1,0:T(8,128)} %get-tuple-element.12.ranks_ref, bf16[432,384]{1,0:T(8,128)(2,1)} %get-tuple-element.13.fin_ref, f32[8,1536]{1,0:T(8,128)} %get-tuple-element.14.comb_ref, ...), custom_call_target="tpu_custom_call" | custom-call | flops 509607936 | bytes 12582912 | tf_op jit(solution)/shard_map/pallas_call | solution.py:701

commit v10 on v9

--- a/solution.py
+++ b/solution.py
@@ -526,8 +526,6 @@
         add_rows(p, fsend.at[0], [bown.at[x, zh], xrecv.at[0, zh], xrecv.at[1, zh]])
 
     def go_home(p):
-        home(p, False).start()
-
         @pl.when(fixed)
         def _():
             fin2[zh, part(p), :] = fsend[0, part(p), :]
@@ -535,6 +533,8 @@
         @pl.when(moves)
         def _():
             home(p, True).start()
+
+        home(p, False).start()
 
     arrive("xr0", 0, "xro", "c_xr0")
     arrive("xl0", 0, "c_xl0")
@@ -609,13 +609,13 @@
     for s in range(2, 4):
         near(0, s)
     back_blocks((0, yr), (0, yl))
+    back_sum(0, y)
     forward(1, 2)
+    back_sum(0, yr)
+    back_sum(0, yl)
     for s in range(2, 4):
         far(0, s)
     back_blocks((0, yo),)
-    back_sum(0, y)
-    back_sum(0, yr)
-    back_sum(0, yl)
     forward(1, 3)
     back_sum(0, yo)
     near(1, 2)

time: 205 us -> 202 us (0.985)
  no operation moved by 1% of the time
where the time goes in v10:
time: 202 us; the launch traced here: 200 us
  Pallas kernels  199 us (99%)
    pallas_call x1, Pallas kernels, exchange_and_compute(): pl.pallas_call(kernel, out_shape=(jax.ShapeDtypeStruct(piece, BF16), jax....  194 us
    pallas_call x1, Pallas kernels, finish(): pl.pallas_call(body, grid=(steps,), out_shape=(jax.ShapeDtypeStruct((tota...  5.45 us

profile of v10, /device:TPU:24, one launch (start us, length us, event | category | flops | bytes accessed | tf_op | source)
XLA Modules:
  0.0 200.0 jit_solution(6012645225185509064)
XLA Ops:
  0.6 193.9 %shard_map.93 = (bf16[432,384]{1,0:T(8,128)(2,1)}, f32[8,1536]{1,0:T(8,128)}, s32[8,1536]{1,0:T(8,128)}, f32[12,768,128]{2,1,0:T(8,128)}) custom-call(bf16[1536,384]{1,0:T(8,128)(2,1)} %tokens.1, bf16[1536,384]{1,0:T(8,128)(2,1)} %cotangent.1, bf16[768,2,512]{2,1,0:T(2,128)(2,1)} %gate_up.1, bf16[768,512]{1,0:T(8,128)(2,1)} %down_w.1, ...), custom_call_target="tpu_custom_call" | custom-call | flops 21743271936 | bytes 20971520 | tf_op jit(solution)/shard_map/pallas_call | solution.py:727
  194.5 5.4 %shard_map.94 = (bf16[1536,384]{1,0:T(8,128)(2,1)}, f32[2,1536]{1,0:T(2,128)}, f32[6144,128]{1,0:T(8,128)}, f32[768,512]{1,0:T(8,128)}) custom-call(s32[8,1536]{1,0:T(8,128)} %get-tuple-element.12.ranks_ref, bf16[432,384]{1,0:T(8,128)(2,1)} %get-tuple-element.13.fin_ref, f32[8,1536]{1,0:T(8,128)} %get-tuple-element.14.comb_ref, ...), custom_call_target="tpu_custom_call" | custom-call | flops 509607936 | bytes 12582912 | tf_op jit(solution)/shard_map/pallas_call | solution.py:701

commit v11 on v10

--- a/solution.py
+++ b/solution.py
@@ -341,9 +341,11 @@
         ag("fwd_r", p, s).wait_recv()
         ag("fwd_l", p, s).wait_recv()
 
-    def exchange(s, half=None):
-        at = pl.ds(0, own) if half is None else pl.ds(half * (own // 4), own // 4)
-        return copy(("gz", s, half), gsend.at[s, at, :], grecv.at[s, at, :], zl=1 - zl)
+    gz_base = index("gz", 12)
+
+    def exchange(s, i):
+        at = pl.ds(pl.multiple_of(i * 256, 256), 256)
+        return copy_at(gz_base + s * 3 + i, gsend.at[s, at, :], grecv.at[s, at, :], zl=1 - zl)
 
     def grads_tile(s, at):
         gu = dot_f32(rows[0, :, pl.ds(at, 256)], mids[s, :, : 2 * PART], ((0,), (0,)))
@@ -355,6 +357,7 @@
             to = pl.ds(pl.multiple_of(i * 256, 256), 256)
             gsend[s, to, : 2 * PART] = gu.astype(BF16)
             gsend[s, to, 2 * PART :] = d.astype(BF16)
+            exchange(s, i).start()
             return carry
 
         lax.fori_loop(0, own // 256, one, 0)
@@ -370,8 +373,9 @@
 
         lax.fori_loop(0, own // 256, one, 0)
 
-    def add_grads(s, half=None):
-        exchange(s, half).wait_recv()
+    def add_grads(s):
+        for i in range(own // 256):
+            exchange(s, i).wait_recv()
 
         def one(i, carry):
             at = pl.ds(pl.multiple_of(i * 64, 16), 64)
@@ -380,13 +384,8 @@
                 acc[3 * s + g, at, :] += got[:, PART * g : PART * (g + 1)]
             return carry
 
-        count = own // 64
-        if half is None:
-            lax.fori_loop(0, count, one, 0)
-        else:
-            lax.fori_loop(half * (count // 4), (half + 1) * (count // 4), one, 0)
-        at = pl.ds(0, own) if half is None else pl.ds(half * (own // 4), own // 4)
-        put_out(acc.at[pl.ds(3 * s, 3), at, :], acc_out.at[pl.ds(3 * s, 3), at, :])
+        lax.fori_loop(0, own // 64, one, 0)
+        put_out(acc.at[pl.ds(3 * s, 3)], acc_out.at[pl.ds(3 * s, 3)])
 
     def score(key):
         src, dst, to = {
@@ -582,14 +581,12 @@
         near(p, 0)
         far(p, 0)
     grads_theirs(0)
-    start(exchange(0))
     relay(0, 2)
     relay(0, 3)
     for p in range(2):
         near(p, 1)
         far(p, 1)
     grads_theirs(1)
-    start(exchange(1))
     relay(1, 2)
     relay(1, 3)
     grads_mine(0)
@@ -621,17 +618,15 @@
     near(1, 2)
     far(1, 2)
     grads_theirs(2)
-    start(exchange(2))
     near(1, 3)
     back_blocks((1, yr), (1, yl))
     ring_relay(0)
     far(1, 3)
-    grads_theirs(3)
-    start(exchange(3))
-    back_blocks((1, yo),)
-    back_sum(1, y)
     back_sum(1, yr)
     back_sum(1, yl)
+    grads_theirs(3)
+    back_sum(1, y)
+    back_blocks((1, yo),)
     back_sum(1, yo)
     scores_x()
     ring_relay(1)
@@ -662,6 +657,9 @@
     for p in range(2):
         for i in range(8):
             pair(p, i).wait_send()
+    for s in range(4):
+        for i in range(own // 256):
+            exchange(s, i).wait_send()
     for cp in started:
         cp.wait_send()
     owned(0)

time: 202 us -> 202 us (level)
  no operation moved by 1% of the time
where the time goes in v11:
time: 202 us; the launch traced here: 200 us
  Pallas kernels  199 us (99%)
    pallas_call x1, Pallas kernels, exchange_and_compute(): pl.pallas_call(kernel, out_shape=(jax.ShapeDtypeStruct(piece, BF16), jax....  194 us
    pallas_call x1, Pallas kernels, finish(): pl.pallas_call(body, grid=(steps,), out_shape=(jax.ShapeDtypeStruct((tota...  5.44 us

profile of v11, /device:TPU:24, one launch (start us, length us, event | category | flops | bytes accessed | tf_op | source)
XLA Modules:
  0.0 199.8 jit_solution(18433217237986840684)
XLA Ops:
  0.6 193.7 %shard_map.93 = (bf16[432,384]{1,0:T(8,128)(2,1)}, f32[8,1536]{1,0:T(8,128)}, s32[8,1536]{1,0:T(8,128)}, f32[12,768,128]{2,1,0:T(8,128)}) custom-call(bf16[1536,384]{1,0:T(8,128)(2,1)} %tokens.1, bf16[1536,384]{1,0:T(8,128)(2,1)} %cotangent.1, bf16[768,2,512]{2,1,0:T(2,128)(2,1)} %gate_up.1, bf16[768,512]{1,0:T(8,128)(2,1)} %down_w.1, ...), custom_call_target="tpu_custom_call" | custom-call | flops 21743271936 | bytes 20971520 | tf_op jit(solution)/shard_map/pallas_call | solution.py:725
  194.3 5.4 %shard_map.94 = (bf16[1536,384]{1,0:T(8,128)(2,1)}, f32[2,1536]{1,0:T(2,128)}, f32[6144,128]{1,0:T(8,128)}, f32[768,512]{1,0:T(8,128)}) custom-call(s32[8,1536]{1,0:T(8,128)} %get-tuple-element.12.ranks_ref, bf16[432,384]{1,0:T(8,128)(2,1)} %get-tuple-element.13.fin_ref, f32[8,1536]{1,0:T(8,128)} %get-tuple-element.14.comb_ref, ...), custom_call_target="tpu_custom_call" | custom-call | flops 509607936 | bytes 12582912 | tf_op jit(solution)/shard_map/pallas_call | solution.py:699
